TPU v7x, 32 devices: a whole 2x2x4 slice. The times are simulated.
32 devices in a mesh: groups: 1, ep: 16 (over z, y, x), hp: 2 (over core).
Axes of the slice: x: 2, y: 2, z: 4, core: 2. Of those that a mesh axis runs over, the one named last changes fastest.
Arguments:
- x_pre: bfloat16 [896, 1536], P(('groups', 'ep')), may hold values from -6 to 6
- x_dec: bfloat16 [128, 1536], P(('groups', 'ep')), may hold values from -6 to 6
- prefill_query_rows: bfloat16 [896, 2048], P(('groups', 'ep'), 'hp'), may hold values from -240 to 240
- prefill_key_values: bfloat16 [2, 896, 256], P(None, ('groups', 'ep'), 'hp'), may hold values from -6.1 to 6.1
- decode_query_rows: bfloat16 [128, 2048], P(('groups', 'ep'), 'hp'), may hold values from -240 to 240
- decode_key_values: bfloat16 [2, 128, 256], P(None, ('groups', 'ep'), 'hp'), may hold values from -6 to 6
- cache: bfloat16 [2, 128, 128, 256], P(None, ('groups', 'ep'), None, 'hp'), may hold values from -6.1 to 6.1
- cache_len: int32 [128], P(('groups', 'ep')), may hold values from 2 to 128
- sinks: float32 [32], P('hp'), may hold values from -1 to 5
- o_weight: bfloat16 [2048, 1536], P('hp', 'ep'), may hold values from -0.125 to 0.125
- norm_gain: float32 [1536], replicated, may hold values from 0.5 to 1.5
- expert_ids: int32 [1024, 4], P(('groups', 'ep')), may hold values from 0 to 7, all different within a row; in each aligned block of 64 rows (0 to 63, 64 to 127, ...) at most 48 rows name the same one
- route_logits: float32 [1024, 4], P(('groups', 'ep')), may hold values from -6 to 6
- w_gate_up: bfloat16 [16, 2, 1536, 768], P('ep', None, None, 'hp'), may hold values from -0.15625 to 0.15625
- w_down: bfloat16 [16, 768, 1536], P('ep', 'hp'), may hold values from -0.15625 to 0.15625
Outputs:
- layer_out: bfloat16 [1024, 1536], P(('groups', 'ep', 'hp'))
Inputs may be any that keep to these rules, and one draw needn't show every extreme that they name: `expert_ids`: each row names 4 different experts; among the rows of one index of ep no expert is named by more than 48 rows, and in every draw some expert is named by exactly 48 rows of some index.
All inputs are finite; a program needn't handle non-finite values.
Results may differ from a plain program's by a relative error of at most 0.0065.
Values may be sent and summed in bfloat16 or wider, within the bound.
No kernel may reach another device: no remote copies, remote signals or barrier semaphores. Data moves between devices by JAX's collectives and lax.ppermute only.
A program may use at most 64 MiB of HBM per device.

v0:
```python
import functools
import jax
import jax.numpy as jnp
from jax import lax
from jax.experimental import pallas as pl
from jax.experimental.pallas import tpu as pltpu
from jax.sharding import PartitionSpec as P


HEAD_SIZE = 64


EPS = 1e-05


def rms_norm(stream, gain):
    mean_sq = jnp.mean(stream * stream, axis=-1, keepdims=True)
    return (stream * lax.rsqrt(mean_sq + EPS) * gain).astype(jnp.bfloat16)


def attention_kernel(
    sinks_ref, len_ref, pre_q_ref, pre_kv_ref, dec_q_ref, dec_kv_ref, cache_ref, out_ref
):
    attend(sinks_ref, len_ref, pre_q_ref, pre_kv_ref, dec_q_ref, dec_kv_ref, cache_ref, out_ref)


def start_kernel(
    where_ref,
    sinks_ref,
    len_ref,
    pre_q_ref,
    pre_kv_ref,
    dec_q_ref,
    dec_kv_ref,
    cache_ref,
    pre_x_ref,
    dec_x_ref,
    ids_ref,
    logits_ref,
    out_ref,
    *rest,
    experts,
):
    pieces, x_ref = rest[:-1], rest[-1]
    attend(sinks_ref, len_ref, pre_q_ref, pre_kv_ref, dec_q_ref, dec_kv_ref, cache_ref, out_ref)
    line, core = where_ref[0], where_ref[1]
    half, width = x_ref.shape
    pre_rows = pre_x_ref.shape[0]
    second = jnp.concatenate(
        [pre_x_ref[half:pre_rows].astype(jnp.float32), dec_x_ref[...].astype(jnp.float32)], 0
    )
    x_ref[...] = jnp.where(core == 0, pre_x_ref[:half].astype(jnp.float32), second)
    topk, tokens = ids_ref.shape
    logits = [logits_ref[pl.ds(k, 1), :] for k in range(topk)]
    top = functools.reduce(jnp.maximum, logits)
    expo = [jnp.exp(value - top) for value in logits]
    total = functools.reduce(lambda a, b: a + b, expo)
    tail_width = pieces[0].shape[1] - width // len(pieces)
    place = lax.broadcasted_iota(jnp.int32, (tail_width, tokens), 0)
    factor = jnp.zeros((tail_width, tokens), jnp.float32)
    for k in range(topk):
        factor = factor + jnp.where(place % experts == ids_ref[pl.ds(k, 1), :], expo[k] / total, 0.0)
    high = factor.astype(jnp.bfloat16).astype(jnp.float32)
    factor = jnp.where(place < experts, high, jnp.where(place < 2 * experts, factor - high, 0.0))
    factor = factor.T
    tail = jnp.where(core == 0, factor[:half], factor[half:]).astype(jnp.bfloat16)
    share = width // len(pieces)
    for k, piece in enumerate(pieces):
        begin = pl.multiple_of(lax.rem(line + k, len(pieces)) * share, 128)
        piece[:, :share] = x_ref[:, pl.ds(begin, share)].astype(jnp.bfloat16)
        piece[:, share:] = tail


def attend(sinks_ref, len_ref, pre_q_ref, pre_kv_ref, dec_q_ref, dec_kv_ref, cache_ref, out_ref):
    pre_rows, q_width = pre_q_ref.shape
    dec_rows = dec_q_ref.shape[0]
    lanes = 2 * HEAD_SIZE
    group = (q_width // HEAD_SIZE) // (pre_kv_ref.shape[2] // HEAD_SIZE)
    scale = HEAD_SIZE ** (-0.5)
    padded = -(-pre_rows // 16) * 16
    positions = cache_ref.shape[2]

    def lane(rows):
        return lax.broadcasted_iota(jnp.int32, (rows, lanes), 1)

    def aligned(pair, side, head, rows):
        value = pair if side == head % 2 else pltpu.roll(pair, HEAD_SIZE, 1)
        return jnp.where((lane(rows) // HEAD_SIZE) == head % 2, value, 0.0)

    def joined(low, high, head, rows):
        low = low if head % 2 == 0 else pltpu.roll(low, HEAD_SIZE, 1)
        high = high if head % 2 == 1 else pltpu.roll(high, HEAD_SIZE, 1)
        return jnp.where(lane(rows) < HEAD_SIZE, low, high)

    def weights(scores, sink, more=None):
        top = jnp.maximum(jnp.max(scores, axis=-1, keepdims=True), sink)
        if more is not None:
            top = jnp.maximum(top, more)
        expo = jnp.exp(scores - top)
        total = jnp.sum(expo, axis=-1, keepdims=True) + jnp.exp(sink - top)
        if more is None:
            return (expo / total).astype(jnp.bfloat16), None
        extra = jnp.exp(more - top)
        total = total + extra
        return (expo / total).astype(jnp.bfloat16), (extra / total).astype(jnp.bfloat16)

    def filled(value):
        return jnp.concatenate(
            [value.astype(jnp.float32), jnp.zeros((padded - pre_rows, lanes), jnp.float32)], 0
        ).astype(jnp.bfloat16)

    contract = (((1,), (1,)), ((), ()))
    key_at = lax.broadcasted_iota(jnp.int32, (pre_rows, padded), 1)
    visible = key_at <= lax.broadcasted_iota(jnp.int32, (pre_rows, padded), 0)
    row_seq = lax.broadcasted_iota(jnp.int32, (dec_rows, positions), 0)
    length = jnp.zeros((dec_rows, positions), jnp.int32)
    for s in range(dec_rows):
        length = jnp.where(row_seq == s, len_ref[s], length)
    live = lax.broadcasted_iota(jnp.int32, (dec_rows, positions), 1) < length

    for head in range(pre_kv_ref.shape[2] // HEAD_SIZE):
        at_lanes = pl.ds((head // 2) * lanes, lanes)
        first_pair = head * group // 2
        here = range(first_pair, first_pair + group // 2)
        stacked = []
        for p in here:
            pair = pre_q_ref[:, pl.ds(p * lanes, lanes)].astype(jnp.float32)
            stacked += [aligned(pair, side, head, pre_rows) for side in (0, 1)]
        queries = jnp.concatenate(stacked, axis=0).astype(jnp.bfloat16)
        keys = filled(pre_kv_ref[0, :, at_lanes])
        scores = lax.dot_general(queries, keys, contract, preferred_element_type=jnp.float32)
        probs = []
        for i in range(group):
            block = scores[i * pre_rows : (i + 1) * pre_rows] * scale
            block = jnp.where(visible, block, -jnp.inf)
            probs.append(weights(block, sinks_ref[head * group + i])[0].astype(jnp.float32))
        pre_out = jnp.dot(
            jnp.concatenate(probs, axis=0).astype(jnp.bfloat16),
            filled(pre_kv_ref[1, :, at_lanes]),
            preferred_element_type=jnp.float32,
        )
        stacked = []
        for p in here:
            pair = dec_q_ref[:, pl.ds(p * lanes, lanes)].astype(jnp.float32)
            stacked += [aligned(pair, side, head, dec_rows) for side in (0, 1)]
        flat = jnp.concatenate(stacked, axis=0)
        queries = flat.astype(jnp.bfloat16)
        owner = lax.broadcasted_iota(jnp.int32, (group * dec_rows, positions), 0) % dec_rows
        past = jnp.zeros((group * dec_rows, positions), jnp.float32)
        for s in range(dec_rows):
            block = lax.dot_general(
                queries, cache_ref[0, s, :, at_lanes], contract, preferred_element_type=jnp.float32
            )
            past = jnp.where(owner == s, block, past)
        own_keys = dec_kv_ref[0, :, at_lanes].astype(jnp.float32)
        own_values = dec_kv_ref[1, :, at_lanes].astype(jnp.float32)
        probs, extras = [], []
        for i in range(group):
            rows = slice(i * dec_rows, (i + 1) * dec_rows)
            block = jnp.where(live, past[rows] * scale, -jnp.inf)
            own = jnp.sum(flat[rows] * own_keys, axis=1, keepdims=True) * scale
            prob, extra = weights(block, sinks_ref[head * group + i], own)
            probs.append(prob.astype(jnp.float32))
            extras.append(extra.astype(jnp.float32) * own_values)
        probs = jnp.concatenate(probs, axis=0)
        dec_out = jnp.concatenate(extras, axis=0)
        for s in range(dec_rows):
            dec_out = dec_out + jnp.dot(
                jnp.where(owner == s, probs, 0.0).astype(jnp.bfloat16),
                cache_ref[1, s, :, at_lanes],
                preferred_element_type=jnp.float32,
            )
        for n, p in enumerate(here):
            low, high = 2 * n, 2 * n + 1
            pre_pair = joined(
                pre_out[low * pre_rows : (low + 1) * pre_rows],
                pre_out[high * pre_rows : (high + 1) * pre_rows],
                head,
                pre_rows,
            )
            dec_pair = joined(
                dec_out[low * dec_rows : (low + 1) * dec_rows],
                dec_out[high * dec_rows : (high + 1) * dec_rows],
                head,
                dec_rows,
            )
            out_ref[:, pl.ds(p * lanes, lanes)] = jnp.concatenate([pre_pair, dec_pair], 0).astype(
                out_ref.dtype
            )


def attention(
    prefill_query_rows,
    prefill_key_values,
    decode_query_rows,
    decode_key_values,
    cache,
    cache_len,
    sinks,
):
    rows = prefill_query_rows.shape[0] + decode_query_rows.shape[0]
    width = prefill_query_rows.shape[1]
    scalars = pl.BlockSpec(memory_space=pltpu.SMEM)
    vectors = pl.BlockSpec(memory_space=pltpu.VMEM)
    return pl.pallas_call(
        attention_kernel,
        out_shape=jax.ShapeDtypeStruct((rows, width), jnp.bfloat16),
        in_specs=[scalars] * 2 + [vectors] * 5,
        out_specs=vectors,
        cost_estimate=pl.CostEstimate(
            flops=4_000_000_000, bytes_accessed=1_000_000, transcendentals=200_000
        ),
        compiler_params=pltpu.CompilerParams(vmem_limit_bytes=8 * 2**20),
        name="attention",
    )(
        sinks,
        cache_len,
        prefill_query_rows,
        prefill_key_values,
        decode_query_rows,
        decode_key_values,
        cache,
    )


def from_hbm(*values):
    return [pltpu.with_memory_space_constraint(v, pltpu.HBM) for v in values]


SCALARS = pl.BlockSpec(memory_space=pltpu.SMEM)
VECTORS = pl.BlockSpec(memory_space=pltpu.VMEM)


def start(where, inputs, x_pre, x_dec, expert_ids, route_logits, experts, deep):
    queries = inputs[0]
    rows = x_pre.shape[0] + x_dec.shape[0]
    half, width = rows // 2, x_pre.shape[1]
    piece = jax.ShapeDtypeStruct(
        (half, width // deep + -(-2 * experts // 128) * 128), jnp.bfloat16
    )
    pre_q, pre_kv, dec_q, dec_kv, cache, cache_len, sinks = inputs
    outs = pl.pallas_call(
        functools.partial(start_kernel, experts=experts),
        out_shape=[jax.ShapeDtypeStruct((rows, queries.shape[1]), jnp.bfloat16)] + [piece] * deep,
        in_specs=[SCALARS] * 3 + [VECTORS] * 9,
        out_specs=[VECTORS] * (deep + 1),
        scratch_shapes=[pltpu.VMEM((half, width), jnp.float32)],
        cost_estimate=pl.CostEstimate(
            flops=4_000_000_000, bytes_accessed=1_000_000, transcendentals=200_000
        ),
        compiler_params=pltpu.CompilerParams(vmem_limit_bytes=8 * 2**20),
        name="start",
    )(
        where,
        *from_hbm(sinks, cache_len, pre_q, pre_kv, dec_q, dec_kv, cache, x_pre, x_dec),
        *from_hbm(expert_ids.T, route_logits.T),
    )
    return outs[0], outs[1:]


def project_kernel(where_ref, *refs, deep):
    attn = refs[:deep]
    columns, beside, across = refs[deep : deep + 3]
    pieces = refs[deep + 3 : 2 * deep + 3]
    kept_ref, given_ref, tail_ref, weight_ref = refs[2 * deep + 3 :]
    line, core, spot = where_ref[0], where_ref[1], where_ref[2]
    count = columns.shape[0]
    for near in range(PLANE):
        other = (near >> 1) | ((near & 1) << 1)
        chip = jnp.bitwise_xor(spot, jnp.where(core == 0, near, other))
        block = (columns, beside, across.at[0], across.at[1])[near]
        weight_ref[pl.ds(pl.multiple_of(chip * count, 16), count), :] = block[...]
    half, share = kept_ref.shape[1], kept_ref.shape[2]
    for k in range(deep):
        part = lax.dot_general(
            attn[k][...],
            weight_ref[...],
            (((1,), (1,)), ((), ())),
            preferred_element_type=jnp.float32,
        )
        chip = lax.rem(line + deep - k, deep)
        mine = jnp.where(core == 0, part[:half], part[half:])
        kept_ref[chip] = mine + pieces[k][:, :share].astype(jnp.float32)
        given_ref[chip] = jnp.where(core == 0, part[half:], part[:half])
        tail_ref[chip] = pieces[k][:, share:]


def project(where, attn, columns, beside, across, pieces):
    deep, half = len(attn), pieces[0].shape[0]
    share = PLANE * columns.shape[0]
    tail = pieces[0].shape[1] - share
    blocks = jax.ShapeDtypeStruct((deep, half, share), jnp.float32)
    return pl.pallas_call(
        functools.partial(project_kernel, deep=deep),
        out_shape=[blocks, blocks, jax.ShapeDtypeStruct((deep, half, tail), jnp.bfloat16)],
        in_specs=[SCALARS] + [VECTORS] * (2 * deep + 3),
        out_specs=[VECTORS] * 3,
        scratch_shapes=[pltpu.VMEM((share, columns.shape[1]), jnp.bfloat16)],
        cost_estimate=pl.CostEstimate(
            flops=4 * deep * half * share * columns.shape[1],
            bytes_accessed=2_000_000,
            transcendentals=0,
        ),
        compiler_params=pltpu.CompilerParams(vmem_limit_bytes=8 * 2**20),
        name="project",
    )(where, *attn, columns, beside, across, *pieces)


def norm_kernel(where_ref, gain_ref, tail_ref, *refs):
    blocks = refs[:-3]
    tokens_ref, own_ref, stream_ref = refs[-3:]
    deep, line = len(blocks), where_ref[0]
    chips, half, share = blocks[0].shape
    for k, block in enumerate(blocks):
        begin = pl.multiple_of(lax.rem(line + deep - k, deep) * share, 128)
        stream_ref[:, pl.ds(begin, share)] = (
            block[...].astype(jnp.float32).reshape(chips * half, share)
        )
    width = deep * share
    stream = stream_ref[...]
    mean_sq = jnp.sum(stream * stream, axis=-1, keepdims=True) * (1.0 / width)
    tokens_ref[:, :width] = (stream * lax.rsqrt(mean_sq + EPS) * gain_ref[...]).astype(jnp.bfloat16)
    tokens_ref[:, width:] = tail_ref[...].reshape(chips * half, tail_ref.shape[2])
    own_ref[...] = stream_ref[pl.ds(pl.multiple_of(line * half, 8), half), :]


def norm(where, gain, tails, blocks):
    chips, half, share = blocks[0].shape
    width = len(blocks) * share
    return pl.pallas_call(
        norm_kernel,
        out_shape=[
            jax.ShapeDtypeStruct((chips * half, width + tails.shape[2]), jnp.bfloat16),
            jax.ShapeDtypeStruct((half, width), jnp.float32),
        ],
        in_specs=[SCALARS] + [VECTORS] * (2 + len(blocks)),
        out_specs=[VECTORS] * 2,
        scratch_shapes=[pltpu.VMEM((chips * half, width), jnp.float32)],
        cost_estimate=pl.CostEstimate(
            flops=1_000_000_000, bytes_accessed=1_000_000, transcendentals=1000
        ),
        compiler_params=pltpu.CompilerParams(vmem_limit_bytes=8 * 2**20),
        name="norm",
    )(where, gain.reshape(1, width), tails, *blocks)


def slot_count(tokens_here, topk, experts):
    return min(
        tokens_here, 2 * ((3 * max(1, (tokens_here * topk + experts - 1) // experts) + 3) // 4)
    )


def slot_plan(
    attn_rows, resid, o_weight, norm_gain, expert_ids, route_logits, w_gate_up, w_down
):
    width = resid.shape[1]
    half = attn_rows.shape[0] // 2
    mine = lax.axis_index("hp") * half
    head_part = jnp.dot(
        attn_rows,
        lax.all_gather(o_weight, "ep", axis=1, tiled=True),
        preferred_element_type=jnp.float32,
    )
    summed = lax.psum_scatter(head_part, "hp", scatter_dimension=0, tiled=True)
    stream = lax.dynamic_slice_in_dim(resid, mine, half, 0).astype(jnp.float32) + summed
    normed = lax.all_gather(rms_norm(stream, norm_gain), "hp", axis=0, tiled=True)
    tokens_here, topk = expert_ids.shape
    holders = lax.axis_size("ep")
    experts = holders // 2
    slot = slot_count(tokens_here, topk, experts)
    plane = slot // 2
    flat_ids = expert_ids.reshape(-1)
    onehot = (flat_ids[:, None] == jnp.arange(experts, dtype=jnp.int32)[None, :]).astype(jnp.int32)
    rank = jnp.sum(jnp.cumsum(onehot, axis=0) * onehot, axis=1) - 1
    position = (flat_ids * slot + rank).reshape(tokens_here, topk)
    columns = jnp.arange(experts * slot, dtype=jnp.int32)[None, None, :] == position[:, :, None]
    picked_rows = jnp.any(columns, axis=1).T.astype(jnp.bfloat16)
    per_expert = (
        jnp.dot(picked_rows, normed, preferred_element_type=jnp.float32)
        .astype(jnp.bfloat16)
        .reshape(experts, slot, width)
    )
    send = jnp.repeat(per_expert, 2, axis=0)
    own_plane = lax.dynamic_slice_in_dim(send, lax.axis_index("hp") * plane, plane, 1)
    arrived_plane = lax.all_to_all(own_plane, "ep", split_axis=0, concat_axis=0, tiled=True)
    arrived = lax.all_gather(arrived_plane, "hp", axis=1, tiled=True)
    rows = arrived.reshape(-1, width)
    gate = jnp.dot(rows, w_gate_up[0, 0], preferred_element_type=jnp.float32)
    upper = jnp.dot(rows, w_gate_up[0, 1], preferred_element_type=jnp.float32)
    hidden = ((upper + 1.0) * gate * jax.nn.sigmoid(1.702 * gate)).astype(jnp.bfloat16)
    partial_out = jnp.dot(hidden, w_down[0], preferred_element_type=jnp.float32).reshape(
        -1, slot, width
    )
    share = lax.psum_scatter(
        partial_out.astype(jnp.bfloat16), "hp", scatter_dimension=1, tiled=True
    )
    returned = lax.all_to_all(share, "ep", split_axis=0, concat_axis=0, tiled=True)
    mix = jax.nn.softmax(route_logits, axis=-1)
    blend = jnp.sum(jnp.where(columns, mix[:, :, None], 0.0), axis=1).reshape(
        tokens_here, experts, slot
    )
    blend = jnp.repeat(blend, 2, axis=1)
    blend_plane = lax.dynamic_slice_in_dim(blend, lax.axis_index("hp") * plane, plane, 2).reshape(
        tokens_here, holders * plane
    )
    terms = jnp.dot(
        blend_plane,
        returned.reshape(-1, width).astype(jnp.float32),
        precision=lax.Precision.HIGHEST,
    )
    moe = lax.psum_scatter(
        terms.astype(jnp.bfloat16), "hp", scatter_dimension=0, tiled=True
    ).astype(jnp.float32)
    return (stream + moe).astype(jnp.bfloat16)


def expert_kernel(mine_ref, rows_ref, gate_up_a, gate_up_b, down_a, down_b, out_ref, *, experts):
    width = gate_up_a.shape[1]
    inputs = rows_ref[:, :width]
    tail = rows_ref[:, width:].astype(jnp.float32)
    lanes = lax.broadcasted_iota(jnp.int32, tail.shape, 1)
    mine = mine_ref[0]
    scale = jnp.sum(
        jnp.where((lanes == mine) | (lanes == mine + experts), tail, 0.0), 1, keepdims=True
    )
    total = None
    for gate_up, down in ((gate_up_a, down_a), (gate_up_b, down_b)):
        gate = jnp.dot(inputs, gate_up[0], preferred_element_type=jnp.float32)
        upper = jnp.dot(inputs, gate_up[1], preferred_element_type=jnp.float32)
        hidden = ((upper + 1.0) * gate * jax.nn.sigmoid(1.702 * gate)).astype(jnp.bfloat16)
        part = jnp.dot(hidden, down[...], preferred_element_type=jnp.float32)
        total = part if total is None else total + part
    out_ref[...] = (total * scale).astype(out_ref.dtype)


def expert_rows(mine, rows, weights, experts, out_type):
    count, width, units = rows.shape[0], weights[0].shape[1], 2 * weights[0].shape[2]
    vectors = pl.BlockSpec(memory_space=pltpu.VMEM)
    return pl.pallas_call(
        functools.partial(expert_kernel, experts=experts),
        out_shape=jax.ShapeDtypeStruct((count, width), out_type),
        in_specs=[pl.BlockSpec(memory_space=pltpu.SMEM)] + [vectors] * 5,
        out_specs=vectors,
        cost_estimate=pl.CostEstimate(
            flops=6 * count * width * units,
            bytes_accessed=6 * width * units,
            transcendentals=count * units,
        ),
        compiler_params=pltpu.CompilerParams(vmem_limit_bytes=12 * 2**20),
        name="expert",
    )(mine, rows, *weights)


PLANE = 4


def plane_perm(holders, stage):
    return [
        (2 * e + h, 2 * (e ^ (1 if h == stage else 2)) + h) for e in range(holders) for h in (0, 1)
    ]


def line_perm(holders, step):
    return [(e, (e + PLANE * step) % holders) for e in range(holders)]


def at(blocks, index):
    return lax.dynamic_index_in_dim(blocks, index, 0, keepdims=False)


def dense_plan(
    inputs, x_pre, x_dec, o_weight, norm_gain, expert_ids, route_logits, w_gate_up, w_down
):
    tokens_here, width = x_pre.shape[0] + x_dec.shape[0], x_pre.shape[1]
    holders = lax.axis_size("ep")
    experts = holders // 2
    deep = holders // PLANE
    place, core = lax.axis_index("ep"), lax.axis_index("hp")
    line, spot = place // PLANE, place % PLANE
    half = tokens_here // 2
    swap = [(0, 1), (1, 0)]
    far_first = range(deep - 1, 0, -1)
    where = jnp.stack([line, core, spot]).astype(jnp.int32)

    def plane(value, stage):
        return lax.ppermute(value, ("ep", "hp"), plane_perm(holders, stage))

    def along(value, step):
        return lax.ppermute(value, "ep", line_perm(holders, step))

    def gather_line(value):
        got = {k: along(value, k) for k in far_first}
        return [value] + [got[k] for k in range(1, deep)]

    gate_up_here, down_here = w_gate_up[0], w_down[0]
    gate_up_there = lax.ppermute(gate_up_here, "hp", swap)
    down_there = lax.ppermute(down_here, "hp", swap)

    columns = o_weight.T
    beside = plane(columns, 0)
    across = plane(jnp.stack([columns, beside]), 1)

    attn_rows, pieces = start(where, inputs, x_pre, x_dec, expert_ids, route_logits, experts, deep)
    attn = gather_line(attn_rows)
    arrived = {k: along(pieces[k], k) for k in far_first}
    arrived[0] = pieces[0]
    kept, given, tails = project(
        where, attn, columns, beside, across, [arrived[k] for k in range(deep)]
    )
    given, gate_up_there, down_there = lax.optimization_barrier((given, gate_up_there, down_there))
    weights = tuple(
        pltpu.with_memory_space_constraint(w, pltpu.VMEM)
        for w in (gate_up_here, gate_up_there, down_here, down_there)
    )
    summed = (kept + lax.ppermute(given, "hp", swap)).astype(jnp.bfloat16)
    tokens, own_stream = norm(where, norm_gain, tails, gather_line(summed))

    mine = jnp.reshape(place // 2, (1,))

    def expert(block, out_type):
        return expert_rows(mine, block, weights, experts, out_type)

    near_tokens = plane(tokens, 0)
    both_tokens = plane(near_tokens, 1)
    far_tokens = plane(tokens, 1)
    own = expert(tokens, jnp.float32)
    near_out = expert(near_tokens, jnp.bfloat16)
    both_out = expert(both_tokens, jnp.bfloat16)
    far_out = expert(far_tokens, jnp.float32)
    far_back = plane(both_out, 0)
    near_back = plane(near_out, 0)
    over = plane((far_out + far_back.astype(jnp.float32)).astype(jnp.bfloat16), 1)
    moe = own + near_back.astype(jnp.float32) + over.astype(jnp.float32)
    moe = moe.reshape(deep, half, width)
    sent = moe.astype(jnp.bfloat16)
    got = [along(at(sent, (line + k) % deep), k) for k in far_first]
    total = own_stream + at(moe, line)
    for block in got:
        total = total + block.astype(jnp.float32)
    return total.astype(jnp.bfloat16)


def on_device(
    x_pre,
    x_dec,
    prefill_query_rows,
    prefill_key_values,
    decode_query_rows,
    decode_key_values,
    cache,
    cache_len,
    sinks,
    o_weight,
    norm_gain,
    expert_ids,
    route_logits,
    w_gate_up,
    w_down,
):
    inputs = (
        prefill_query_rows,
        prefill_key_values,
        decode_query_rows,
        decode_key_values,
        cache,
        cache_len,
        sinks,
    )
    rest = (o_weight, norm_gain, expert_ids, route_logits, w_gate_up, w_down)
    tokens_here, topk = expert_ids.shape
    holders = lax.axis_size("ep")
    dense = tokens_here <= 2 * slot_count(tokens_here, topk, holders // 2)
    even = holders % PLANE == 0 and x_pre.shape[1] % (holders // PLANE * 128) == 0
    if dense and even and holders > PLANE and lax.axis_size("hp") == 2:
        return dense_plan(inputs, x_pre, x_dec, *rest)
    return slot_plan(attention(*inputs), jnp.concatenate([x_pre, x_dec], axis=0), *rest)


def solution(mesh):
    placed = (
        P(("groups", "ep"), None),
        P(("groups", "ep"), None),
        P(("groups", "ep"), "hp"),
        P(None, ("groups", "ep"), "hp"),
        P(("groups", "ep"), "hp"),
        P(None, ("groups", "ep"), "hp"),
        P(None, ("groups", "ep"), None, "hp"),
        P(("groups", "ep")),
        P("hp"),
        P("hp", "ep"),
        P(),
        P(("groups", "ep"), None),
        P(("groups", "ep"), None),
        P("ep", None, None, "hp"),
        P("ep", "hp", None),
    )
    return jax.shard_map(
        on_device,
        mesh=mesh,
        in_specs=placed,
        out_specs=P(("groups", "ep", "hp"), None),
        check_vma=False,
    )
```

profile of v0, /device:TPU:0, one launch (start us, length us, event | category | flops | bytes accessed | tf_op | source)
XLA Modules:
  0.0 107.0 jit_solution(13296786352351357109)
XLA Ops:
  0.5 3.0 %collective-permute-start.3 = (bf16[96,1024]{1,0:T(8,128)(2,1)}, bf16[96,1024]{1,0:T(8,128)(2,1)S(1)}, u32[]{:S(2)}, u32[]{:S(2)}) collective-permute-start(bf16[96,1024]{1,0:T(8,128)(2,1)} %bitcast.39), channel_id=1, source_target_pairs={{0,2},{1,5},{2,0},{3,7},{4,6},{5,1},{6,4},{7,3},{8,10},{9,13},{10,... | collective-permute-start | bytes 589832 | tf_op jit(solution)/shard_map/ppermute | solution.py:486
  3.6 3.8 %collective-permute-done.3.refs_5_ = bf16[96,1024]{1,0:T(8,128)(2,1)S(1)} collective-permute-done((bf16[96,1024]{1,0:T(8,128)(2,1)}, bf16[96,1024]{1,0:T(8,128)(2,1)S(1)}, u32[]{:S(2)}, u32[]{:S(2)}) %collective-permute-start.3) | collective-permute-done | bytes 196640 | tf_op jit(solution)/shard_map/ppermute | solution.py:486
  8.3 2.1 %collective-permute-start.4 = (bf16[2,96,1024]{2,1,0:T(8,128)(2,1)S(1)}, bf16[2,96,1024]{2,1,0:T(8,128)(2,1)S(1)}, u32[]{:S(2)}, u32[]{:S(2)}) collective-permute-start(bf16[2,96,1024]{2,1,0:T(8,128)(2,1)S(1)} %pad_maximum_fusion), channel_id=1, source_target_pairs={{0,4},{1,3},{2,6},{3,1},{4,0},{5,7},{6,2},{7,5},{8,12},{9,11},{10,... | collective-permute-start | bytes 1179656 | tf_op jit(solution)/shard_map/ppermute | solution.py:486
  10.4 3.4 %start.1 = (bf16[64,1024]{1,0:T(8,128)(2,1)S(1)}, bf16[32,512]{1,0:T(8,128)(2,1)S(1)}, bf16[32,512]{1,0:T(8,128)(2,1)S(1)}, bf16[32,512]{1,0:T(8,128)(2,1)S(1)}, bf16[32,512]{1,0:T(8,128)(2,1)S(1)}) custom-call(s32[3]{0:T(128)S(1)} %pad_add_fusion.where_ref, f32[16]{0:T(128)} %sinks_ref.1, s32[8]{0:T(128)} %len_ref.1, bf16[56,1024]{1,0:T(8,128)(2,1)} %pre_q_ref.1, ...), custom_call_target="tpu_custom_call" | custom-call | flops 4000000000 | bytes 1000000 | tf_op jit(solution)/shard_map/start/pallas_call | solution.py:242
  13.9 1.6 %collective-permute-start = (bf16[64,1024]{1,0:T(8,128)(2,1)S(1)}, bf16[64,1024]{1,0:T(8,128)(2,1)S(1)}, u32[]{:S(2)}, u32[]{:S(2)}) collective-permute-start(bf16[64,1024]{1,0:T(8,128)(2,1)S(1)} %get-tuple-element.18.refs_0_), channel_id=1, source_target_pairs={{0,8},{2,10},{4,12},{6,14},{8,16},{10,18},{12,20},{14,22},{16,24},... | collective-permute-start | bytes 393224 | tf_op jit(solution)/shard_map/ppermute | solution.py:489
  15.5 1.6 %collective-permute-start.5 = (bf16[32,512]{1,0:T(8,128)(2,1)S(1)}, bf16[32,512]{1,0:T(8,128)(2,1)S(1)}, u32[]{:S(2)}, u32[]{:S(2)}) collective-permute-start(bf16[32,512]{1,0:T(8,128)(2,1)S(1)} %get-tuple-element.20), channel_id=1, source_target_pairs={{0,8},{2,10},{4,12},{6,14},{8,16},{10,18},{12,20},{14,22},{16,24},... | collective-permute-start | bytes 98312 | tf_op jit(solution)/shard_map/ppermute | solution.py:489
  17.1 4.1 %collective-permute-done.5.refs_8_ = bf16[32,512]{1,0:T(8,128)(2,1)S(1)} collective-permute-done((bf16[32,512]{1,0:T(8,128)(2,1)S(1)}, bf16[32,512]{1,0:T(8,128)(2,1)S(1)}, u32[]{:S(2)}, u32[]{:S(2)}) %collective-permute-start.5) | collective-permute-done | bytes 32800 | tf_op jit(solution)/shard_map/ppermute | solution.py:489
  22.0 4.0 %collective-permute-done.6.refs_9_ = bf16[32,512]{1,0:T(8,128)(2,1)S(1)} collective-permute-done((bf16[32,512]{1,0:T(8,128)(2,1)S(1)}, bf16[32,512]{1,0:T(8,128)(2,1)S(1)}, u32[]{:S(2)}, u32[]{:S(2)}) %collective-permute-start.6) | collective-permute-done | bytes 32800 | tf_op jit(solution)/shard_map/ppermute | solution.py:489
  26.0 2.0 %collective-permute-start.7 = (bf16[32,512]{1,0:T(8,128)(2,1)S(1)}, bf16[32,512]{1,0:T(8,128)(2,1)S(1)}, u32[]{:S(2)}, u32[]{:S(2)}) collective-permute-start(bf16[32,512]{1,0:T(8,128)(2,1)S(1)} %get-tuple-element.22), channel_id=1, source_target_pairs={{0,24},{2,26},{4,28},{6,30},{8,0},{10,2},{12,4},{14,6},{16,8},{18,... | collective-permute-start | bytes 98312 | tf_op jit(solution)/shard_map/ppermute | solution.py:489
  28.0 2.7 %collective-permute-done.7.refs_10_ = bf16[32,512]{1,0:T(8,128)(2,1)S(1)} collective-permute-done((bf16[32,512]{1,0:T(8,128)(2,1)S(1)}, bf16[32,512]{1,0:T(8,128)(2,1)S(1)}, u32[]{:S(2)}, u32[]{:S(2)}) %collective-permute-start.7) | collective-permute-done | bytes 32800 | tf_op jit(solution)/shard_map/ppermute | solution.py:489
  31.2 3.0 %collective-permute-start.2 = (bf16[64,1024]{1,0:T(8,128)(2,1)S(1)}, bf16[64,1024]{1,0:T(8,128)(2,1)S(1)}, u32[]{:S(2)}, u32[]{:S(2)}) collective-permute-start(bf16[64,1024]{1,0:T(8,128)(2,1)S(1)} %get-tuple-element.18.refs_0_), channel_id=1, source_target_pairs={{0,24},{2,26},{4,28},{6,30},{8,0},{10,2},{12,4},{14,6},{16,8},{18,... | collective-permute-start | bytes 393224 | tf_op jit(solution)/shard_map/ppermute | solution.py:489
  34.1 4.0 %collective-permute-done.1.refs_2_ = bf16[64,1024]{1,0:T(8,128)(2,1)S(1)} collective-permute-done((bf16[64,1024]{1,0:T(8,128)(2,1)S(1)}, bf16[64,1024]{1,0:T(8,128)(2,1)S(1)}, u32[]{:S(2)}, u32[]{:S(2)}) %collective-permute-start.1) | collective-permute-done | bytes 131104 | tf_op jit(solution)/shard_map/ppermute | solution.py:489
  38.5 1.7 %project.1 = (f32[4,32,384]{2,1,0:T(8,128)S(1)}, f32[4,32,384]{2,1,0:T(8,128)S(1)}, bf16[4,32,128]{2,1,0:T(8,128)(2,1)S(1)}) custom-call(s32[3]{0:T(128)S(1)} %pad_add_fusion.where_ref, bf16[64,1024]{1,0:T(8,128)(2,1)S(1)} %get-tuple-element.18.refs_0_, bf16[64,1024]{1,0:T(8,128)(2,1)S(1)} %collective-permute-done.refs_1_, ...), custom_call_target="tpu_custom_call" | custom-call | flops 201326592 | bytes 2000000 | tf_op jit(solution)/shard_map/project/pallas_call | solution.py:293
  41.7 1.6 %collective-permute-start.11 = (bf16[4,32,384]{2,1,0:T(8,128)(2,1)S(1)}, bf16[4,32,384]{2,1,0:T(8,128)(2,1)S(1)}, u32[]{:S(2)}, u32[]{:S(2)}) collective-permute-start(bf16[4,32,384]{2,1,0:T(8,128)(2,1)S(1)} %add_convert_fusion.1.refs_0_), channel_id=1, source_target_pairs={{0,8},{2,10},{4,12},{6,14},{8,16},{10,18},{12,20},{14,22},{16,24},... | collective-permute-start | bytes 294920 | tf_op jit(solution)/shard_map/ppermute | solution.py:489
  43.3 2.0 %collective-permute-start.12 = (bf16[4,32,384]{2,1,0:T(8,128)(2,1)S(1)}, bf16[4,32,384]{2,1,0:T(8,128)(2,1)S(1)}, u32[]{:S(2)}, u32[]{:S(2)}) collective-permute-start(bf16[4,32,384]{2,1,0:T(8,128)(2,1)S(1)} %add_convert_fusion.1.refs_0_), channel_id=1, source_target_pairs={{0,16},{2,18},{4,20},{6,22},{8,24},{10,26},{12,28},{14,30},{16,0},... | collective-permute-start | bytes 294920 | tf_op jit(solution)/shard_map/ppermute | solution.py:489
  45.7 3.6 %collective-permute-done.11.refs_1_ = bf16[4,32,384]{2,1,0:T(8,128)(2,1)S(1)} collective-permute-done((bf16[4,32,384]{2,1,0:T(8,128)(2,1)S(1)}, bf16[4,32,384]{2,1,0:T(8,128)(2,1)S(1)}, u32[]{:S(2)}, u32[]{:S(2)}) %collective-permute-start.11) | collective-permute-done | bytes 98336 | tf_op jit(solution)/shard_map/ppermute | solution.py:489
  49.3 3.4 %collective-permute-done.12.refs_2_ = bf16[4,32,384]{2,1,0:T(8,128)(2,1)S(1)} collective-permute-done((bf16[4,32,384]{2,1,0:T(8,128)(2,1)S(1)}, bf16[4,32,384]{2,1,0:T(8,128)(2,1)S(1)}, u32[]{:S(2)}, u32[]{:S(2)}) %collective-permute-start.12) | collective-permute-done | bytes 98336 | tf_op jit(solution)/shard_map/ppermute | solution.py:489
  52.7 1.6 %norm.1 = (bf16[128,1664]{1,0:T(8,128)(2,1)}, f32[32,1536]{1,0:T(8,128)S(1)}) custom-call(s32[3]{0:T(128)S(1)} %pad_add_fusion.where_ref, f32[1,1536]{1,0:T(1,128)S(1)} %reshape.9.gain_ref, bf16[4,32,128]{2,1,0:T(8,128)(2,1)S(1)} %get-tuple-element.23.tail_ref, bf16[4,32,384]{2,1,0:T(8,128)(2,1)S(1)} %add_convert_fusion.1.refs_0_, ...), custom_call_target="tpu_custom_call" | custom-call | flops 1000000000 | bytes 1000000 | tf_op jit(solution)/shard_map/norm/pallas_call | solution.py:330
  55.0 1.5 %collective-permute-start.14 = (bf16[128,1664]{1,0:T(8,128)(2,1)}, bf16[128,1664]{1,0:T(8,128)(2,1)}, u32[]{:S(2)}, u32[]{:S(2)}) collective-permute-start(bf16[128,1664]{1,0:T(8,128)(2,1)} %get-tuple-element.28.rows_ref), channel_id=1, source_target_pairs={{0,2},{1,5},{2,0},{3,7},{4,6},{5,1},{6,4},{7,3},{8,10},{9,13},{10,... | collective-permute-start | bytes 1277960 | tf_op jit(solution)/shard_map/ppermute | solution.py:486
  56.4 7.0 %collective-permute-done.14.rows_ref = bf16[128,1664]{1,0:T(8,128)(2,1)} collective-permute-done((bf16[128,1664]{1,0:T(8,128)(2,1)}, bf16[128,1664]{1,0:T(8,128)(2,1)}, u32[]{:S(2)}, u32[]{:S(2)}) %collective-permute-start.14) | collective-permute-done | bytes 426016 | tf_op jit(solution)/shard_map/ppermute | solution.py:486
  64.0 1.5 %collective-permute-start.16 = (bf16[128,1664]{1,0:T(8,128)(2,1)}, bf16[128,1664]{1,0:T(8,128)(2,1)}, u32[]{:S(2)}, u32[]{:S(2)}) collective-permute-start(bf16[128,1664]{1,0:T(8,128)(2,1)} %get-tuple-element.28.rows_ref), channel_id=1, source_target_pairs={{0,4},{1,3},{2,6},{3,1},{4,0},{5,7},{6,2},{7,5},{8,12},{9,11},{10,... | collective-permute-start | bytes 1277960 | tf_op jit(solution)/shard_map/ppermute | solution.py:486
  65.4 6.4 %collective-permute-done.17.rows_ref = bf16[128,1664]{1,0:T(8,128)(2,1)} collective-permute-done((bf16[128,1664]{1,0:T(8,128)(2,1)}, bf16[128,1664]{1,0:T(8,128)(2,1)}, u32[]{:S(2)}, u32[]{:S(2)}) %collective-permute-start.17) | collective-permute-done | bytes 426016 | tf_op jit(solution)/shard_map/ppermute | solution.py:486
  71.9 3.6 %expert.7 = bf16[128,1536]{1,0:T(8,128)(2,1)S(1)} custom-call(s32[1]{0:T(128)} %bitcast.10.mine_ref, bf16[128,1664]{1,0:T(8,128)(2,1)} %collective-permute-done.17.rows_ref, bf16[2,1536,384]{2,1,0:T(8,128)(2,1)S(1)} %bitcast.30, bf16[2,1536,384]{2,1,0:T(8,128)(2,1)} %collective-permute-done.8.gate_up_b, bf16[384,1536]{1,0:T(8,128)(2,1)S(1)} %bitcast.35, ...), custom_call_target="tpu_custom_call" | custom-call | flops 905969664 | bytes 7077888 | tf_op jit(solution)/shard_map/expert/pallas_call | solution.py:439
  75.5 1.5 %collective-permute-start.18 = (bf16[128,1536]{1,0:T(8,128)(2,1)S(1)}, bf16[128,1536]{1,0:T(8,128)(2,1)S(1)}, u32[]{:S(2)}, u32[]{:S(2)}) collective-permute-start(bf16[128,1536]{1,0:T(8,128)(2,1)S(1)} %expert.7), channel_id=1, source_target_pairs={{0,2},{1,5},{2,0},{3,7},{4,6},{5,1},{6,4},{7,3},{8,10},{9,13},{10,... | collective-permute-start | bytes 1179656 | tf_op jit(solution)/shard_map/ppermute | solution.py:486
  77.0 4.4 %expert.5 = bf16[128,1536]{1,0:T(8,128)(2,1)} custom-call(s32[1]{0:T(128)} %bitcast.10.mine_ref, bf16[128,1664]{1,0:T(8,128)(2,1)} %collective-permute-done.14.rows_ref, bf16[2,1536,384]{2,1,0:T(8,128)(2,1)S(1)} %bitcast.31, bf16[2,1536,384]{2,1,0:T(8,128)(2,1)} %collective-permute-done.8.gate_up_b, bf16[384,1536]{1,0:T(8,128)(2,1)S(1)} %bitcast.36, ...), custom_call_target="tpu_custom_call" | custom-call | flops 905969664 | bytes 7077888 | tf_op jit(solution)/shard_map/expert/pallas_call | solution.py:439
  82.0 3.6 %expert.6 = f32[128,1536]{1,0:T(8,128)S(1)} custom-call(s32[1]{0:T(128)} %bitcast.10.mine_ref, bf16[128,1664]{1,0:T(8,128)(2,1)} %collective-permute-done.16.rows_ref, bf16[2,1536,384]{2,1,0:T(8,128)(2,1)S(1)} %bitcast.32, bf16[2,1536,384]{2,1,0:T(8,128)(2,1)} %collective-permute-done.8.gate_up_b, bf16[384,1536]{1,0:T(8,128)(2,1)S(1)} %bitcast.37, ...), custom_call_target="tpu_custom_call" | custom-call | flops 905969664 | bytes 7077888 | tf_op jit(solution)/shard_map/expert/pallas_call | solution.py:439
  87.0 3.6 %expert.4 = f32[128,1536]{1,0:T(8,128)S(1)} custom-call(s32[1]{0:T(128)} %bitcast.10.mine_ref, bf16[128,1664]{1,0:T(8,128)(2,1)} %get-tuple-element.28.rows_ref, bf16[2,1536,384]{2,1,0:T(8,128)(2,1)S(1)} %bitcast.33, bf16[2,1536,384]{2,1,0:T(8,128)(2,1)} %collective-permute-done.8.gate_up_b, bf16[384,1536]{1,0:T(8,128)(2,1)S(1)} %bitcast.38, ...), custom_call_target="tpu_custom_call" | custom-call | flops 905969664 | bytes 7077888 | tf_op jit(solution)/shard_map/expert/pallas_call | solution.py:439
  92.0 2.6 %collective-permute-done.19 = bf16[128,1536]{1,0:T(8,128)(2,1)} collective-permute-done((bf16[128,1536]{1,0:T(8,128)(2,1)}, bf16[128,1536]{1,0:T(8,128)(2,1)}, u32[]{:S(2)}, u32[]{:S(2)}) %collective-permute-start.19) | collective-permute-done | bytes 393248 | tf_op jit(solution)/shard_map/ppermute | solution.py:486
  95.8 2.6 %collective-permute-start.22 = (bf16[32,1536]{1,0:T(8,128)(2,1)S(1)}, bf16[32,1536]{1,0:T(8,128)(2,1)S(1)}, u32[]{:S(2)}, u32[]{:S(2)}) collective-permute-start(bf16[32,1536]{1,0:T(8,128)(2,1)S(1)} %get-tuple-element.32), channel_id=1, source_target_pairs={{0,8},{2,10},{4,12},{6,14},{8,16},{10,18},{12,20},{14,22},{16,24},... | collective-permute-start | bytes 294920 | tf_op jit(solution)/shard_map/ppermute | solution.py:489
  99.0 1.9 %collective-permute-start.20 = (bf16[32,1536]{1,0:T(8,128)(2,1)S(1)}, bf16[32,1536]{1,0:T(8,128)(2,1)S(1)}, u32[]{:S(2)}, u32[]{:S(2)}) collective-permute-start(bf16[32,1536]{1,0:T(8,128)(2,1)S(1)} %get-tuple-element.31), channel_id=1, source_target_pairs={{0,24},{2,26},{4,28},{6,30},{8,0},{10,2},{12,4},{14,6},{16,8},{18,... | collective-permute-start | bytes 294920 | tf_op jit(solution)/shard_map/ppermute | solution.py:489
  100.9 2.5 %collective-permute-done.22 = bf16[32,1536]{1,0:T(8,128)(2,1)S(1)} collective-permute-done((bf16[32,1536]{1,0:T(8,128)(2,1)S(1)}, bf16[32,1536]{1,0:T(8,128)(2,1)S(1)}, u32[]{:S(2)}, u32[]{:S(2)}) %collective-permute-start.22) | collective-permute-done | bytes 98336 | tf_op jit(solution)/shard_map/ppermute | solution.py:489
  103.3 2.9 %collective-permute-done.21 = bf16[32,1536]{1,0:T(8,128)(2,1)S(1)} collective-permute-done((bf16[32,1536]{1,0:T(8,128)(2,1)S(1)}, bf16[32,1536]{1,0:T(8,128)(2,1)S(1)}, u32[]{:S(2)}, u32[]{:S(2)}) %collective-permute-start.21) | collective-permute-done | bytes 98336 | tf_op jit(solution)/shard_map/ppermute | solution.py:489
  (42 shorter events, 12.2 us)
Async XLA Ops:
  0.0 40.2 %collective-permute-start.8 = (bf16[2,1536,384]{2,1,0:T(8,128)(2,1)}, bf16[2,1536,384]{2,1,0:T(8,128)(2,1)}, u32[]{:S(2)}, u32[]{:S(2)}) collective-permute-start(bf16[2,1536,384]{2,1,0:T(8,128)(2,1)} %bitcast.29), channel_id=1, source_target_pairs={{0,1},{1,0},{2,3},{3,2},{4,5},{5,4},{6,7},{7,6},{8,9},{9,8},{10,11... | collective-permute-start | bytes 7077896 | tf_op jit(solution)/shard_map/ppermute | solution.py:496
  0.5 39.7 %collective-permute-start.9 = (bf16[384,1536]{1,0:T(8,128)(2,1)}, bf16[384,1536]{1,0:T(8,128)(2,1)}, u32[]{:S(2)}, u32[]{:S(2)}) collective-permute-start(bf16[384,1536]{1,0:T(8,128)(2,1)} %bitcast.34), channel_id=1, source_target_pairs={{0,1},{1,0},{2,3},{3,2},{4,5},{5,4},{6,7},{7,6},{8,9},{9,8},{10,11... | collective-permute-start | bytes 3538952 | tf_op jit(solution)/shard_map/ppermute | solution.py:497
  0.5 6.8 %collective-permute-start.3 = (bf16[96,1024]{1,0:T(8,128)(2,1)}, bf16[96,1024]{1,0:T(8,128)(2,1)S(1)}, u32[]{:S(2)}, u32[]{:S(2)}) collective-permute-start(bf16[96,1024]{1,0:T(8,128)(2,1)} %bitcast.39), channel_id=1, source_target_pairs={{0,2},{1,5},{2,0},{3,7},{4,6},{5,1},{6,4},{7,3},{8,10},{9,13},{10,... | collective-permute-start | bytes 589832 | tf_op jit(solution)/shard_map/ppermute | solution.py:486
  8.3 30.2 %collective-permute-start.4 = (bf16[2,96,1024]{2,1,0:T(8,128)(2,1)S(1)}, bf16[2,96,1024]{2,1,0:T(8,128)(2,1)S(1)}, u32[]{:S(2)}, u32[]{:S(2)}) collective-permute-start(bf16[2,96,1024]{2,1,0:T(8,128)(2,1)S(1)} %pad_maximum_fusion), channel_id=1, source_target_pairs={{0,4},{1,3},{2,6},{3,1},{4,0},{5,7},{6,2},{7,5},{8,12},{9,11},{10,... | collective-permute-start | bytes 1179656 | tf_op jit(solution)/shard_map/ppermute | solution.py:486
  10.4 28.0 %copy-start.2 = (bf16[1024,96]{0,1:T(8,128)(2,1)S(1)}, bf16[1024,96]{0,1:T(8,128)(2,1)}, u32[]{:S(2)}) copy-start(bf16[1024,96]{0,1:T(8,128)(2,1)} %param.24) | copy-start | bytes 589828
  10.4 35.3 %copy-start.5 = (f32[1536]{0:T(1024)S(1)}, f32[1536]{0:T(1024)}, u32[]{:S(2)}) copy-start(f32[1536]{0:T(1024)} %param.25) | copy-start | bytes 18436
  13.9 17.3 %collective-permute-start = (bf16[64,1024]{1,0:T(8,128)(2,1)S(1)}, bf16[64,1024]{1,0:T(8,128)(2,1)S(1)}, u32[]{:S(2)}, u32[]{:S(2)}) collective-permute-start(bf16[64,1024]{1,0:T(8,128)(2,1)S(1)} %get-tuple-element.18.refs_0_), channel_id=1, source_target_pairs={{0,8},{2,10},{4,12},{6,14},{8,16},{10,18},{12,20},{14,22},{16,24},... | collective-permute-start | bytes 393224 | tf_op jit(solution)/shard_map/ppermute | solution.py:489
  15.5 5.7 %collective-permute-start.5 = (bf16[32,512]{1,0:T(8,128)(2,1)S(1)}, bf16[32,512]{1,0:T(8,128)(2,1)S(1)}, u32[]{:S(2)}, u32[]{:S(2)}) collective-permute-start(bf16[32,512]{1,0:T(8,128)(2,1)S(1)} %get-tuple-element.20), channel_id=1, source_target_pairs={{0,8},{2,10},{4,12},{6,14},{8,16},{10,18},{12,20},{14,22},{16,24},... | collective-permute-start | bytes 98312 | tf_op jit(solution)/shard_map/ppermute | solution.py:489
  21.2 4.8 %collective-permute-start.6 = (bf16[32,512]{1,0:T(8,128)(2,1)S(1)}, bf16[32,512]{1,0:T(8,128)(2,1)S(1)}, u32[]{:S(2)}, u32[]{:S(2)}) collective-permute-start(bf16[32,512]{1,0:T(8,128)(2,1)S(1)} %get-tuple-element.21), channel_id=1, source_target_pairs={{0,16},{2,18},{4,20},{6,22},{8,24},{10,26},{12,28},{14,30},{16,0},... | collective-permute-start | bytes 98312 | tf_op jit(solution)/shard_map/ppermute | solution.py:489
  26.0 4.7 %collective-permute-start.7 = (bf16[32,512]{1,0:T(8,128)(2,1)S(1)}, bf16[32,512]{1,0:T(8,128)(2,1)S(1)}, u32[]{:S(2)}, u32[]{:S(2)}) collective-permute-start(bf16[32,512]{1,0:T(8,128)(2,1)S(1)} %get-tuple-element.22), channel_id=1, source_target_pairs={{0,24},{2,26},{4,28},{6,30},{8,0},{10,2},{12,4},{14,6},{16,8},{18,... | collective-permute-start | bytes 98312 | tf_op jit(solution)/shard_map/ppermute | solution.py:489
  30.7 7.4 %collective-permute-start.1 = (bf16[64,1024]{1,0:T(8,128)(2,1)S(1)}, bf16[64,1024]{1,0:T(8,128)(2,1)S(1)}, u32[]{:S(2)}, u32[]{:S(2)}) collective-permute-start(bf16[64,1024]{1,0:T(8,128)(2,1)S(1)} %get-tuple-element.18.refs_0_), channel_id=1, source_target_pairs={{0,16},{2,18},{4,20},{6,22},{8,24},{10,26},{12,28},{14,30},{16,0},... | collective-permute-start | bytes 393224 | tf_op jit(solution)/shard_map/ppermute | solution.py:489
  31.2 7.3 %collective-permute-start.2 = (bf16[64,1024]{1,0:T(8,128)(2,1)S(1)}, bf16[64,1024]{1,0:T(8,128)(2,1)S(1)}, u32[]{:S(2)}, u32[]{:S(2)}) collective-permute-start(bf16[64,1024]{1,0:T(8,128)(2,1)S(1)} %get-tuple-element.18.refs_0_), channel_id=1, source_target_pairs={{0,24},{2,26},{4,28},{6,30},{8,0},{10,2},{12,4},{14,6},{16,8},{18,... | collective-permute-start | bytes 393224 | tf_op jit(solution)/shard_map/ppermute | solution.py:489
  40.1 31.7 %copy-start = (bf16[1,2,1536,384]{3,2,1,0:T(8,128)(2,1)S(1)}, bf16[1,2,1536,384]{3,2,1,0:T(8,128)(2,1)}, u32[]{:S(2)}) copy-start(bf16[1,2,1536,384]{3,2,1,0:T(8,128)(2,1)} %param.28) | copy-start | bytes 7077892
  40.2 31.7 %copy-start.1 = (bf16[1,384,1536]{2,1,0:T(8,128)(2,1)S(1)}, bf16[1,384,1536]{2,1,0:T(8,128)(2,1)}, u32[]{:S(2)}) copy-start(bf16[1,384,1536]{2,1,0:T(8,128)(2,1)} %param.29) | copy-start | bytes 3538948
  40.2 1.5 %collective-permute-start.10 = (f32[4,32,384]{2,1,0:T(8,128)S(1)}, f32[4,32,384]{2,1,0:T(8,128)S(1)}, u32[]{:S(2)}, u32[]{:S(2)}) collective-permute-start(f32[4,32,384]{2,1,0:T(8,128)S(1)} %get-tuple-element.26), channel_id=1, source_target_pairs={{0,1},{1,0},{2,3},{3,2},{4,5},{5,4},{6,7},{7,6},{8,9},{9,8},{10,11... | collective-permute-start | bytes 589832 | tf_op jit(solution)/shard_map/ppermute | solution.py:515
  41.7 7.6 %collective-permute-start.11 = (bf16[4,32,384]{2,1,0:T(8,128)(2,1)S(1)}, bf16[4,32,384]{2,1,0:T(8,128)(2,1)S(1)}, u32[]{:S(2)}, u32[]{:S(2)}) collective-permute-start(bf16[4,32,384]{2,1,0:T(8,128)(2,1)S(1)} %add_convert_fusion.1.refs_0_), channel_id=1, source_target_pairs={{0,8},{2,10},{4,12},{6,14},{8,16},{10,18},{12,20},{14,22},{16,24},... | collective-permute-start | bytes 294920 | tf_op jit(solution)/shard_map/ppermute | solution.py:489
  43.3 9.4 %collective-permute-start.12 = (bf16[4,32,384]{2,1,0:T(8,128)(2,1)S(1)}, bf16[4,32,384]{2,1,0:T(8,128)(2,1)S(1)}, u32[]{:S(2)}, u32[]{:S(2)}) collective-permute-start(bf16[4,32,384]{2,1,0:T(8,128)(2,1)S(1)} %add_convert_fusion.1.refs_0_), channel_id=1, source_target_pairs={{0,16},{2,18},{4,20},{6,22},{8,24},{10,26},{12,28},{14,30},{16,0},... | collective-permute-start | bytes 294920 | tf_op jit(solution)/shard_map/ppermute | solution.py:489
  45.3 7.4 %collective-permute-start.13 = (bf16[4,32,384]{2,1,0:T(8,128)(2,1)S(1)}, bf16[4,32,384]{2,1,0:T(8,128)(2,1)S(1)}, u32[]{:S(2)}, u32[]{:S(2)}) collective-permute-start(bf16[4,32,384]{2,1,0:T(8,128)(2,1)S(1)} %add_convert_fusion.1.refs_0_), channel_id=1, source_target_pairs={{0,24},{2,26},{4,28},{6,30},{8,0},{10,2},{12,4},{14,6},{16,8},{18,... | collective-permute-start | bytes 294920 | tf_op jit(solution)/shard_map/ppermute | solution.py:489
  54.3 0.7 copy-start.3
  55.0 8.4 %collective-permute-start.14 = (bf16[128,1664]{1,0:T(8,128)(2,1)}, bf16[128,1664]{1,0:T(8,128)(2,1)}, u32[]{:S(2)}, u32[]{:S(2)}) collective-permute-start(bf16[128,1664]{1,0:T(8,128)(2,1)} %get-tuple-element.28.rows_ref), channel_id=1, source_target_pairs={{0,2},{1,5},{2,0},{3,7},{4,6},{5,1},{6,4},{7,3},{8,10},{9,13},{10,... | collective-permute-start | bytes 1277960 | tf_op jit(solution)/shard_map/ppermute | solution.py:486
  63.4 8.4 %collective-permute-start.17 = (bf16[128,1664]{1,0:T(8,128)(2,1)}, bf16[128,1664]{1,0:T(8,128)(2,1)}, u32[]{:S(2)}, u32[]{:S(2)}) collective-permute-start(bf16[128,1664]{1,0:T(8,128)(2,1)} %collective-permute-done.14.rows_ref), channel_id=1, source_target_pairs={{0,4},{1,3},{2,6},{3,1},{4,0},{5,7},{6,2},{7,5},{8,12},{9,11},{10,... | collective-permute-start | bytes 1277960 | tf_op jit(solution)/shard_map/ppermute | solution.py:486
  64.0 18.0 %collective-permute-start.16 = (bf16[128,1664]{1,0:T(8,128)(2,1)}, bf16[128,1664]{1,0:T(8,128)(2,1)}, u32[]{:S(2)}, u32[]{:S(2)}) collective-permute-start(bf16[128,1664]{1,0:T(8,128)(2,1)} %get-tuple-element.28.rows_ref), channel_id=1, source_target_pairs={{0,4},{1,3},{2,6},{3,1},{4,0},{5,7},{6,2},{7,5},{8,12},{9,11},{10,... | collective-permute-start | bytes 1277960 | tf_op jit(solution)/shard_map/ppermute | solution.py:486
  75.5 10.1 %collective-permute-start.18 = (bf16[128,1536]{1,0:T(8,128)(2,1)S(1)}, bf16[128,1536]{1,0:T(8,128)(2,1)S(1)}, u32[]{:S(2)}, u32[]{:S(2)}) collective-permute-start(bf16[128,1536]{1,0:T(8,128)(2,1)S(1)} %expert.7), channel_id=1, source_target_pairs={{0,2},{1,5},{2,0},{3,7},{4,6},{5,1},{6,4},{7,3},{8,10},{9,13},{10,... | collective-permute-start | bytes 1179656 | tf_op jit(solution)/shard_map/ppermute | solution.py:486
  81.4 10.6 %collective-permute-start.15 = (bf16[128,1536]{1,0:T(8,128)(2,1)}, bf16[128,1536]{1,0:T(8,128)(2,1)}, u32[]{:S(2)}, u32[]{:S(2)}) collective-permute-start(bf16[128,1536]{1,0:T(8,128)(2,1)} %expert.5), channel_id=1, source_target_pairs={{0,2},{1,5},{2,0},{3,7},{4,6},{5,1},{6,4},{7,3},{8,10},{9,13},{10,... | collective-permute-start | bytes 1179656 | tf_op jit(solution)/shard_map/ppermute | solution.py:486
  86.4 8.1 %collective-permute-start.19 = (bf16[128,1536]{1,0:T(8,128)(2,1)}, bf16[128,1536]{1,0:T(8,128)(2,1)}, u32[]{:S(2)}, u32[]{:S(2)}) collective-permute-start(bf16[128,1536]{1,0:T(8,128)(2,1)} %add_convert_fusion), channel_id=1, source_target_pairs={{0,4},{1,3},{2,6},{3,1},{4,0},{5,7},{6,2},{7,5},{8,12},{9,11},{10,... | collective-permute-start | bytes 1179656 | tf_op jit(solution)/shard_map/ppermute | solution.py:486
  90.6 15.7 %copy-start.4 = (f32[32,1536]{1,0:T(8,128)S(1)}, f32[32,1536]{1,0:T(8,128)}, u32[]{:S(2)}) copy-start(f32[32,1536]{1,0:T(8,128)} %copy-done.3) | copy-start | bytes 589828
  95.8 7.5 %collective-permute-start.22 = (bf16[32,1536]{1,0:T(8,128)(2,1)S(1)}, bf16[32,1536]{1,0:T(8,128)(2,1)S(1)}, u32[]{:S(2)}, u32[]{:S(2)}) collective-permute-start(bf16[32,1536]{1,0:T(8,128)(2,1)S(1)} %get-tuple-element.32), channel_id=1, source_target_pairs={{0,8},{2,10},{4,12},{6,14},{8,16},{10,18},{12,20},{14,22},{16,24},... | collective-permute-start | bytes 294920 | tf_op jit(solution)/shard_map/ppermute | solution.py:489
  98.4 7.8 %collective-permute-start.21 = (bf16[32,1536]{1,0:T(8,128)(2,1)S(1)}, bf16[32,1536]{1,0:T(8,128)(2,1)S(1)}, u32[]{:S(2)}, u32[]{:S(2)}) collective-permute-start(bf16[32,1536]{1,0:T(8,128)(2,1)S(1)} %get-tuple-element.33), channel_id=1, source_target_pairs={{0,16},{2,18},{4,20},{6,22},{8,24},{10,26},{12,28},{14,30},{16,0},... | collective-permute-start | bytes 294920 | tf_op jit(solution)/shard_map/ppermute | solution.py:489
  99.0 7.3 %collective-permute-start.20 = (bf16[32,1536]{1,0:T(8,128)(2,1)S(1)}, bf16[32,1536]{1,0:T(8,128)(2,1)S(1)}, u32[]{:S(2)}, u32[]{:S(2)}) collective-permute-start(bf16[32,1536]{1,0:T(8,128)(2,1)S(1)} %get-tuple-element.31), channel_id=1, source_target_pairs={{0,24},{2,26},{4,28},{6,30},{8,0},{10,2},{12,4},{14,6},{16,8},{18,... | collective-permute-start | bytes 294920 | tf_op jit(solution)/shard_map/ppermute | solution.py:489
where the time goes:
time: 107 us
  waiting for transfers between devices  50.2 us (47%)
  starting transfers between devices  30.2 us (28%)
  Pallas kernels  21.9 us (20%)
  other arithmetic  3.86 us (4%)
    ppermute x12, waiting for transfers between devices, along(): return lax.ppermute(value, 'ep', line_perm(holders, step))  27.6 us
    ppermute x8, waiting for transfers between devices, plane(): return lax.ppermute(value, ('ep', 'hp'), plane_perm(holders, stage))  21.1 us
    ppermute x12, starting transfers between devices, along(): return lax.ppermute(value, 'ep', line_perm(holders, step))  18.4 us
    pallas_call x4, Pallas kernels, expert_rows(): pl.pallas_call(functools.partial(expert_kernel, experts=experts), out_sha...  15.2 us
    ppermute x8, starting transfers between devices, plane(): return lax.ppermute(value, ('ep', 'hp'), plane_perm(holders, stage))  11.2 us
    pallas_call x1, Pallas kernels, start(): pl.pallas_call(functools.partial(start_kernel, experts=experts), out_shap...  3.42 us
  transfers between devices with their start and end apart: 23, of which 15 were waited for; matrix products, arithmetic and copies ran while one was open for 2% of the time, Pallas kernels for 19%

commit v1 on v0

--- a/solution.py
+++ b/solution.py
@@ -25,7 +25,10 @@
 
 
 def start_kernel(
-    where_ref,
+    line_ref,
+    core_ref,
+    spot_ref,
+    mine_ref,
     sinks_ref,
     len_ref,
     pre_q_ref,
@@ -43,7 +46,7 @@
 ):
     pieces, x_ref = rest[:-1], rest[-1]
     attend(sinks_ref, len_ref, pre_q_ref, pre_kv_ref, dec_q_ref, dec_kv_ref, cache_ref, out_ref)
-    line, core = where_ref[0], where_ref[1]
+    line, core = line_ref[0], core_ref[0]
     half, width = x_ref.shape
     pre_rows = pre_x_ref.shape[0]
     second = jnp.concatenate(
@@ -242,7 +245,7 @@
     outs = pl.pallas_call(
         functools.partial(start_kernel, experts=experts),
         out_shape=[jax.ShapeDtypeStruct((rows, queries.shape[1]), jnp.bfloat16)] + [piece] * deep,
-        in_specs=[SCALARS] * 3 + [VECTORS] * 9,
+        in_specs=[SCALARS] * 6 + [VECTORS] * 9,
         out_specs=[VECTORS] * (deep + 1),
         scratch_shapes=[pltpu.VMEM((half, width), jnp.float32)],
         cost_estimate=pl.CostEstimate(
@@ -251,50 +254,45 @@
         compiler_params=pltpu.CompilerParams(vmem_limit_bytes=8 * 2**20),
         name="start",
     )(
-        where,
+        *where,
         *from_hbm(sinks, cache_len, pre_q, pre_kv, dec_q, dec_kv, cache, x_pre, x_dec),
         *from_hbm(expert_ids.T, route_logits.T),
     )
     return outs[0], outs[1:]
 
 
-def project_kernel(where_ref, *refs, deep):
+def project_kernel(core_ref, spot_ref, *refs, deep):
     attn = refs[:deep]
-    columns, beside, across = refs[deep : deep + 3]
-    pieces = refs[deep + 3 : 2 * deep + 3]
-    kept_ref, given_ref, tail_ref, weight_ref = refs[2 * deep + 3 :]
-    line, core, spot = where_ref[0], where_ref[1], where_ref[2]
+    columns, beside, across, kept_ref, given_ref, weight_ref = refs[deep:]
+    core, spot = core_ref[0], spot_ref[0]
     count = columns.shape[0]
     for near in range(PLANE):
         other = (near >> 1) | ((near & 1) << 1)
         chip = jnp.bitwise_xor(spot, jnp.where(core == 0, near, other))
         block = (columns, beside, across.at[0], across.at[1])[near]
         weight_ref[pl.ds(pl.multiple_of(chip * count, 16), count), :] = block[...]
-    half, share = kept_ref.shape[1], kept_ref.shape[2]
+    half = kept_ref.shape[1]
+    parts = lax.dot_general(
+        jnp.concatenate([block[...] for block in attn], axis=0),
+        weight_ref[...],
+        (((1,), (1,)), ((), ())),
+        preferred_element_type=jnp.float32,
+    )
     for k in range(deep):
-        part = lax.dot_general(
-            attn[k][...],
-            weight_ref[...],
-            (((1,), (1,)), ((), ())),
-            preferred_element_type=jnp.float32,
-        )
-        chip = lax.rem(line + deep - k, deep)
-        mine = jnp.where(core == 0, part[:half], part[half:])
-        kept_ref[chip] = mine + pieces[k][:, :share].astype(jnp.float32)
-        given_ref[chip] = jnp.where(core == 0, part[half:], part[:half])
-        tail_ref[chip] = pieces[k][:, share:]
-
-
-def project(where, attn, columns, beside, across, pieces):
-    deep, half = len(attn), pieces[0].shape[0]
+        part = parts[2 * half * k : 2 * half * (k + 1)]
+        kept_ref[k] = jnp.where(core == 0, part[:half], part[half:])
+        given_ref[k] = jnp.where(core == 0, part[half:], part[:half])
+
+
+def project(core_at, spot_at, attn, columns, beside, across):
+    deep, half = len(attn), attn[0].shape[0] // 2
     share = PLANE * columns.shape[0]
-    tail = pieces[0].shape[1] - share
-    blocks = jax.ShapeDtypeStruct((deep, half, share), jnp.float32)
+    blocks = pltpu.VMEM((deep, half, share), jnp.float32)
     return pl.pallas_call(
         functools.partial(project_kernel, deep=deep),
-        out_shape=[blocks, blocks, jax.ShapeDtypeStruct((deep, half, tail), jnp.bfloat16)],
-        in_specs=[SCALARS] + [VECTORS] * (2 * deep + 3),
-        out_specs=[VECTORS] * 3,
+        out_shape=[blocks, blocks],
+        in_specs=[SCALARS] * 2 + [VECTORS] * (deep + 3),
+        out_specs=[VECTORS] * 2,
         scratch_shapes=[pltpu.VMEM((share, columns.shape[1]), jnp.bfloat16)],
         cost_estimate=pl.CostEstimate(
             flops=4 * deep * half * share * columns.shape[1],
@@ -303,45 +301,47 @@
         ),
         compiler_params=pltpu.CompilerParams(vmem_limit_bytes=8 * 2**20),
         name="project",
-    )(where, *attn, columns, beside, across, *pieces)
-
-
-def norm_kernel(where_ref, gain_ref, tail_ref, *refs):
-    blocks = refs[:-3]
-    tokens_ref, own_ref, stream_ref = refs[-3:]
-    deep, line = len(blocks), where_ref[0]
-    chips, half, share = blocks[0].shape
-    for k, block in enumerate(blocks):
-        begin = pl.multiple_of(lax.rem(line + deep - k, deep) * share, 128)
-        stream_ref[:, pl.ds(begin, share)] = (
-            block[...].astype(jnp.float32).reshape(chips * half, share)
-        )
+    )(core_at, spot_at, *attn, columns, beside, across)
+
+
+def norm_kernel(line_ref, gain_ref, *refs, deep):
+    pieces, blocks = refs[:deep], refs[deep : 2 * deep]
+    tokens_ref, own_ref = refs[2 * deep :]
+    line = line_ref[0]
+    _, half, share = blocks[0].shape
     width = deep * share
-    stream = stream_ref[...]
-    mean_sq = jnp.sum(stream * stream, axis=-1, keepdims=True) * (1.0 / width)
-    tokens_ref[:, :width] = (stream * lax.rsqrt(mean_sq + EPS) * gain_ref[...]).astype(jnp.bfloat16)
-    tokens_ref[:, width:] = tail_ref[...].reshape(chips * half, tail_ref.shape[2])
-    own_ref[...] = stream_ref[pl.ds(pl.multiple_of(line * half, 8), half), :]
-
-
-def norm(where, gain, tails, blocks):
-    chips, half, share = blocks[0].shape
-    width = len(blocks) * share
+    order = [[(c - b) % deep for b in range(deep)] for c in range(deep)]
+    for c in range(deep):
+        values = [blocks[b][order[c][b]].astype(jnp.float32) for b in range(deep)]
+        square = functools.reduce(lambda x, y: x + y, [v * v for v in values])
+        root = lax.rsqrt(jnp.sum(square, axis=-1, keepdims=True) * (1.0 / width) + EPS)
+        rows = pl.ds(pl.multiple_of(lax.rem(line + deep - c, deep) * half, 16), half)
+        for b, value in enumerate(values):
+            columns = pl.ds(pl.multiple_of(lax.rem(line + deep - b, deep) * share, 128), share)
+            tokens_ref[rows, columns] = (value * root * gain_ref[:, columns]).astype(jnp.bfloat16)
+            if c == 0:
+                own_ref[:, columns] = value
+        tokens_ref[rows, width:] = pieces[c][:, share:]
+
+
+def norm(line_at, gain, pieces, blocks):
+    deep, half, share = blocks[0].shape
+    width = deep * share
+    tail = pieces[0].shape[1] - share
     return pl.pallas_call(
-        norm_kernel,
+        functools.partial(norm_kernel, deep=deep),
         out_shape=[
-            jax.ShapeDtypeStruct((chips * half, width + tails.shape[2]), jnp.bfloat16),
-            jax.ShapeDtypeStruct((half, width), jnp.float32),
+            pltpu.VMEM((deep * half, width + tail), jnp.bfloat16),
+            pltpu.VMEM((half, width), jnp.float32),
         ],
-        in_specs=[SCALARS] + [VECTORS] * (2 + len(blocks)),
+        in_specs=[SCALARS] + [VECTORS] * (1 + 2 * deep),
         out_specs=[VECTORS] * 2,
-        scratch_shapes=[pltpu.VMEM((chips * half, width), jnp.float32)],
         cost_estimate=pl.CostEstimate(
             flops=1_000_000_000, bytes_accessed=1_000_000, transcendentals=1000
         ),
         compiler_params=pltpu.CompilerParams(vmem_limit_bytes=8 * 2**20),
         name="norm",
-    )(where, gain.reshape(1, width), tails, *blocks)
+    )(line_at, gain.reshape(1, width), *pieces, *blocks)
 
 
 def slot_count(tokens_here, topk, experts):
@@ -414,8 +414,39 @@
     return (stream + moe).astype(jnp.bfloat16)
 
 
-def expert_kernel(mine_ref, rows_ref, gate_up_a, gate_up_b, down_a, down_b, out_ref, *, experts):
-    width = gate_up_a.shape[1]
+def pack_kernel(gate_up_a, gate_up_b, down_a, down_b, gate_up_ref, down_ref, sems):
+    units = down_a.shape[0]
+    copies = [
+        pltpu.make_async_copy(gate_up_a, gate_up_ref.at[:, :, :units], sems.at[0]),
+        pltpu.make_async_copy(gate_up_b, gate_up_ref.at[:, :, units:], sems.at[1]),
+        pltpu.make_async_copy(down_a, down_ref.at[:units], sems.at[2]),
+        pltpu.make_async_copy(down_b, down_ref.at[units:], sems.at[3]),
+    ]
+    for copy in copies:
+        copy.start()
+    for copy in copies:
+        copy.wait()
+
+
+def pack(gate_up_a, gate_up_b, down_a, down_b):
+    units, width = down_a.shape
+    kinds = gate_up_a.dtype
+    return pl.pallas_call(
+        pack_kernel,
+        out_shape=[pltpu.VMEM((2, width, 2 * units), kinds), pltpu.VMEM((2 * units, width), kinds)],
+        in_specs=[pl.BlockSpec(memory_space=pltpu.HBM)] * 4,
+        out_specs=[VECTORS] * 2,
+        scratch_shapes=[pltpu.SemaphoreType.DMA((4,))],
+        cost_estimate=pl.CostEstimate(
+            flops=2_000_000_000, bytes_accessed=12 * width * units, transcendentals=0
+        ),
+        compiler_params=pltpu.CompilerParams(vmem_limit_bytes=10 * 2**20),
+        name="pack",
+    )(gate_up_a, gate_up_b, down_a, down_b)
+
+
+def expert_kernel(mine_ref, rows_ref, gate_up, down, out_ref, *, experts):
+    width = gate_up.shape[1]
     inputs = rows_ref[:, :width]
     tail = rows_ref[:, width:].astype(jnp.float32)
     lanes = lax.broadcasted_iota(jnp.int32, tail.shape, 1)
@@ -423,24 +454,20 @@
     scale = jnp.sum(
         jnp.where((lanes == mine) | (lanes == mine + experts), tail, 0.0), 1, keepdims=True
     )
-    total = None
-    for gate_up, down in ((gate_up_a, down_a), (gate_up_b, down_b)):
-        gate = jnp.dot(inputs, gate_up[0], preferred_element_type=jnp.float32)
-        upper = jnp.dot(inputs, gate_up[1], preferred_element_type=jnp.float32)
-        hidden = ((upper + 1.0) * gate * jax.nn.sigmoid(1.702 * gate)).astype(jnp.bfloat16)
-        part = jnp.dot(hidden, down[...], preferred_element_type=jnp.float32)
-        total = part if total is None else total + part
+    gate = jnp.dot(inputs, gate_up[0], preferred_element_type=jnp.float32)
+    upper = jnp.dot(inputs, gate_up[1], preferred_element_type=jnp.float32)
+    hidden = ((upper + 1.0) * gate * jax.nn.sigmoid(1.702 * gate)).astype(jnp.bfloat16)
+    total = jnp.dot(hidden, down[...], preferred_element_type=jnp.float32)
     out_ref[...] = (total * scale).astype(out_ref.dtype)
 
 
-def expert_rows(mine, rows, weights, experts, out_type):
-    count, width, units = rows.shape[0], weights[0].shape[1], 2 * weights[0].shape[2]
-    vectors = pl.BlockSpec(memory_space=pltpu.VMEM)
+def expert_rows(mine_at, rows, weights, experts, out_type):
+    count, (units, width) = rows.shape[0], weights[1].shape
     return pl.pallas_call(
         functools.partial(expert_kernel, experts=experts),
-        out_shape=jax.ShapeDtypeStruct((count, width), out_type),
-        in_specs=[pl.BlockSpec(memory_space=pltpu.SMEM)] + [vectors] * 5,
-        out_specs=vectors,
+        out_shape=pltpu.VMEM((count, width), out_type),
+        in_specs=[SCALARS] + [VECTORS] * 3,
+        out_specs=VECTORS,
         cost_estimate=pl.CostEstimate(
             flops=6 * count * width * units,
             bytes_accessed=6 * width * units,
@@ -448,7 +475,36 @@
         ),
         compiler_params=pltpu.CompilerParams(vmem_limit_bytes=12 * 2**20),
         name="expert",
-    )(mine, rows, *weights)
+    )(mine_at, rows, *weights)
+
+
+def finish_kernel(line_ref, own_ref, near_ref, over_ref, stream_ref, rest_ref, *sent):
+    deep, line = len(sent) + 1, line_ref[0]
+    half = rest_ref.shape[0]
+    for k in range(deep):
+        rows = pl.ds(pl.multiple_of(lax.rem(line + k, deep) * half, 16), half)
+        total = own_ref[rows, :] + near_ref[rows, :].astype(jnp.float32)
+        total = total + over_ref[rows, :].astype(jnp.float32)
+        if k == 0:
+            rest_ref[...] = stream_ref[...] + total
+        else:
+            sent[k - 1][...] = total.astype(jnp.bfloat16)
+
+
+def finish(line_at, own, near_back, over, own_stream, deep):
+    half, width = own_stream.shape
+    return pl.pallas_call(
+        finish_kernel,
+        out_shape=[pltpu.VMEM((half, width), jnp.float32)]
+        + [pltpu.VMEM((half, width), jnp.bfloat16)] * (deep - 1),
+        in_specs=[SCALARS] + [VECTORS] * 4,
+        out_specs=[VECTORS] * deep,
+        cost_estimate=pl.CostEstimate(
+            flops=500_000_000, bytes_accessed=1_000_000, transcendentals=0
+        ),
+        compiler_params=pltpu.CompilerParams(vmem_limit_bytes=8 * 2**20),
+        name="finish",
+    )(line_at, own, near_back, over, own_stream)
 
 
 PLANE = 4
@@ -464,23 +520,18 @@
     return [(e, (e + PLANE * step) % holders) for e in range(holders)]
 
 
-def at(blocks, index):
-    return lax.dynamic_index_in_dim(blocks, index, 0, keepdims=False)
-
-
 def dense_plan(
     inputs, x_pre, x_dec, o_weight, norm_gain, expert_ids, route_logits, w_gate_up, w_down
 ):
-    tokens_here, width = x_pre.shape[0] + x_dec.shape[0], x_pre.shape[1]
     holders = lax.axis_size("ep")
     experts = holders // 2
     deep = holders // PLANE
     place, core = lax.axis_index("ep"), lax.axis_index("hp")
     line, spot = place // PLANE, place % PLANE
-    half = tokens_here // 2
     swap = [(0, 1), (1, 0)]
     far_first = range(deep - 1, 0, -1)
-    where = jnp.stack([line, core, spot]).astype(jnp.int32)
+    where = [jnp.reshape(v, (1,)).astype(jnp.int32) for v in (line, core, spot, place // 2)]
+    line_at, core_at, spot_at, mine_at = where
 
     def plane(value, stage):
         return lax.ppermute(value, ("ep", "hp"), plane_perm(holders, stage))
@@ -495,6 +546,8 @@
     gate_up_here, down_here = w_gate_up[0], w_down[0]
     gate_up_there = lax.ppermute(gate_up_here, "hp", swap)
     down_there = lax.ppermute(down_here, "hp", swap)
+
+    weights = pack(gate_up_here, gate_up_there, down_here, down_there)
 
     columns = o_weight.T
     beside = plane(columns, 0)
@@ -504,21 +557,14 @@
     attn = gather_line(attn_rows)
     arrived = {k: along(pieces[k], k) for k in far_first}
     arrived[0] = pieces[0]
-    kept, given, tails = project(
-        where, attn, columns, beside, across, [arrived[k] for k in range(deep)]
-    )
-    given, gate_up_there, down_there = lax.optimization_barrier((given, gate_up_there, down_there))
-    weights = tuple(
-        pltpu.with_memory_space_constraint(w, pltpu.VMEM)
-        for w in (gate_up_here, gate_up_there, down_here, down_there)
-    )
-    summed = (kept + lax.ppermute(given, "hp", swap)).astype(jnp.bfloat16)
-    tokens, own_stream = norm(where, norm_gain, tails, gather_line(summed))
-
-    mine = jnp.reshape(place // 2, (1,))
+    pieces = [arrived[k] for k in range(deep)]
+    kept, given = project(core_at, spot_at, attn, columns, beside, across)
+    added = jnp.stack([piece[:, : kept.shape[2]] for piece in pieces]).astype(jnp.float32)
+    summed = (kept + lax.ppermute(given, "hp", swap) + added).astype(jnp.bfloat16)
+    tokens, own_stream = norm(line_at, norm_gain, pieces, gather_line(summed))
 
     def expert(block, out_type):
-        return expert_rows(mine, block, weights, experts, out_type)
+        return expert_rows(mine_at, block, weights, experts, out_type)
 
     near_tokens = plane(tokens, 0)
     both_tokens = plane(near_tokens, 1)
@@ -530,14 +576,11 @@
     far_back = plane(both_out, 0)
     near_back = plane(near_out, 0)
     over = plane((far_out + far_back.astype(jnp.float32)).astype(jnp.bfloat16), 1)
-    moe = own + near_back.astype(jnp.float32) + over.astype(jnp.float32)
-    moe = moe.reshape(deep, half, width)
-    sent = moe.astype(jnp.bfloat16)
-    got = [along(at(sent, (line + k) % deep), k) for k in far_first]
-    total = own_stream + at(moe, line)
+    rest, *sent = finish(line_at, own, near_back, over, own_stream, deep)
+    got = [along(sent[k - 1], k) for k in far_first]
     for block in got:
-        total = total + block.astype(jnp.float32)
-    return total.astype(jnp.bfloat16)
+        rest = rest + block.astype(jnp.float32)
+    return rest.astype(jnp.bfloat16)
 
 
 def on_device(

time: 107 us -> 87.1 us (0.81)
  Pallas kernels: 21.9 us -> 10.2 us
  waiting for transfers between devices: 50.2 us -> 45.1 us
  other arithmetic: 3.86 us -> 0.84 us
    pallas_call x4, Pallas kernels: 15.2 us -> 4.8 us  [expert_rows(): pl.pallas_call(functools.partial(expert_kernel, experts=experts), out_sha...]
    ppermute x12, waiting for transfers between devices: 27.6 us -> 20.2 us  [along(): return lax.ppermute(value, 'ep', line_perm(holders, step))]
    ppermute x8, waiting for transfers between devices: 21.1 us -> 24.9 us  [plane(): return lax.ppermute(value, ('ep', 'hp'), plane_perm(holders, stage))]
    ppermute x1, waiting for transfers between devices: 1.43 us -> 0.01 us  [dense_plan(): lax.ppermute(given, 'hp', swap)]
    add x1 -> x0, other arithmetic: 1.22 us -> none  [dense_plan(): moe = own + near_back.astype(jnp.float32) + over.astype(jnp.float32)]
    pallas_call x1, Pallas kernels: 1.68 us -> 0.51 us  [project(): pl.pallas_call(functools.partial(project_kernel, deep=deep), out_shape=[b...]
  transfers between devices with their start and end apart: 23 -> 23, of which waited for: 15 -> 15; matrix products, arithmetic and copies ran while one was open for 2% -> 0% of each run, Pallas kernels for 19% -> 12%
where the time goes in v1:
time: 87.1 us; the launch traced here: 86.9 us
  waiting for transfers between devices  45.1 us (52%)
  starting transfers between devices  30.7 us (35%)
  Pallas kernels  10.2 us (12%)
    ppermute x8, waiting for transfers between devices, plane(): return lax.ppermute(value, ('ep', 'hp'), plane_perm(holders, stage))  24.9 us
    ppermute x12, waiting for transfers between devices, along(): return lax.ppermute(value, 'ep', line_perm(holders, step))  20.2 us
    ppermute x12, starting transfers between devices, along(): return lax.ppermute(value, 'ep', line_perm(holders, step))  19.4 us
    ppermute x8, starting transfers between devices, plane(): return lax.ppermute(value, ('ep', 'hp'), plane_perm(holders, stage))  10.7 us
    pallas_call x4, Pallas kernels, expert_rows(): pl.pallas_call(functools.partial(expert_kernel, experts=experts), out_sha...  4.8 us
    pallas_call x1, Pallas kernels, start(): pl.pallas_call(functools.partial(start_kernel, experts=experts), out_shap...  3.49 us
  transfers between devices with their start and end apart: 23, of which 15 were waited for; matrix products, arithmetic and copies ran while one was open for 0% of the time, Pallas kernels for 12%

profile of v1, /device:TPU:0, one launch (start us, length us, event | category | flops | bytes accessed | tf_op | source)
XLA Modules:
  0.0 86.9 jit_solution(3218083538648196343)
XLA Ops:
  0.5 3.5 %start.1 = (bf16[64,1024]{1,0:T(8,128)(2,1)S(1)}, bf16[32,512]{1,0:T(8,128)(2,1)S(1)}, bf16[32,512]{1,0:T(8,128)(2,1)S(1)}, bf16[32,512]{1,0:T(8,128)(2,1)S(1)}, bf16[32,512]{1,0:T(8,128)(2,1)S(1)}) custom-call(s32[1]{0:T(128)} %bitcast.line_ref, s32[1]{0:T(128)} %bitcast.2.core_ref, s32[1]{0:T(128)} %bitcast.3.spot_ref, s32[1]{0:T(128)} %bitcast.1.mine_ref, ...), custom_call_target="tpu_custom_call" | custom-call | flops 4000000000 | bytes 1000000 | tf_op jit(solution)/shard_map/start/pallas_call | solution.py:245
  4.0 2.6 %collective-permute-start.3 = (bf16[64,1024]{1,0:T(8,128)(2,1)S(1)}, bf16[64,1024]{1,0:T(8,128)(2,1)S(1)}, u32[]{:S(2)}, u32[]{:S(2)}) collective-permute-start(bf16[64,1024]{1,0:T(8,128)(2,1)S(1)} %get-tuple-element.24.refs_0_), channel_id=1, source_target_pairs={{0,8},{2,10},{4,12},{6,14},{8,16},{10,18},{12,20},{14,22},{16,24},... | collective-permute-start | bytes 393224 | tf_op jit(solution)/shard_map/ppermute | solution.py:540
  6.6 2.6 %collective-permute-start.4 = (bf16[64,1024]{1,0:T(8,128)(2,1)S(1)}, bf16[64,1024]{1,0:T(8,128)(2,1)S(1)}, u32[]{:S(2)}, u32[]{:S(2)}) collective-permute-start(bf16[64,1024]{1,0:T(8,128)(2,1)S(1)} %get-tuple-element.24.refs_0_), channel_id=1, source_target_pairs={{0,16},{2,18},{4,20},{6,22},{8,24},{10,26},{12,28},{14,30},{16,0},... | collective-permute-start | bytes 393224 | tf_op jit(solution)/shard_map/ppermute | solution.py:540
  9.6 1.5 %collective-permute-start.6 = (bf16[96,1024]{1,0:T(8,128)(2,1)S(1)}, bf16[96,1024]{1,0:T(8,128)(2,1)S(1)}, u32[]{:S(2)}, u32[]{:S(2)}) collective-permute-start(bf16[96,1024]{1,0:T(8,128)(2,1)S(1)} %bitcast.20), channel_id=1, source_target_pairs={{0,2},{1,5},{2,0},{3,7},{4,6},{5,1},{6,4},{7,3},{8,10},{9,13},{10,... | collective-permute-start | bytes 589832 | tf_op jit(solution)/shard_map/ppermute | solution.py:537
  11.1 4.2 %collective-permute-done.6.refs_5_ = bf16[96,1024]{1,0:T(8,128)(2,1)S(1)} collective-permute-done((bf16[96,1024]{1,0:T(8,128)(2,1)S(1)}, bf16[96,1024]{1,0:T(8,128)(2,1)S(1)}, u32[]{:S(2)}, u32[]{:S(2)}) %collective-permute-start.6) | collective-permute-done | bytes 196640 | tf_op jit(solution)/shard_map/ppermute | solution.py:537
  15.2 2.1 %collective-permute-start.2 = (bf16[32,512]{1,0:T(8,128)(2,1)S(1)}, bf16[32,512]{1,0:T(8,128)(2,1)S(1)}, u32[]{:S(2)}, u32[]{:S(2)}) collective-permute-start(bf16[32,512]{1,0:T(8,128)(2,1)S(1)} %get-tuple-element.23), channel_id=1, source_target_pairs={{0,24},{2,26},{4,28},{6,30},{8,0},{10,2},{12,4},{14,6},{16,8},{18,... | collective-permute-start | bytes 98312 | tf_op jit(solution)/shard_map/ppermute | solution.py:540
  17.4 3.2 %collective-permute-done.2.refs_3_ = bf16[32,512]{1,0:T(8,128)(2,1)S(1)} collective-permute-done((bf16[32,512]{1,0:T(8,128)(2,1)S(1)}, bf16[32,512]{1,0:T(8,128)(2,1)S(1)}, u32[]{:S(2)}, u32[]{:S(2)}) %collective-permute-start.2) | collective-permute-done | bytes 32800 | tf_op jit(solution)/shard_map/ppermute | solution.py:540
  20.5 1.5 %collective-permute-start.7 = (bf16[2,96,1024]{2,1,0:T(8,128)(2,1)S(1)}, bf16[2,96,1024]{2,1,0:T(8,128)(2,1)S(1)}, u32[]{:S(2)}, u32[]{:S(2)}) collective-permute-start(bf16[2,96,1024]{2,1,0:T(8,128)(2,1)S(1)} %pad_maximum_fusion), channel_id=1, source_target_pairs={{0,4},{1,3},{2,6},{3,1},{4,0},{5,7},{6,2},{7,5},{8,12},{9,11},{10,... | collective-permute-start | bytes 1179656 | tf_op jit(solution)/shard_map/ppermute | solution.py:537
  22.1 2.6 %collective-permute-start.5 = (bf16[64,1024]{1,0:T(8,128)(2,1)S(1)}, bf16[64,1024]{1,0:T(8,128)(2,1)S(1)}, u32[]{:S(2)}, u32[]{:S(2)}) collective-permute-start(bf16[64,1024]{1,0:T(8,128)(2,1)S(1)} %get-tuple-element.24.refs_0_), channel_id=1, source_target_pairs={{0,24},{2,26},{4,28},{6,30},{8,0},{10,2},{12,4},{14,6},{16,8},{18,... | collective-permute-start | bytes 393224 | tf_op jit(solution)/shard_map/ppermute | solution.py:540
  24.8 2.7 %collective-permute-done.5.refs_3_ = bf16[64,1024]{1,0:T(8,128)(2,1)S(1)} collective-permute-done((bf16[64,1024]{1,0:T(8,128)(2,1)S(1)}, bf16[64,1024]{1,0:T(8,128)(2,1)S(1)}, u32[]{:S(2)}, u32[]{:S(2)}) %collective-permute-start.5) | collective-permute-done | bytes 131104 | tf_op jit(solution)/shard_map/ppermute | solution.py:540
  28.9 1.5 %collective-permute-done.refs_1_ = bf16[32,512]{1,0:T(8,128)(2,1)S(1)} collective-permute-done((bf16[32,512]{1,0:T(8,128)(2,1)S(1)}, bf16[32,512]{1,0:T(8,128)(2,1)S(1)}, u32[]{:S(2)}, u32[]{:S(2)}) %collective-permute-start) | collective-permute-done | bytes 32800 | tf_op jit(solution)/shard_map/ppermute | solution.py:540
  31.0 3.1 %collective-permute-start.10 = (bf16[4,32,384]{2,1,0:T(8,128)(2,1)S(1)}, bf16[4,32,384]{2,1,0:T(8,128)(2,1)S(1)}, u32[]{:S(2)}, u32[]{:S(2)}) collective-permute-start(bf16[4,32,384]{2,1,0:T(8,128)(2,1)S(1)} %add_convert_fusion.2.refs_4_), channel_id=1, source_target_pairs={{0,16},{2,18},{4,20},{6,22},{8,24},{10,26},{12,28},{14,30},{16,0},... | collective-permute-start | bytes 294920 | tf_op jit(solution)/shard_map/ppermute | solution.py:540
  34.6 3.5 %collective-permute-done.9.refs_5_ = bf16[4,32,384]{2,1,0:T(8,128)(2,1)S(1)} collective-permute-done((bf16[4,32,384]{2,1,0:T(8,128)(2,1)S(1)}, bf16[4,32,384]{2,1,0:T(8,128)(2,1)S(1)}, u32[]{:S(2)}, u32[]{:S(2)}) %collective-permute-start.9) | collective-permute-done | bytes 98336 | tf_op jit(solution)/shard_map/ppermute | solution.py:540
  38.1 3.3 %collective-permute-done.10.refs_6_ = bf16[4,32,384]{2,1,0:T(8,128)(2,1)S(1)} collective-permute-done((bf16[4,32,384]{2,1,0:T(8,128)(2,1)S(1)}, bf16[4,32,384]{2,1,0:T(8,128)(2,1)S(1)}, u32[]{:S(2)}, u32[]{:S(2)}) %collective-permute-start.10) | collective-permute-done | bytes 98336 | tf_op jit(solution)/shard_map/ppermute | solution.py:540
  41.6 1.6 %collective-permute-start.14 = (bf16[128,1664]{1,0:T(8,128)(2,1)S(1)}, bf16[128,1664]{1,0:T(8,128)(2,1)S(1)}, u32[]{:S(2)}, u32[]{:S(2)}) collective-permute-start(bf16[128,1664]{1,0:T(8,128)(2,1)S(1)} %get-tuple-element.27.rows_ref), channel_id=1, source_target_pairs={{0,2},{1,5},{2,0},{3,7},{4,6},{5,1},{6,4},{7,3},{8,10},{9,13},{10,... | collective-permute-start | bytes 1277960 | tf_op jit(solution)/shard_map/ppermute | solution.py:537
  43.2 6.6 %collective-permute-done.14.rows_ref = bf16[128,1664]{1,0:T(8,128)(2,1)S(1)} collective-permute-done((bf16[128,1664]{1,0:T(8,128)(2,1)S(1)}, bf16[128,1664]{1,0:T(8,128)(2,1)S(1)}, u32[]{:S(2)}, u32[]{:S(2)}) %collective-permute-start.14) | collective-permute-done | bytes 426016 | tf_op jit(solution)/shard_map/ppermute | solution.py:537
  49.8 1.5 %collective-permute-start.17 = (bf16[128,1664]{1,0:T(8,128)(2,1)S(1)}, bf16[128,1664]{1,0:T(8,128)(2,1)S(1)}, u32[]{:S(2)}, u32[]{:S(2)}) collective-permute-start(bf16[128,1664]{1,0:T(8,128)(2,1)S(1)} %collective-permute-done.14.rows_ref), channel_id=1, source_target_pairs={{0,4},{1,3},{2,6},{3,1},{4,0},{5,7},{6,2},{7,5},{8,12},{9,11},{10,... | collective-permute-start | bytes 1277960 | tf_op jit(solution)/shard_map/ppermute | solution.py:537
  51.8 1.0 %pack.1 = (bf16[2,1536,768]{2,1,0:T(8,128)(2,1)S(1)}, bf16[768,1536]{1,0:T(8,128)(2,1)S(1)}) custom-call(bf16[2,1536,384]{2,1,0:T(8,128)(2,1)S(1)} %bitcast.25, bf16[2,1536,384]{2,1,0:T(8,128)(2,1)S(1)} %collective-permute-done.12.gate_up_b, bf16[384,1536]{1,0:T(8,128)(2,1)S(1)} %bitcast.27, bf16[384,1536]{1,0:T(8,128)(2,1)S(1)} %collective-permute-done.13.down_b), custom_call_target="tpu_custom_call" | custom-call | flops 2000000000 | bytes 7077888 | tf_op jit(solution)/shard_map/pack/pallas_call | solution.py:434
  52.8 5.1 %collective-permute-done.17.rows_ref = bf16[128,1664]{1,0:T(8,128)(2,1)S(1)} collective-permute-done((bf16[128,1664]{1,0:T(8,128)(2,1)S(1)}, bf16[128,1664]{1,0:T(8,128)(2,1)S(1)}, u32[]{:S(2)}, u32[]{:S(2)}) %collective-permute-start.17) | collective-permute-done | bytes 426016 | tf_op jit(solution)/shard_map/ppermute | solution.py:537
  57.9 1.2 %expert.7 = bf16[128,1536]{1,0:T(8,128)(2,1)S(1)} custom-call(s32[1]{0:T(128)} %bitcast.1.mine_ref, bf16[128,1664]{1,0:T(8,128)(2,1)S(1)} %collective-permute-done.17.rows_ref, bf16[2,1536,768]{2,1,0:T(8,128)(2,1)S(1)} %get-tuple-element.28.gate_up, bf16[768,1536]{1,0:T(8,128)(2,1)S(1)} %get-tuple-element.29.down), custom_call_target="tpu_custom_call" | custom-call | flops 905969664 | bytes 7077888 | tf_op jit(solution)/shard_map/expert/pallas_call | solution.py:466
  59.1 1.6 %collective-permute-start.18 = (bf16[128,1536]{1,0:T(8,128)(2,1)S(1)}, bf16[128,1536]{1,0:T(8,128)(2,1)S(1)}, u32[]{:S(2)}, u32[]{:S(2)}) collective-permute-start(bf16[128,1536]{1,0:T(8,128)(2,1)S(1)} %expert.7), channel_id=1, source_target_pairs={{0,2},{1,5},{2,0},{3,7},{4,6},{5,1},{6,4},{7,3},{8,10},{9,13},{10,... | collective-permute-start | bytes 1179656 | tf_op jit(solution)/shard_map/ppermute | solution.py:537
  60.7 1.2 %expert.5 = bf16[128,1536]{1,0:T(8,128)(2,1)S(1)} custom-call(s32[1]{0:T(128)} %bitcast.1.mine_ref, bf16[128,1664]{1,0:T(8,128)(2,1)S(1)} %collective-permute-done.14.rows_ref, bf16[2,1536,768]{2,1,0:T(8,128)(2,1)S(1)} %get-tuple-element.28.gate_up, bf16[768,1536]{1,0:T(8,128)(2,1)S(1)} %get-tuple-element.29.down), custom_call_target="tpu_custom_call" | custom-call | flops 905969664 | bytes 7077888 | tf_op jit(solution)/shard_map/expert/pallas_call | solution.py:466
  62.5 2.7 %collective-permute-done.16.rows_ref = bf16[128,1664]{1,0:T(8,128)(2,1)S(1)} collective-permute-done((bf16[128,1664]{1,0:T(8,128)(2,1)S(1)}, bf16[128,1664]{1,0:T(8,128)(2,1)S(1)}, u32[]{:S(2)}, u32[]{:S(2)}) %collective-permute-start.16) | collective-permute-done | bytes 426016 | tf_op jit(solution)/shard_map/ppermute | solution.py:537
  65.2 1.2 %expert.6 = f32[128,1536]{1,0:T(8,128)S(1)} custom-call(s32[1]{0:T(128)} %bitcast.1.mine_ref, bf16[128,1664]{1,0:T(8,128)(2,1)S(1)} %collective-permute-done.16.rows_ref, bf16[2,1536,768]{2,1,0:T(8,128)(2,1)S(1)} %get-tuple-element.28.gate_up, bf16[768,1536]{1,0:T(8,128)(2,1)S(1)} %get-tuple-element.29.down), custom_call_target="tpu_custom_call" | custom-call | flops 905969664 | bytes 7077888 | tf_op jit(solution)/shard_map/expert/pallas_call | solution.py:466
  67.1 2.0 %collective-permute-start.19 = (bf16[128,1536]{1,0:T(8,128)(2,1)S(1)}, bf16[128,1536]{1,0:T(8,128)(2,1)S(1)}, u32[]{:S(2)}, u32[]{:S(2)}) collective-permute-start(bf16[128,1536]{1,0:T(8,128)(2,1)S(1)} %add_convert_fusion), channel_id=1, source_target_pairs={{0,4},{1,3},{2,6},{3,1},{4,0},{5,7},{6,2},{7,5},{8,12},{9,11},{10,... | collective-permute-start | bytes 1179656 | tf_op jit(solution)/shard_map/ppermute | solution.py:537
  69.0 1.2 %expert.4.own_ref = f32[128,1536]{1,0:T(8,128)S(1)} custom-call(s32[1]{0:T(128)} %bitcast.1.mine_ref, bf16[128,1664]{1,0:T(8,128)(2,1)S(1)} %get-tuple-element.27.rows_ref, bf16[2,1536,768]{2,1,0:T(8,128)(2,1)S(1)} %get-tuple-element.28.gate_up, bf16[768,1536]{1,0:T(8,128)(2,1)S(1)} %get-tuple-element.29.down), custom_call_target="tpu_custom_call" | custom-call | flops 905969664 | bytes 7077888 | tf_op jit(solution)/shard_map/expert/pallas_call | solution.py:466
  70.2 2.6 %collective-permute-done.15.near_ref = bf16[128,1536]{1,0:T(8,128)(2,1)S(1)} collective-permute-done((bf16[128,1536]{1,0:T(8,128)(2,1)S(1)}, bf16[128,1536]{1,0:T(8,128)(2,1)S(1)}, u32[]{:S(2)}, u32[]{:S(2)}) %collective-permute-start.15) | collective-permute-done | bytes 393248 | tf_op jit(solution)/shard_map/ppermute | solution.py:537
  72.8 2.3 %collective-permute-done.19.over_ref = bf16[128,1536]{1,0:T(8,128)(2,1)S(1)} collective-permute-done((bf16[128,1536]{1,0:T(8,128)(2,1)S(1)}, bf16[128,1536]{1,0:T(8,128)(2,1)S(1)}, u32[]{:S(2)}, u32[]{:S(2)}) %collective-permute-start.19) | collective-permute-done | bytes 393248 | tf_op jit(solution)/shard_map/ppermute | solution.py:537
  75.3 2.5 %collective-permute-start.22 = (bf16[32,1536]{1,0:T(8,128)(2,1)S(1)}, bf16[32,1536]{1,0:T(8,128)(2,1)S(1)}, u32[]{:S(2)}, u32[]{:S(2)}) collective-permute-start(bf16[32,1536]{1,0:T(8,128)(2,1)S(1)} %get-tuple-element.34), channel_id=1, source_target_pairs={{0,8},{2,10},{4,12},{6,14},{8,16},{10,18},{12,20},{14,22},{16,24},... | collective-permute-start | bytes 294920 | tf_op jit(solution)/shard_map/ppermute | solution.py:540
  78.5 1.8 %collective-permute-start.20 = (bf16[32,1536]{1,0:T(8,128)(2,1)S(1)}, bf16[32,1536]{1,0:T(8,128)(2,1)S(1)}, u32[]{:S(2)}, u32[]{:S(2)}) collective-permute-start(bf16[32,1536]{1,0:T(8,128)(2,1)S(1)} %get-tuple-element.32), channel_id=1, source_target_pairs={{0,24},{2,26},{4,28},{6,30},{8,0},{10,2},{12,4},{14,6},{16,8},{18,... | collective-permute-start | bytes 294920 | tf_op jit(solution)/shard_map/ppermute | solution.py:540
  80.3 2.6 %collective-permute-done.22 = bf16[32,1536]{1,0:T(8,128)(2,1)S(1)} collective-permute-done((bf16[32,1536]{1,0:T(8,128)(2,1)S(1)}, bf16[32,1536]{1,0:T(8,128)(2,1)S(1)}, u32[]{:S(2)}, u32[]{:S(2)}) %collective-permute-start.22) | collective-permute-done | bytes 98336 | tf_op jit(solution)/shard_map/ppermute | solution.py:540
  82.9 3.4 %collective-permute-done.21 = bf16[32,1536]{1,0:T(8,128)(2,1)S(1)} collective-permute-done((bf16[32,1536]{1,0:T(8,128)(2,1)S(1)}, bf16[32,1536]{1,0:T(8,128)(2,1)S(1)}, u32[]{:S(2)}, u32[]{:S(2)}) %collective-permute-start.21) | collective-permute-done | bytes 98336 | tf_op jit(solution)/shard_map/ppermute | solution.py:540
  (40 shorter events, 6.8 us)
Async XLA Ops:
  0.0 51.8 %collective-permute-start.12 = (bf16[2,1536,384]{2,1,0:T(8,128)(2,1)}, bf16[2,1536,384]{2,1,0:T(8,128)(2,1)S(1)}, u32[]{:S(2)}, u32[]{:S(2)}) collective-permute-start(bf16[2,1536,384]{2,1,0:T(8,128)(2,1)} %bitcast.24), channel_id=1, source_target_pairs={{0,1},{1,0},{2,3},{3,2},{4,5},{5,4},{6,7},{7,6},{8,9},{9,8},{10,11... | collective-permute-start | bytes 7077896 | tf_op jit(solution)/shard_map/ppermute | solution.py:547
  0.5 9.1 %copy-start = (bf16[1024,96]{0,1:T(8,128)(2,1)S(1)}, bf16[1024,96]{0,1:T(8,128)(2,1)}, u32[]{:S(2)}) copy-start(bf16[1024,96]{0,1:T(8,128)(2,1)} %param.24) | copy-start | bytes 589828
  0.5 24.2 %copy-start.2 = (bf16[1,384,1536]{2,1,0:T(8,128)(2,1)S(1)}, bf16[1,384,1536]{2,1,0:T(8,128)(2,1)}, u32[]{:S(2)}) copy-start(bf16[1,384,1536]{2,1,0:T(8,128)(2,1)} %param.29) | copy-start | bytes 3538948
  4.0 30.6 %copy-start.3 = (f32[1536]{0:T(1024)S(1)}, f32[1536]{0:T(1024)}, u32[]{:S(2)}) copy-start(f32[1536]{0:T(1024)} %param.25) | copy-start | bytes 18436
  4.0 20.7 %collective-permute-start.3 = (bf16[64,1024]{1,0:T(8,128)(2,1)S(1)}, bf16[64,1024]{1,0:T(8,128)(2,1)S(1)}, u32[]{:S(2)}, u32[]{:S(2)}) collective-permute-start(bf16[64,1024]{1,0:T(8,128)(2,1)S(1)} %get-tuple-element.24.refs_0_), channel_id=1, source_target_pairs={{0,8},{2,10},{4,12},{6,14},{8,16},{10,18},{12,20},{14,22},{16,24},... | collective-permute-start | bytes 393224 | tf_op jit(solution)/shard_map/ppermute | solution.py:540
  6.6 18.1 %collective-permute-start.4 = (bf16[64,1024]{1,0:T(8,128)(2,1)S(1)}, bf16[64,1024]{1,0:T(8,128)(2,1)S(1)}, u32[]{:S(2)}, u32[]{:S(2)}) collective-permute-start(bf16[64,1024]{1,0:T(8,128)(2,1)S(1)} %get-tuple-element.24.refs_0_), channel_id=1, source_target_pairs={{0,16},{2,18},{4,20},{6,22},{8,24},{10,26},{12,28},{14,30},{16,0},... | collective-permute-start | bytes 393224 | tf_op jit(solution)/shard_map/ppermute | solution.py:540
  9.2 12.8 %collective-permute-start.1 = (bf16[32,512]{1,0:T(8,128)(2,1)S(1)}, bf16[32,512]{1,0:T(8,128)(2,1)S(1)}, u32[]{:S(2)}, u32[]{:S(2)}) collective-permute-start(bf16[32,512]{1,0:T(8,128)(2,1)S(1)} %get-tuple-element.22), channel_id=1, source_target_pairs={{0,16},{2,18},{4,20},{6,22},{8,24},{10,26},{12,28},{14,30},{16,0},... | collective-permute-start | bytes 98312 | tf_op jit(solution)/shard_map/ppermute | solution.py:540
  9.6 5.7 %collective-permute-start.6 = (bf16[96,1024]{1,0:T(8,128)(2,1)S(1)}, bf16[96,1024]{1,0:T(8,128)(2,1)S(1)}, u32[]{:S(2)}, u32[]{:S(2)}) collective-permute-start(bf16[96,1024]{1,0:T(8,128)(2,1)S(1)} %bitcast.20), channel_id=1, source_target_pairs={{0,2},{1,5},{2,0},{3,7},{4,6},{5,1},{6,4},{7,3},{8,10},{9,13},{10,... | collective-permute-start | bytes 589832 | tf_op jit(solution)/shard_map/ppermute | solution.py:537
  15.2 5.3 %collective-permute-start.2 = (bf16[32,512]{1,0:T(8,128)(2,1)S(1)}, bf16[32,512]{1,0:T(8,128)(2,1)S(1)}, u32[]{:S(2)}, u32[]{:S(2)}) collective-permute-start(bf16[32,512]{1,0:T(8,128)(2,1)S(1)} %get-tuple-element.23), channel_id=1, source_target_pairs={{0,24},{2,26},{4,28},{6,30},{8,0},{10,2},{12,4},{14,6},{16,8},{18,... | collective-permute-start | bytes 98312 | tf_op jit(solution)/shard_map/ppermute | solution.py:540
  20.5 7.8 %collective-permute-start.7 = (bf16[2,96,1024]{2,1,0:T(8,128)(2,1)S(1)}, bf16[2,96,1024]{2,1,0:T(8,128)(2,1)S(1)}, u32[]{:S(2)}, u32[]{:S(2)}) collective-permute-start(bf16[2,96,1024]{2,1,0:T(8,128)(2,1)S(1)} %pad_maximum_fusion), channel_id=1, source_target_pairs={{0,4},{1,3},{2,6},{3,1},{4,0},{5,7},{6,2},{7,5},{8,12},{9,11},{10,... | collective-permute-start | bytes 1179656 | tf_op jit(solution)/shard_map/ppermute | solution.py:537
  22.1 5.5 %collective-permute-start.5 = (bf16[64,1024]{1,0:T(8,128)(2,1)S(1)}, bf16[64,1024]{1,0:T(8,128)(2,1)S(1)}, u32[]{:S(2)}, u32[]{:S(2)}) collective-permute-start(bf16[64,1024]{1,0:T(8,128)(2,1)S(1)} %get-tuple-element.24.refs_0_), channel_id=1, source_target_pairs={{0,24},{2,26},{4,28},{6,30},{8,0},{10,2},{12,4},{14,6},{16,8},{18,... | collective-permute-start | bytes 393224 | tf_op jit(solution)/shard_map/ppermute | solution.py:540
  24.7 5.7 %collective-permute-start = (bf16[32,512]{1,0:T(8,128)(2,1)S(1)}, bf16[32,512]{1,0:T(8,128)(2,1)S(1)}, u32[]{:S(2)}, u32[]{:S(2)}) collective-permute-start(bf16[32,512]{1,0:T(8,128)(2,1)S(1)} %get-tuple-element.21), channel_id=1, source_target_pairs={{0,8},{2,10},{4,12},{6,14},{8,16},{10,18},{12,20},{14,22},{16,24},... | collective-permute-start | bytes 98312 | tf_op jit(solution)/shard_map/ppermute | solution.py:540
  24.7 27.1 %collective-permute-start.13 = (bf16[384,1536]{1,0:T(8,128)(2,1)S(1)}, bf16[384,1536]{1,0:T(8,128)(2,1)S(1)}, u32[]{:S(2)}, u32[]{:S(2)}) collective-permute-start(bf16[384,1536]{1,0:T(8,128)(2,1)S(1)} %bitcast.26), channel_id=1, source_target_pairs={{0,1},{1,0},{2,3},{3,2},{4,5},{5,4},{6,7},{7,6},{8,9},{9,8},{10,11... | collective-permute-start | bytes 3538952 | tf_op jit(solution)/shard_map/ppermute | solution.py:548
  28.8 23.0 %copy-start.1 = (bf16[1,2,1536,384]{3,2,1,0:T(8,128)(2,1)S(1)}, bf16[1,2,1536,384]{3,2,1,0:T(8,128)(2,1)}, u32[]{:S(2)}) copy-start(bf16[1,2,1536,384]{3,2,1,0:T(8,128)(2,1)} %param.28) | copy-start | bytes 7077892
  28.8 1.6 %collective-permute-start.8 = (f32[4,32,384]{2,1,0:T(8,128)S(1)}, f32[4,32,384]{2,1,0:T(8,128)S(1)}, u32[]{:S(2)}, u32[]{:S(2)}) collective-permute-start(f32[4,32,384]{2,1,0:T(8,128)S(1)} %get-tuple-element.26), channel_id=1, source_target_pairs={{0,1},{1,0},{2,3},{3,2},{4,5},{5,4},{6,7},{7,6},{8,9},{9,8},{10,11... | collective-permute-start | bytes 589832 | tf_op jit(solution)/shard_map/ppermute | solution.py:563
  30.5 7.6 %collective-permute-start.9 = (bf16[4,32,384]{2,1,0:T(8,128)(2,1)S(1)}, bf16[4,32,384]{2,1,0:T(8,128)(2,1)S(1)}, u32[]{:S(2)}, u32[]{:S(2)}) collective-permute-start(bf16[4,32,384]{2,1,0:T(8,128)(2,1)S(1)} %add_convert_fusion.2.refs_4_), channel_id=1, source_target_pairs={{0,8},{2,10},{4,12},{6,14},{8,16},{10,18},{12,20},{14,22},{16,24},... | collective-permute-start | bytes 294920 | tf_op jit(solution)/shard_map/ppermute | solution.py:540
  31.0 10.3 %collective-permute-start.10 = (bf16[4,32,384]{2,1,0:T(8,128)(2,1)S(1)}, bf16[4,32,384]{2,1,0:T(8,128)(2,1)S(1)}, u32[]{:S(2)}, u32[]{:S(2)}) collective-permute-start(bf16[4,32,384]{2,1,0:T(8,128)(2,1)S(1)} %add_convert_fusion.2.refs_4_), channel_id=1, source_target_pairs={{0,16},{2,18},{4,20},{6,22},{8,24},{10,26},{12,28},{14,30},{16,0},... | collective-permute-start | bytes 294920 | tf_op jit(solution)/shard_map/ppermute | solution.py:540
  34.2 7.2 %collective-permute-start.11 = (bf16[4,32,384]{2,1,0:T(8,128)(2,1)S(1)}, bf16[4,32,384]{2,1,0:T(8,128)(2,1)S(1)}, u32[]{:S(2)}, u32[]{:S(2)}) collective-permute-start(bf16[4,32,384]{2,1,0:T(8,128)(2,1)S(1)} %add_convert_fusion.2.refs_4_), channel_id=1, source_target_pairs={{0,24},{2,26},{4,28},{6,30},{8,0},{10,2},{12,4},{14,6},{16,8},{18,... | collective-permute-start | bytes 294920 | tf_op jit(solution)/shard_map/ppermute | solution.py:540
  41.6 8.2 %collective-permute-start.14 = (bf16[128,1664]{1,0:T(8,128)(2,1)S(1)}, bf16[128,1664]{1,0:T(8,128)(2,1)S(1)}, u32[]{:S(2)}, u32[]{:S(2)}) collective-permute-start(bf16[128,1664]{1,0:T(8,128)(2,1)S(1)} %get-tuple-element.27.rows_ref), channel_id=1, source_target_pairs={{0,2},{1,5},{2,0},{3,7},{4,6},{5,1},{6,4},{7,3},{8,10},{9,13},{10,... | collective-permute-start | bytes 1277960 | tf_op jit(solution)/shard_map/ppermute | solution.py:537
  49.8 8.1 %collective-permute-start.17 = (bf16[128,1664]{1,0:T(8,128)(2,1)S(1)}, bf16[128,1664]{1,0:T(8,128)(2,1)S(1)}, u32[]{:S(2)}, u32[]{:S(2)}) collective-permute-start(bf16[128,1664]{1,0:T(8,128)(2,1)S(1)} %collective-permute-done.14.rows_ref), channel_id=1, source_target_pairs={{0,4},{1,3},{2,6},{3,1},{4,0},{5,7},{6,2},{7,5},{8,12},{9,11},{10,... | collective-permute-start | bytes 1277960 | tf_op jit(solution)/shard_map/ppermute | solution.py:537
  51.3 13.9 %collective-permute-start.16 = (bf16[128,1664]{1,0:T(8,128)(2,1)S(1)}, bf16[128,1664]{1,0:T(8,128)(2,1)S(1)}, u32[]{:S(2)}, u32[]{:S(2)}) collective-permute-start(bf16[128,1664]{1,0:T(8,128)(2,1)S(1)} %get-tuple-element.27.rows_ref), channel_id=1, source_target_pairs={{0,4},{1,3},{2,6},{3,1},{4,0},{5,7},{6,2},{7,5},{8,12},{9,11},{10,... | collective-permute-start | bytes 1277960 | tf_op jit(solution)/shard_map/ppermute | solution.py:537
  59.1 7.8 %collective-permute-start.18 = (bf16[128,1536]{1,0:T(8,128)(2,1)S(1)}, bf16[128,1536]{1,0:T(8,128)(2,1)S(1)}, u32[]{:S(2)}, u32[]{:S(2)}) collective-permute-start(bf16[128,1536]{1,0:T(8,128)(2,1)S(1)} %expert.7), channel_id=1, source_target_pairs={{0,2},{1,5},{2,0},{3,7},{4,6},{5,1},{6,4},{7,3},{8,10},{9,13},{10,... | collective-permute-start | bytes 1179656 | tf_op jit(solution)/shard_map/ppermute | solution.py:537
  61.9 10.9 %collective-permute-start.15 = (bf16[128,1536]{1,0:T(8,128)(2,1)S(1)}, bf16[128,1536]{1,0:T(8,128)(2,1)S(1)}, u32[]{:S(2)}, u32[]{:S(2)}) collective-permute-start(bf16[128,1536]{1,0:T(8,128)(2,1)S(1)} %expert.5), channel_id=1, source_target_pairs={{0,2},{1,5},{2,0},{3,7},{4,6},{5,1},{6,4},{7,3},{8,10},{9,13},{10,... | collective-permute-start | bytes 1179656 | tf_op jit(solution)/shard_map/ppermute | solution.py:537
  67.1 8.1 %collective-permute-start.19 = (bf16[128,1536]{1,0:T(8,128)(2,1)S(1)}, bf16[128,1536]{1,0:T(8,128)(2,1)S(1)}, u32[]{:S(2)}, u32[]{:S(2)}) collective-permute-start(bf16[128,1536]{1,0:T(8,128)(2,1)S(1)} %add_convert_fusion), channel_id=1, source_target_pairs={{0,4},{1,3},{2,6},{3,1},{4,0},{5,7},{6,2},{7,5},{8,12},{9,11},{10,... | collective-permute-start | bytes 1179656 | tf_op jit(solution)/shard_map/ppermute | solution.py:537
  75.3 7.6 %collective-permute-start.22 = (bf16[32,1536]{1,0:T(8,128)(2,1)S(1)}, bf16[32,1536]{1,0:T(8,128)(2,1)S(1)}, u32[]{:S(2)}, u32[]{:S(2)}) collective-permute-start(bf16[32,1536]{1,0:T(8,128)(2,1)S(1)} %get-tuple-element.34), channel_id=1, source_target_pairs={{0,8},{2,10},{4,12},{6,14},{8,16},{10,18},{12,20},{14,22},{16,24},... | collective-permute-start | bytes 294920 | tf_op jit(solution)/shard_map/ppermute | solution.py:540
  77.8 8.4 %collective-permute-start.21 = (bf16[32,1536]{1,0:T(8,128)(2,1)S(1)}, bf16[32,1536]{1,0:T(8,128)(2,1)S(1)}, u32[]{:S(2)}, u32[]{:S(2)}) collective-permute-start(bf16[32,1536]{1,0:T(8,128)(2,1)S(1)} %get-tuple-element.33), channel_id=1, source_target_pairs={{0,16},{2,18},{4,20},{6,22},{8,24},{10,26},{12,28},{14,30},{16,0},... | collective-permute-start | bytes 294920 | tf_op jit(solution)/shard_map/ppermute | solution.py:540
  78.5 7.8 %collective-permute-start.20 = (bf16[32,1536]{1,0:T(8,128)(2,1)S(1)}, bf16[32,1536]{1,0:T(8,128)(2,1)S(1)}, u32[]{:S(2)}, u32[]{:S(2)}) collective-permute-start(bf16[32,1536]{1,0:T(8,128)(2,1)S(1)} %get-tuple-element.32), channel_id=1, source_target_pairs={{0,24},{2,26},{4,28},{6,30},{8,0},{10,2},{12,4},{14,6},{16,8},{18,... | collective-permute-start | bytes 294920 | tf_op jit(solution)/shard_map/ppermute | solution.py:540

commit v2 on v1

--- a/solution.py
+++ b/solution.py
@@ -304,46 +304,6 @@
     )(core_at, spot_at, *attn, columns, beside, across)
 
 
-def norm_kernel(line_ref, gain_ref, *refs, deep):
-    pieces, blocks = refs[:deep], refs[deep : 2 * deep]
-    tokens_ref, own_ref = refs[2 * deep :]
-    line = line_ref[0]
-    _, half, share = blocks[0].shape
-    width = deep * share
-    order = [[(c - b) % deep for b in range(deep)] for c in range(deep)]
-    for c in range(deep):
-        values = [blocks[b][order[c][b]].astype(jnp.float32) for b in range(deep)]
-        square = functools.reduce(lambda x, y: x + y, [v * v for v in values])
-        root = lax.rsqrt(jnp.sum(square, axis=-1, keepdims=True) * (1.0 / width) + EPS)
-        rows = pl.ds(pl.multiple_of(lax.rem(line + deep - c, deep) * half, 16), half)
-        for b, value in enumerate(values):
-            columns = pl.ds(pl.multiple_of(lax.rem(line + deep - b, deep) * share, 128), share)
-            tokens_ref[rows, columns] = (value * root * gain_ref[:, columns]).astype(jnp.bfloat16)
-            if c == 0:
-                own_ref[:, columns] = value
-        tokens_ref[rows, width:] = pieces[c][:, share:]
-
-
-def norm(line_at, gain, pieces, blocks):
-    deep, half, share = blocks[0].shape
-    width = deep * share
-    tail = pieces[0].shape[1] - share
-    return pl.pallas_call(
-        functools.partial(norm_kernel, deep=deep),
-        out_shape=[
-            pltpu.VMEM((deep * half, width + tail), jnp.bfloat16),
-            pltpu.VMEM((half, width), jnp.float32),
-        ],
-        in_specs=[SCALARS] + [VECTORS] * (1 + 2 * deep),
-        out_specs=[VECTORS] * 2,
-        cost_estimate=pl.CostEstimate(
-            flops=1_000_000_000, bytes_accessed=1_000_000, transcendentals=1000
-        ),
-        compiler_params=pltpu.CompilerParams(vmem_limit_bytes=8 * 2**20),
-        name="norm",
-    )(line_at, gain.reshape(1, width), *pieces, *blocks)
-
-
 def slot_count(tokens_here, topk, experts):
     return min(
         tokens_here, 2 * ((3 * max(1, (tokens_here * topk + experts - 1) // experts) + 3) // 4)
@@ -445,10 +405,36 @@
     )(gate_up_a, gate_up_b, down_a, down_b)
 
 
-def expert_kernel(mine_ref, rows_ref, gate_up, down, out_ref, *, experts):
-    width = gate_up.shape[1]
-    inputs = rows_ref[:, :width]
-    tail = rows_ref[:, width:].astype(jnp.float32)
+def held_kernel(value_ref, out_ref):
+    out_ref[...] = value_ref[...]
+
+
+def held(value):
+    return pl.pallas_call(
+        held_kernel,
+        out_shape=pltpu.VMEM(value.shape, value.dtype),
+        in_specs=[VECTORS],
+        out_specs=VECTORS,
+        cost_estimate=pl.CostEstimate(flops=1_000_000, bytes_accessed=10_000, transcendentals=0),
+        compiler_params=pltpu.CompilerParams(vmem_limit_bytes=2**20),
+        name="held",
+    )(value)
+
+
+def expert_kernel(
+    mine_ref, line_ref, gain_ref, first, second, others, gate_up, down, out_ref, inputs_ref, *, experts
+):
+    width, share = gate_up.shape[1], second.shape[1]
+    deep, line = width // share, line_ref[0]
+    blocks = [first[:, :share], second[...]] + [others[i] for i in range(deep - 2)]
+    blocks = [block.astype(jnp.float32) for block in blocks]
+    square = functools.reduce(lambda x, y: x + y, [block * block for block in blocks])
+    root = lax.rsqrt(jnp.sum(square, axis=-1, keepdims=True) * (1.0 / width) + EPS)
+    for b, block in enumerate(blocks):
+        columns = pl.ds(pl.multiple_of(lax.rem(line + deep - b, deep) * share, 128), share)
+        inputs_ref[:, columns] = (block * root * gain_ref[:, columns]).astype(jnp.bfloat16)
+    inputs = inputs_ref[...]
+    tail = first[:, share:].astype(jnp.float32)
     lanes = lax.broadcasted_iota(jnp.int32, tail.shape, 1)
     mine = mine_ref[0]
     scale = jnp.sum(
@@ -461,13 +447,14 @@
     out_ref[...] = (total * scale).astype(out_ref.dtype)
 
 
-def expert_rows(mine_at, rows, weights, experts, out_type):
-    count, (units, width) = rows.shape[0], weights[1].shape
+def expert_rows(mine_at, line_at, gain, groups, weights, experts, out_type):
+    count, (units, width) = groups[0].shape[0], weights[1].shape
     return pl.pallas_call(
         functools.partial(expert_kernel, experts=experts),
         out_shape=pltpu.VMEM((count, width), out_type),
-        in_specs=[SCALARS] + [VECTORS] * 3,
+        in_specs=[SCALARS] * 2 + [VECTORS] * 6,
         out_specs=VECTORS,
+        scratch_shapes=[pltpu.VMEM((count, width), jnp.bfloat16)],
         cost_estimate=pl.CostEstimate(
             flops=6 * count * width * units,
             bytes_accessed=6 * width * units,
@@ -475,36 +462,40 @@
         ),
         compiler_params=pltpu.CompilerParams(vmem_limit_bytes=12 * 2**20),
         name="expert",
-    )(mine_at, rows, *weights)
-
-
-def finish_kernel(line_ref, own_ref, near_ref, over_ref, stream_ref, rest_ref, *sent):
-    deep, line = len(sent) + 1, line_ref[0]
-    half = rest_ref.shape[0]
-    for k in range(deep):
-        rows = pl.ds(pl.multiple_of(lax.rem(line + k, deep) * half, 16), half)
+    )(mine_at, line_at, gain, *groups, *weights)
+
+
+def finish_kernel(line_ref, own_ref, near_ref, over_ref, *refs, deep):
+    blocks, rest_ref, sent = refs[:deep], refs[deep], refs[deep + 1 :]
+    half, share, line = rest_ref.shape[0], blocks[0].shape[2], line_ref[0]
+    for c in range(deep):
+        rows = pl.ds(c * half, half)
         total = own_ref[rows, :] + near_ref[rows, :].astype(jnp.float32)
         total = total + over_ref[rows, :].astype(jnp.float32)
-        if k == 0:
-            rest_ref[...] = stream_ref[...] + total
+        if c == 0:
+            rest_ref[...] = total
         else:
-            sent[k - 1][...] = total.astype(jnp.bfloat16)
-
-
-def finish(line_at, own, near_back, over, own_stream, deep):
-    half, width = own_stream.shape
+            sent[deep - c - 1][...] = total.astype(jnp.bfloat16)
+    for b, block in enumerate(blocks):
+        columns = pl.ds(pl.multiple_of(lax.rem(line + deep - b, deep) * share, 128), share)
+        rest_ref[:, columns] += block[(deep - b) % deep].astype(jnp.float32)
+
+
+def finish(line_at, own, near_back, over, blocks):
+    deep, half, share = blocks[0].shape
+    width = deep * share
     return pl.pallas_call(
-        finish_kernel,
+        functools.partial(finish_kernel, deep=deep),
         out_shape=[pltpu.VMEM((half, width), jnp.float32)]
         + [pltpu.VMEM((half, width), jnp.bfloat16)] * (deep - 1),
-        in_specs=[SCALARS] + [VECTORS] * 4,
+        in_specs=[SCALARS] + [VECTORS] * (3 + deep),
         out_specs=[VECTORS] * deep,
         cost_estimate=pl.CostEstimate(
             flops=500_000_000, bytes_accessed=1_000_000, transcendentals=0
         ),
         compiler_params=pltpu.CompilerParams(vmem_limit_bytes=8 * 2**20),
         name="finish",
-    )(line_at, own, near_back, over, own_stream)
+    )(line_at, own, near_back, over, *blocks)
 
 
 PLANE = 4
@@ -523,6 +514,7 @@
 def dense_plan(
     inputs, x_pre, x_dec, o_weight, norm_gain, expert_ids, route_logits, w_gate_up, w_down
 ):
+    width = x_pre.shape[1]
     holders = lax.axis_size("ep")
     experts = holders // 2
     deep = holders // PLANE
@@ -561,22 +553,36 @@
     kept, given = project(core_at, spot_at, attn, columns, beside, across)
     added = jnp.stack([piece[:, : kept.shape[2]] for piece in pieces]).astype(jnp.float32)
     summed = (kept + lax.ppermute(given, "hp", swap) + added).astype(jnp.bfloat16)
-    tokens, own_stream = norm(line_at, norm_gain, pieces, gather_line(summed))
-
-    def expert(block, out_type):
-        return expert_rows(mine_at, block, weights, experts, out_type)
-
-    near_tokens = plane(tokens, 0)
-    both_tokens = plane(near_tokens, 1)
-    far_tokens = plane(tokens, 1)
-    own = expert(tokens, jnp.float32)
-    near_out = expert(near_tokens, jnp.bfloat16)
-    both_out = expert(both_tokens, jnp.bfloat16)
-    far_out = expert(far_tokens, jnp.float32)
+    blocks = gather_line(summed)
+
+    def back_from_here(block, back):
+        turned = [block[(c - back) % deep] for c in range(deep)]
+        return jnp.concatenate(turned, axis=0)
+
+    columns_of = [back_from_here(block, b) for b, block in enumerate(blocks)]
+    tails = jnp.concatenate([piece[:, kept.shape[2] :] for piece in pieces], axis=0)
+    groups = [
+        jnp.concatenate([columns_of[0], tails], axis=1),
+        columns_of[1],
+        jnp.stack(columns_of[2:]),
+    ]
+    parts = range(len(groups))
+    gain = held(norm_gain.reshape(1, width))
+
+    def expert(groups, out_type):
+        return expert_rows(mine_at, line_at, gain, groups, weights, experts, out_type)
+
+    near_groups = [plane(groups[i], 0) for i in parts]
+    both_groups = [plane(near_groups[i], 1) for i in parts]
+    far_groups = [plane(groups[i], 1) for i in parts]
+    own = expert(groups, jnp.float32)
+    near_out = expert(near_groups, jnp.bfloat16)
+    both_out = expert(both_groups, jnp.bfloat16)
+    far_out = expert(far_groups, jnp.float32)
     far_back = plane(both_out, 0)
     near_back = plane(near_out, 0)
     over = plane((far_out + far_back.astype(jnp.float32)).astype(jnp.bfloat16), 1)
-    rest, *sent = finish(line_at, own, near_back, over, own_stream, deep)
+    rest, *sent = finish(line_at, own, near_back, over, blocks)
     got = [along(sent[k - 1], k) for k in far_first]
     for block in got:
         rest = rest + block.astype(jnp.float32)
@@ -613,8 +619,8 @@
     tokens_here, topk = expert_ids.shape
     holders = lax.axis_size("ep")
     dense = tokens_here <= 2 * slot_count(tokens_here, topk, holders // 2)
-    even = holders % PLANE == 0 and x_pre.shape[1] % (holders // PLANE * 128) == 0
-    if dense and even and holders > PLANE and lax.axis_size("hp") == 2:
+    even = holders % PLANE == 0 and holders >= 3 * PLANE and x_pre.shape[1] % (holders // PLANE * 128) == 0
+    if dense and even and lax.axis_size("hp") == 2:
         return dense_plan(inputs, x_pre, x_dec, *rest)
     return slot_plan(attention(*inputs), jnp.concatenate([x_pre, x_dec], axis=0), *rest)
 

time: 87.1 us -> 89.4 us (1.026)
  starting transfers between devices: 30.7 us -> 36.6 us
  waiting for transfers between devices: 45.1 us -> 40.9 us
    ppermute x8 -> x14, starting transfers between devices: 10.7 us -> 18.1 us  [plane(): return lax.ppermute(value, ('ep', 'hp'), plane_perm(holders, stage))]
    ppermute x8 -> x14, waiting for transfers between devices: 24.9 us -> 20.6 us  [plane(): return lax.ppermute(value, ('ep', 'hp'), plane_perm(holders, stage))]
    ppermute x1, waiting for transfers between devices: 0.01 us -> 1.42 us  [dense_plan(): lax.ppermute(given, 'hp', swap)]
    ppermute x12, waiting for transfers between devices: 20.2 us -> 18.8 us  [along(): return lax.ppermute(value, 'ep', line_perm(holders, step))]
    ppermute x12, starting transfers between devices: 19.4 us -> 18 us  [along(): return lax.ppermute(value, 'ep', line_perm(holders, step))]
  transfers between devices with their start and end apart: 23 -> 29, of which waited for: 15 -> 15; matrix products, arithmetic and copies ran while one was open for 0% -> 0% of each run, Pallas kernels for 12% -> 6%
where the time goes in v2:
time: 89.4 us; the launch traced here: 89.3 us
  waiting for transfers between devices  40.9 us (46%)
  starting transfers between devices  36.6 us (41%)
  Pallas kernels  10.6 us (12%)
  other arithmetic  0.91 us (1%)
    ppermute x14, waiting for transfers between devices, plane(): return lax.ppermute(value, ('ep', 'hp'), plane_perm(holders, stage))  20.6 us
    ppermute x12, waiting for transfers between devices, along(): return lax.ppermute(value, 'ep', line_perm(holders, step))  18.8 us
    ppermute x14, starting transfers between devices, plane(): return lax.ppermute(value, ('ep', 'hp'), plane_perm(holders, stage))  18.1 us
    ppermute x12, starting transfers between devices, along(): return lax.ppermute(value, 'ep', line_perm(holders, step))  18 us
    pallas_call x4, Pallas kernels, expert_rows(): pl.pallas_call(functools.partial(expert_kernel, experts=experts), out_sha...  5.42 us
    pallas_call x1, Pallas kernels, start(): pl.pallas_call(functools.partial(start_kernel, experts=experts), out_shap...  3.52 us
  transfers between devices with their start and end apart: 29, of which 15 were waited for; matrix products, arithmetic and copies ran while one was open for 0% of the time, Pallas kernels for 6%

profile of v2, /device:TPU:0, one launch (start us, length us, event | category | flops | bytes accessed | tf_op | source)
XLA Modules:
  0.0 89.3 jit_solution(315788483365447353)
XLA Ops:
  0.0 3.5 %start.1 = (bf16[64,1024]{1,0:T(8,128)(2,1)S(1)}, bf16[32,512]{1,0:T(8,128)(2,1)S(1)}, bf16[32,512]{1,0:T(8,128)(2,1)S(1)}, bf16[32,512]{1,0:T(8,128)(2,1)S(1)}, bf16[32,512]{1,0:T(8,128)(2,1)S(1)}) custom-call(s32[1]{0:T(128)} %bitcast.line_ref, s32[1]{0:T(128)} %bitcast.2.core_ref, s32[1]{0:T(128)} %bitcast.3.spot_ref, s32[1]{0:T(128)} %bitcast.1.mine_ref, ...), custom_call_target="tpu_custom_call" | custom-call | flops 4000000000 | bytes 1000000 | tf_op jit(solution)/shard_map/start/pallas_call | solution.py:245
  3.5 5.1 %collective-permute-start.8 = (bf16[32,512]{1,0:T(8,128)(2,1)S(1)}, bf16[32,512]{1,0:T(8,128)(2,1)S(1)}, u32[]{:S(2)}, u32[]{:S(2)}) collective-permute-start(bf16[32,512]{1,0:T(8,128)(2,1)S(1)} %get-tuple-element.24), channel_id=1, source_target_pairs={{0,24},{2,26},{4,28},{6,30},{8,0},{10,2},{12,4},{14,6},{16,8},{18,... | collective-permute-start | bytes 98312 | tf_op jit(solution)/shard_map/ppermute | solution.py:532
  9.7 2.5 %collective-permute-start = (bf16[64,1024]{1,0:T(8,128)(2,1)S(1)}, bf16[64,1024]{1,0:T(8,128)(2,1)S(1)}, u32[]{:S(2)}, u32[]{:S(2)}) collective-permute-start(bf16[64,1024]{1,0:T(8,128)(2,1)S(1)} %get-tuple-element.18.refs_0_), channel_id=1, source_target_pairs={{0,8},{2,10},{4,12},{6,14},{8,16},{10,18},{12,20},{14,22},{16,24},... | collective-permute-start | bytes 393224 | tf_op jit(solution)/shard_map/ppermute | solution.py:532
  12.2 1.5 %collective-permute-start.3 = (bf16[96,1024]{1,0:T(8,128)(2,1)S(1)}, bf16[96,1024]{1,0:T(8,128)(2,1)S(1)}, u32[]{:S(2)}, u32[]{:S(2)}) collective-permute-start(bf16[96,1024]{1,0:T(8,128)(2,1)S(1)} %bitcast.56), channel_id=1, source_target_pairs={{0,2},{1,5},{2,0},{3,7},{4,6},{5,1},{6,4},{7,3},{8,10},{9,13},{10,... | collective-permute-start | bytes 589832 | tf_op jit(solution)/shard_map/ppermute | solution.py:529
  14.6 3.9 %collective-permute-done.7 = bf16[32,512]{1,0:T(8,128)(2,1)S(1)} collective-permute-done((bf16[32,512]{1,0:T(8,128)(2,1)S(1)}, bf16[32,512]{1,0:T(8,128)(2,1)S(1)}, u32[]{:S(2)}, u32[]{:S(2)}) %collective-permute-start.7) | collective-permute-done | bytes 32800 | tf_op jit(solution)/shard_map/ppermute | solution.py:532
  18.7 1.6 %collective-permute-start.4 = (bf16[2,96,1024]{2,1,0:T(8,128)(2,1)S(1)}, bf16[2,96,1024]{2,1,0:T(8,128)(2,1)S(1)}, u32[]{:S(2)}, u32[]{:S(2)}) collective-permute-start(bf16[2,96,1024]{2,1,0:T(8,128)(2,1)S(1)} %pad_maximum_fusion), channel_id=1, source_target_pairs={{0,4},{1,3},{2,6},{3,1},{4,0},{5,7},{6,2},{7,5},{8,12},{9,11},{10,... | collective-permute-start | bytes 1179656 | tf_op jit(solution)/shard_map/ppermute | solution.py:529
  20.8 1.5 %collective-permute-done.1.refs_2_ = bf16[64,1024]{1,0:T(8,128)(2,1)S(1)} collective-permute-done((bf16[64,1024]{1,0:T(8,128)(2,1)S(1)}, bf16[64,1024]{1,0:T(8,128)(2,1)S(1)}, u32[]{:S(2)}, u32[]{:S(2)}) %collective-permute-start.1) | collective-permute-done | bytes 131104 | tf_op jit(solution)/shard_map/ppermute | solution.py:532
  23.6 3.0 %collective-permute-done.4.refs_6_ = bf16[2,96,1024]{2,1,0:T(8,128)(2,1)S(1)} collective-permute-done((bf16[2,96,1024]{2,1,0:T(8,128)(2,1)S(1)}, bf16[2,96,1024]{2,1,0:T(8,128)(2,1)S(1)}, u32[]{:S(2)}, u32[]{:S(2)}) %collective-permute-start.4) | collective-permute-done | bytes 393248 | tf_op jit(solution)/shard_map/ppermute | solution.py:529
  27.2 1.4 %collective-permute-done.5 = f32[4,32,384]{2,1,0:T(8,128)S(1)} collective-permute-done((f32[4,32,384]{2,1,0:T(8,128)S(1)}, f32[4,32,384]{2,1,0:T(8,128)S(1)}, u32[]{:S(2)}, u32[]{:S(2)}) %collective-permute-start.5) | collective-permute-done | bytes 196640 | tf_op jit(solution)/shard_map/ppermute | solution.py:555
  28.7 2.1 %collective-permute-start.9 = (bf16[4,32,384]{2,1,0:T(8,128)(2,1)S(1)}, bf16[4,32,384]{2,1,0:T(8,128)(2,1)S(1)}, u32[]{:S(2)}, u32[]{:S(2)}) collective-permute-start(bf16[4,32,384]{2,1,0:T(8,128)(2,1)S(1)} %add_convert_fusion.2.refs_0_), channel_id=1, source_target_pairs={{0,8},{2,10},{4,12},{6,14},{8,16},{10,18},{12,20},{14,22},{16,24},... | collective-permute-start | bytes 294920 | tf_op jit(solution)/shard_map/ppermute | solution.py:532
  30.7 2.4 %collective-permute-start.11 = (bf16[4,32,384]{2,1,0:T(8,128)(2,1)S(1)}, bf16[4,32,384]{2,1,0:T(8,128)(2,1)S(1)}, u32[]{:S(2)}, u32[]{:S(2)}) collective-permute-start(bf16[4,32,384]{2,1,0:T(8,128)(2,1)S(1)} %add_convert_fusion.2.refs_0_), channel_id=1, source_target_pairs={{0,24},{2,26},{4,28},{6,30},{8,0},{10,2},{12,4},{14,6},{16,8},{18,... | collective-permute-start | bytes 294920 | tf_op jit(solution)/shard_map/ppermute | solution.py:532
  33.2 6.4 %collective-permute-done.10.refs_2_ = bf16[4,32,384]{2,1,0:T(8,128)(2,1)S(1)} collective-permute-done((bf16[4,32,384]{2,1,0:T(8,128)(2,1)S(1)}, bf16[4,32,384]{2,1,0:T(8,128)(2,1)S(1)}, u32[]{:S(2)}, u32[]{:S(2)}) %collective-permute-start.10) | collective-permute-done | bytes 98336 | tf_op jit(solution)/shard_map/ppermute | solution.py:532
  39.6 1.7 %collective-permute-start.14 = (bf16[128,512]{1,0:T(8,128)(2,1)S(1)}, bf16[128,512]{1,0:T(8,128)(2,1)S(1)}, u32[]{:S(2)}, u32[]{:S(2)}) collective-permute-start(bf16[128,512]{1,0:T(8,128)(2,1)S(1)} %maximum_maximum_fusion.first), channel_id=1, source_target_pairs={{0,2},{1,5},{2,0},{3,7},{4,6},{5,1},{6,4},{7,3},{8,10},{9,13},{10,... | collective-permute-start | bytes 393224 | tf_op jit(solution)/shard_map/ppermute | solution.py:529
  41.9 1.8 %collective-permute-start.15 = (bf16[128,384]{1,0:T(8,128)(2,1)S(1)}, bf16[128,384]{1,0:T(8,128)(2,1)S(1)}, u32[]{:S(2)}, u32[]{:S(2)}) collective-permute-start(bf16[128,384]{1,0:T(8,128)(2,1)S(1)} %pad_maximum_fusion.2.second), channel_id=1, source_target_pairs={{0,2},{1,5},{2,0},{3,7},{4,6},{5,1},{6,4},{7,3},{8,10},{9,13},{10,... | collective-permute-start | bytes 294920 | tf_op jit(solution)/shard_map/ppermute | solution.py:529
  43.6 3.5 %collective-permute-done.16.others = bf16[2,128,384]{2,1,0:T(8,128)(2,1)S(1)} collective-permute-done((bf16[2,128,384]{2,1,0:T(8,128)(2,1)S(1)}, bf16[2,128,384]{2,1,0:T(8,128)(2,1)S(1)}, u32[]{:S(2)}, u32[]{:S(2)}) %collective-permute-start.16) | collective-permute-done | bytes 196640 | tf_op jit(solution)/shard_map/ppermute | solution.py:529
  47.2 1.4 %collective-permute-start.23 = (bf16[2,128,384]{2,1,0:T(8,128)(2,1)S(1)}, bf16[2,128,384]{2,1,0:T(8,128)(2,1)S(1)}, u32[]{:S(2)}, u32[]{:S(2)}) collective-permute-start(bf16[2,128,384]{2,1,0:T(8,128)(2,1)S(1)} %collective-permute-done.16.others), channel_id=1, source_target_pairs={{0,4},{1,3},{2,6},{3,1},{4,0},{5,7},{6,2},{7,5},{8,12},{9,11},{10,... | collective-permute-start | bytes 589832 | tf_op jit(solution)/shard_map/ppermute | solution.py:529
  49.3 1.4 %collective-permute-start.22 = (bf16[128,384]{1,0:T(8,128)(2,1)S(1)}, bf16[128,384]{1,0:T(8,128)(2,1)S(1)}, u32[]{:S(2)}, u32[]{:S(2)}) collective-permute-start(bf16[128,384]{1,0:T(8,128)(2,1)S(1)} %collective-permute-done.15.second), channel_id=1, source_target_pairs={{0,4},{1,3},{2,6},{3,1},{4,0},{5,7},{6,2},{7,5},{8,12},{9,11},{10,... | collective-permute-start | bytes 294920 | tf_op jit(solution)/shard_map/ppermute | solution.py:529
  51.7 2.6 %collective-permute-done.21.first = bf16[128,512]{1,0:T(8,128)(2,1)S(1)} collective-permute-done((bf16[128,512]{1,0:T(8,128)(2,1)S(1)}, bf16[128,512]{1,0:T(8,128)(2,1)S(1)}, u32[]{:S(2)}, u32[]{:S(2)}) %collective-permute-start.21) | collective-permute-done | bytes 131104 | tf_op jit(solution)/shard_map/ppermute | solution.py:529
  55.3 1.4 %expert.7 = bf16[128,1536]{1,0:T(8,128)(2,1)S(1)} custom-call(s32[1]{0:T(128)} %bitcast.1.mine_ref, s32[1]{0:T(128)} %bitcast.line_ref, f32[1,1536]{1,0:T(1,128)S(1)} %held.1.gain_ref, bf16[128,512]{1,0:T(8,128)(2,1)S(1)} %collective-permute-done.21.first, bf16[128,384]{1,0:T(8,128)(2,1)S(1)} %collective-permute-done.22.second, ...), custom_call_target="tpu_custom_call" | custom-call | flops 905969664 | bytes 7077888 | tf_op jit(solution)/shard_map/expert/pallas_call | solution.py:452
  58.0 1.4 %collective-permute-start.20 = (bf16[2,128,384]{2,1,0:T(8,128)(2,1)S(1)}, bf16[2,128,384]{2,1,0:T(8,128)(2,1)S(1)}, u32[]{:S(2)}, u32[]{:S(2)}) collective-permute-start(bf16[2,128,384]{2,1,0:T(8,128)(2,1)S(1)} %pad_maximum_fusion.1.others), channel_id=1, source_target_pairs={{0,4},{1,3},{2,6},{3,1},{4,0},{5,7},{6,2},{7,5},{8,12},{9,11},{10,... | collective-permute-start | bytes 589832 | tf_op jit(solution)/shard_map/ppermute | solution.py:529
  60.0 1.4 %collective-permute-start.19 = (bf16[128,384]{1,0:T(8,128)(2,1)S(1)}, bf16[128,384]{1,0:T(8,128)(2,1)S(1)}, u32[]{:S(2)}, u32[]{:S(2)}) collective-permute-start(bf16[128,384]{1,0:T(8,128)(2,1)S(1)} %pad_maximum_fusion.2.second), channel_id=1, source_target_pairs={{0,4},{1,3},{2,6},{3,1},{4,0},{5,7},{6,2},{7,5},{8,12},{9,11},{10,... | collective-permute-start | bytes 294920 | tf_op jit(solution)/shard_map/ppermute | solution.py:529
  61.4 1.4 %expert.5 = bf16[128,1536]{1,0:T(8,128)(2,1)S(1)} custom-call(s32[1]{0:T(128)} %bitcast.1.mine_ref, s32[1]{0:T(128)} %bitcast.line_ref, f32[1,1536]{1,0:T(1,128)S(1)} %held.1.gain_ref, bf16[128,512]{1,0:T(8,128)(2,1)S(1)} %collective-permute-done.14.first, bf16[128,384]{1,0:T(8,128)(2,1)S(1)} %collective-permute-done.15.second, ...), custom_call_target="tpu_custom_call" | custom-call | flops 905969664 | bytes 7077888 | tf_op jit(solution)/shard_map/expert/pallas_call | solution.py:452
  63.6 4.0 %collective-permute-done.18.first = bf16[128,512]{1,0:T(8,128)(2,1)S(1)} collective-permute-done((bf16[128,512]{1,0:T(8,128)(2,1)S(1)}, bf16[128,512]{1,0:T(8,128)(2,1)S(1)}, u32[]{:S(2)}, u32[]{:S(2)}) %collective-permute-start.18) | collective-permute-done | bytes 131104 | tf_op jit(solution)/shard_map/ppermute | solution.py:529
  67.6 2.1 %collective-permute-done.19.second = bf16[128,384]{1,0:T(8,128)(2,1)S(1)} collective-permute-done((bf16[128,384]{1,0:T(8,128)(2,1)S(1)}, bf16[128,384]{1,0:T(8,128)(2,1)S(1)}, u32[]{:S(2)}, u32[]{:S(2)}) %collective-permute-start.19) | collective-permute-done | bytes 98336 | tf_op jit(solution)/shard_map/ppermute | solution.py:529
  69.7 1.4 %expert.6 = f32[128,1536]{1,0:T(8,128)S(1)} custom-call(s32[1]{0:T(128)} %bitcast.1.mine_ref, s32[1]{0:T(128)} %bitcast.line_ref, f32[1,1536]{1,0:T(1,128)S(1)} %held.1.gain_ref, bf16[128,512]{1,0:T(8,128)(2,1)S(1)} %collective-permute-done.18.first, bf16[128,384]{1,0:T(8,128)(2,1)S(1)} %collective-permute-done.19.second, ...), custom_call_target="tpu_custom_call" | custom-call | flops 905969664 | bytes 7077888 | tf_op jit(solution)/shard_map/expert/pallas_call | solution.py:452
  71.2 2.1 %collective-permute-start.25 = (bf16[128,1536]{1,0:T(8,128)(2,1)S(1)}, bf16[128,1536]{1,0:T(8,128)(2,1)S(1)}, u32[]{:S(2)}, u32[]{:S(2)}) collective-permute-start(bf16[128,1536]{1,0:T(8,128)(2,1)S(1)} %add_convert_fusion), channel_id=1, source_target_pairs={{0,4},{1,3},{2,6},{3,1},{4,0},{5,7},{6,2},{7,5},{8,12},{9,11},{10,... | collective-permute-start | bytes 1179656 | tf_op jit(solution)/shard_map/ppermute | solution.py:529
  73.2 1.4 %expert.4.own_ref = f32[128,1536]{1,0:T(8,128)S(1)} custom-call(s32[1]{0:T(128)} %bitcast.1.mine_ref, s32[1]{0:T(128)} %bitcast.line_ref, f32[1,1536]{1,0:T(1,128)S(1)} %held.1.gain_ref, bf16[128,512]{1,0:T(8,128)(2,1)S(1)} %maximum_maximum_fusion.first, bf16[128,384]{1,0:T(8,128)(2,1)S(1)} %pad_maximum_fusion.2.second, ...), custom_call_target="tpu_custom_call" | custom-call | flops 905969664 | bytes 7077888 | tf_op jit(solution)/shard_map/expert/pallas_call | solution.py:452
  74.6 4.4 %collective-permute-done.25.over_ref = bf16[128,1536]{1,0:T(8,128)(2,1)S(1)} collective-permute-done((bf16[128,1536]{1,0:T(8,128)(2,1)S(1)}, bf16[128,1536]{1,0:T(8,128)(2,1)S(1)}, u32[]{:S(2)}, u32[]{:S(2)}) %collective-permute-start.25) | collective-permute-done | bytes 393248 | tf_op jit(solution)/shard_map/ppermute | solution.py:529
  79.2 1.4 %collective-permute-start.28 = (bf16[32,1536]{1,0:T(8,128)(2,1)S(1)}, bf16[32,1536]{1,0:T(8,128)(2,1)S(1)}, u32[]{:S(2)}, u32[]{:S(2)}) collective-permute-start(bf16[32,1536]{1,0:T(8,128)(2,1)S(1)} %get-tuple-element.30), channel_id=1, source_target_pairs={{0,8},{2,10},{4,12},{6,14},{8,16},{10,18},{12,20},{14,22},{16,24},... | collective-permute-start | bytes 294920 | tf_op jit(solution)/shard_map/ppermute | solution.py:532
  80.6 2.5 %collective-permute-start.27 = (bf16[32,1536]{1,0:T(8,128)(2,1)S(1)}, bf16[32,1536]{1,0:T(8,128)(2,1)S(1)}, u32[]{:S(2)}, u32[]{:S(2)}) collective-permute-start(bf16[32,1536]{1,0:T(8,128)(2,1)S(1)} %get-tuple-element.29), channel_id=1, source_target_pairs={{0,16},{2,18},{4,20},{6,22},{8,24},{10,26},{12,28},{14,30},{16,0},... | collective-permute-start | bytes 294920 | tf_op jit(solution)/shard_map/ppermute | solution.py:532
  83.0 2.7 %collective-permute-done.28 = bf16[32,1536]{1,0:T(8,128)(2,1)S(1)} collective-permute-done((bf16[32,1536]{1,0:T(8,128)(2,1)S(1)}, bf16[32,1536]{1,0:T(8,128)(2,1)S(1)}, u32[]{:S(2)}, u32[]{:S(2)}) %collective-permute-start.28) | collective-permute-done | bytes 98336 | tf_op jit(solution)/shard_map/ppermute | solution.py:532
  85.7 2.1 %collective-permute-done.27 = bf16[32,1536]{1,0:T(8,128)(2,1)S(1)} collective-permute-done((bf16[32,1536]{1,0:T(8,128)(2,1)S(1)}, bf16[32,1536]{1,0:T(8,128)(2,1)S(1)}, u32[]{:S(2)}, u32[]{:S(2)}) %collective-permute-start.27) | collective-permute-done | bytes 98336 | tf_op jit(solution)/shard_map/ppermute | solution.py:532
  (64 shorter events, 12.3 us)
Async XLA Ops:
  0.0 18.6 %copy-start.1 = (bf16[1,2,1536,384]{3,2,1,0:T(8,128)(2,1)S(1)}, bf16[1,2,1536,384]{3,2,1,0:T(8,128)(2,1)}, u32[]{:S(2)}) copy-start(bf16[1,2,1536,384]{3,2,1,0:T(8,128)(2,1)} %param.28) | copy-start | bytes 7077892
  0.0 20.4 %copy-start.2 = (bf16[1,384,1536]{2,1,0:T(8,128)(2,1)S(1)}, bf16[1,384,1536]{2,1,0:T(8,128)(2,1)}, u32[]{:S(2)}) copy-start(bf16[1,384,1536]{2,1,0:T(8,128)(2,1)} %param.29) | copy-start | bytes 3538948
  3.5 10.1 %collective-permute-start.8 = (bf16[32,512]{1,0:T(8,128)(2,1)S(1)}, bf16[32,512]{1,0:T(8,128)(2,1)S(1)}, u32[]{:S(2)}, u32[]{:S(2)}) collective-permute-start(bf16[32,512]{1,0:T(8,128)(2,1)S(1)} %get-tuple-element.24), channel_id=1, source_target_pairs={{0,24},{2,26},{4,28},{6,30},{8,0},{10,2},{12,4},{14,6},{16,8},{18,... | collective-permute-start | bytes 98312 | tf_op jit(solution)/shard_map/ppermute | solution.py:532
  8.7 9.9 %collective-permute-start.7 = (bf16[32,512]{1,0:T(8,128)(2,1)S(1)}, bf16[32,512]{1,0:T(8,128)(2,1)S(1)}, u32[]{:S(2)}, u32[]{:S(2)}) collective-permute-start(bf16[32,512]{1,0:T(8,128)(2,1)S(1)} %get-tuple-element.23), channel_id=1, source_target_pairs={{0,16},{2,18},{4,20},{6,22},{8,24},{10,26},{12,28},{14,30},{16,0},... | collective-permute-start | bytes 98312 | tf_op jit(solution)/shard_map/ppermute | solution.py:532
  8.7 9.9 %collective-permute-start.6 = (bf16[32,512]{1,0:T(8,128)(2,1)S(1)}, bf16[32,512]{1,0:T(8,128)(2,1)S(1)}, u32[]{:S(2)}, u32[]{:S(2)}) collective-permute-start(bf16[32,512]{1,0:T(8,128)(2,1)S(1)} %get-tuple-element.22), channel_id=1, source_target_pairs={{0,8},{2,10},{4,12},{6,14},{8,16},{10,18},{12,20},{14,22},{16,24},... | collective-permute-start | bytes 98312 | tf_op jit(solution)/shard_map/ppermute | solution.py:532
  9.7 10.7 %collective-permute-start = (bf16[64,1024]{1,0:T(8,128)(2,1)S(1)}, bf16[64,1024]{1,0:T(8,128)(2,1)S(1)}, u32[]{:S(2)}, u32[]{:S(2)}) collective-permute-start(bf16[64,1024]{1,0:T(8,128)(2,1)S(1)} %get-tuple-element.18.refs_0_), channel_id=1, source_target_pairs={{0,8},{2,10},{4,12},{6,14},{8,16},{10,18},{12,20},{14,22},{16,24},... | collective-permute-start | bytes 393224 | tf_op jit(solution)/shard_map/ppermute | solution.py:532
  12.2 6.5 %collective-permute-start.3 = (bf16[96,1024]{1,0:T(8,128)(2,1)S(1)}, bf16[96,1024]{1,0:T(8,128)(2,1)S(1)}, u32[]{:S(2)}, u32[]{:S(2)}) collective-permute-start(bf16[96,1024]{1,0:T(8,128)(2,1)S(1)} %bitcast.56), channel_id=1, source_target_pairs={{0,2},{1,5},{2,0},{3,7},{4,6},{5,1},{6,4},{7,3},{8,10},{9,13},{10,... | collective-permute-start | bytes 589832 | tf_op jit(solution)/shard_map/ppermute | solution.py:529
  13.7 8.7 %collective-permute-start.1 = (bf16[64,1024]{1,0:T(8,128)(2,1)S(1)}, bf16[64,1024]{1,0:T(8,128)(2,1)S(1)}, u32[]{:S(2)}, u32[]{:S(2)}) collective-permute-start(bf16[64,1024]{1,0:T(8,128)(2,1)S(1)} %get-tuple-element.18.refs_0_), channel_id=1, source_target_pairs={{0,16},{2,18},{4,20},{6,22},{8,24},{10,26},{12,28},{14,30},{16,0},... | collective-permute-start | bytes 393224 | tf_op jit(solution)/shard_map/ppermute | solution.py:532
  18.6 5.1 %collective-permute-start.2 = (bf16[64,1024]{1,0:T(8,128)(2,1)S(1)}, bf16[64,1024]{1,0:T(8,128)(2,1)S(1)}, u32[]{:S(2)}, u32[]{:S(2)}) collective-permute-start(bf16[64,1024]{1,0:T(8,128)(2,1)S(1)} %get-tuple-element.18.refs_0_), channel_id=1, source_target_pairs={{0,24},{2,26},{4,28},{6,30},{8,0},{10,2},{12,4},{14,6},{16,8},{18,... | collective-permute-start | bytes 393224 | tf_op jit(solution)/shard_map/ppermute | solution.py:532
  18.6 32.1 %collective-permute-start.12 = (bf16[2,1536,384]{2,1,0:T(8,128)(2,1)S(1)}, bf16[2,1536,384]{2,1,0:T(8,128)(2,1)S(1)}, u32[]{:S(2)}, u32[]{:S(2)}) collective-permute-start(bf16[2,1536,384]{2,1,0:T(8,128)(2,1)S(1)} %bitcast.60), channel_id=1, source_target_pairs={{0,1},{1,0},{2,3},{3,2},{4,5},{5,4},{6,7},{7,6},{8,9},{9,8},{10,11... | collective-permute-start | bytes 7077896 | tf_op jit(solution)/shard_map/ppermute | solution.py:539
  18.7 29.9 %copy-start.3 = (f32[1536]{0:T(1024)S(1)}, f32[1536]{0:T(1024)}, u32[]{:S(2)}) copy-start(f32[1536]{0:T(1024)} %param.25) | copy-start | bytes 18436
  18.7 7.8 %collective-permute-start.4 = (bf16[2,96,1024]{2,1,0:T(8,128)(2,1)S(1)}, bf16[2,96,1024]{2,1,0:T(8,128)(2,1)S(1)}, u32[]{:S(2)}, u32[]{:S(2)}) collective-permute-start(bf16[2,96,1024]{2,1,0:T(8,128)(2,1)S(1)} %pad_maximum_fusion), channel_id=1, source_target_pairs={{0,4},{1,3},{2,6},{3,1},{4,0},{5,7},{6,2},{7,5},{8,12},{9,11},{10,... | collective-permute-start | bytes 1179656 | tf_op jit(solution)/shard_map/ppermute | solution.py:529
  20.4 30.3 %collective-permute-start.13 = (bf16[384,1536]{1,0:T(8,128)(2,1)S(1)}, bf16[384,1536]{1,0:T(8,128)(2,1)S(1)}, u32[]{:S(2)}, u32[]{:S(2)}) collective-permute-start(bf16[384,1536]{1,0:T(8,128)(2,1)S(1)} %bitcast.62), channel_id=1, source_target_pairs={{0,1},{1,0},{2,3},{3,2},{4,5},{5,4},{6,7},{7,6},{8,9},{9,8},{10,11... | collective-permute-start | bytes 3538952 | tf_op jit(solution)/shard_map/ppermute | solution.py:540
  27.1 1.5 %collective-permute-start.5 = (f32[4,32,384]{2,1,0:T(8,128)S(1)}, f32[4,32,384]{2,1,0:T(8,128)S(1)}, u32[]{:S(2)}, u32[]{:S(2)}) collective-permute-start(f32[4,32,384]{2,1,0:T(8,128)S(1)} %get-tuple-element.20), channel_id=1, source_target_pairs={{0,1},{1,0},{2,3},{3,2},{4,5},{5,4},{6,7},{7,6},{8,9},{9,8},{10,11... | collective-permute-start | bytes 589832 | tf_op jit(solution)/shard_map/ppermute | solution.py:555
  28.7 13.2 %collective-permute-start.9 = (bf16[4,32,384]{2,1,0:T(8,128)(2,1)S(1)}, bf16[4,32,384]{2,1,0:T(8,128)(2,1)S(1)}, u32[]{:S(2)}, u32[]{:S(2)}) collective-permute-start(bf16[4,32,384]{2,1,0:T(8,128)(2,1)S(1)} %add_convert_fusion.2.refs_0_), channel_id=1, source_target_pairs={{0,8},{2,10},{4,12},{6,14},{8,16},{10,18},{12,20},{14,22},{16,24},... | collective-permute-start | bytes 294920 | tf_op jit(solution)/shard_map/ppermute | solution.py:532
  30.7 8.9 %collective-permute-start.10 = (bf16[4,32,384]{2,1,0:T(8,128)(2,1)S(1)}, bf16[4,32,384]{2,1,0:T(8,128)(2,1)S(1)}, u32[]{:S(2)}, u32[]{:S(2)}) collective-permute-start(bf16[4,32,384]{2,1,0:T(8,128)(2,1)S(1)} %add_convert_fusion.2.refs_0_), channel_id=1, source_target_pairs={{0,16},{2,18},{4,20},{6,22},{8,24},{10,26},{12,28},{14,30},{16,0},... | collective-permute-start | bytes 294920 | tf_op jit(solution)/shard_map/ppermute | solution.py:532
  30.7 10.6 %collective-permute-start.11 = (bf16[4,32,384]{2,1,0:T(8,128)(2,1)S(1)}, bf16[4,32,384]{2,1,0:T(8,128)(2,1)S(1)}, u32[]{:S(2)}, u32[]{:S(2)}) collective-permute-start(bf16[4,32,384]{2,1,0:T(8,128)(2,1)S(1)} %add_convert_fusion.2.refs_0_), channel_id=1, source_target_pairs={{0,24},{2,26},{4,28},{6,30},{8,0},{10,2},{12,4},{14,6},{16,8},{18,... | collective-permute-start | bytes 294920 | tf_op jit(solution)/shard_map/ppermute | solution.py:532
  39.6 8.9 %collective-permute-start.14 = (bf16[128,512]{1,0:T(8,128)(2,1)S(1)}, bf16[128,512]{1,0:T(8,128)(2,1)S(1)}, u32[]{:S(2)}, u32[]{:S(2)}) collective-permute-start(bf16[128,512]{1,0:T(8,128)(2,1)S(1)} %maximum_maximum_fusion.first), channel_id=1, source_target_pairs={{0,2},{1,5},{2,0},{3,7},{4,6},{5,1},{6,4},{7,3},{8,10},{9,13},{10,... | collective-permute-start | bytes 393224 | tf_op jit(solution)/shard_map/ppermute | solution.py:529
  41.5 5.7 %collective-permute-start.16 = (bf16[2,128,384]{2,1,0:T(8,128)(2,1)S(1)}, bf16[2,128,384]{2,1,0:T(8,128)(2,1)S(1)}, u32[]{:S(2)}, u32[]{:S(2)}) collective-permute-start(bf16[2,128,384]{2,1,0:T(8,128)(2,1)S(1)} %pad_maximum_fusion.1.others), channel_id=1, source_target_pairs={{0,2},{1,5},{2,0},{3,7},{4,6},{5,1},{6,4},{7,3},{8,10},{9,13},{10,... | collective-permute-start | bytes 589832 | tf_op jit(solution)/shard_map/ppermute | solution.py:529
  41.9 7.4 %collective-permute-start.15 = (bf16[128,384]{1,0:T(8,128)(2,1)S(1)}, bf16[128,384]{1,0:T(8,128)(2,1)S(1)}, u32[]{:S(2)}, u32[]{:S(2)}) collective-permute-start(bf16[128,384]{1,0:T(8,128)(2,1)S(1)} %pad_maximum_fusion.2.second), channel_id=1, source_target_pairs={{0,2},{1,5},{2,0},{3,7},{4,6},{5,1},{6,4},{7,3},{8,10},{9,13},{10,... | collective-permute-start | bytes 294920 | tf_op jit(solution)/shard_map/ppermute | solution.py:529
  47.2 8.1 %collective-permute-start.23 = (bf16[2,128,384]{2,1,0:T(8,128)(2,1)S(1)}, bf16[2,128,384]{2,1,0:T(8,128)(2,1)S(1)}, u32[]{:S(2)}, u32[]{:S(2)}) collective-permute-start(bf16[2,128,384]{2,1,0:T(8,128)(2,1)S(1)} %collective-permute-done.16.others), channel_id=1, source_target_pairs={{0,4},{1,3},{2,6},{3,1},{4,0},{5,7},{6,2},{7,5},{8,12},{9,11},{10,... | collective-permute-start | bytes 589832 | tf_op jit(solution)/shard_map/ppermute | solution.py:529
  48.6 5.7 %collective-permute-start.21 = (bf16[128,512]{1,0:T(8,128)(2,1)S(1)}, bf16[128,512]{1,0:T(8,128)(2,1)S(1)}, u32[]{:S(2)}, u32[]{:S(2)}) collective-permute-start(bf16[128,512]{1,0:T(8,128)(2,1)S(1)} %collective-permute-done.14.first), channel_id=1, source_target_pairs={{0,4},{1,3},{2,6},{3,1},{4,0},{5,7},{6,2},{7,5},{8,12},{9,11},{10,... | collective-permute-start | bytes 393224 | tf_op jit(solution)/shard_map/ppermute | solution.py:529
  49.3 6.0 %collective-permute-start.22 = (bf16[128,384]{1,0:T(8,128)(2,1)S(1)}, bf16[128,384]{1,0:T(8,128)(2,1)S(1)}, u32[]{:S(2)}, u32[]{:S(2)}) collective-permute-start(bf16[128,384]{1,0:T(8,128)(2,1)S(1)} %collective-permute-done.15.second), channel_id=1, source_target_pairs={{0,4},{1,3},{2,6},{3,1},{4,0},{5,7},{6,2},{7,5},{8,12},{9,11},{10,... | collective-permute-start | bytes 294920 | tf_op jit(solution)/shard_map/ppermute | solution.py:529
  56.7 14.4 %collective-permute-start.24 = (bf16[128,1536]{1,0:T(8,128)(2,1)S(1)}, bf16[128,1536]{1,0:T(8,128)(2,1)S(1)}, u32[]{:S(2)}, u32[]{:S(2)}) collective-permute-start(bf16[128,1536]{1,0:T(8,128)(2,1)S(1)} %expert.7), channel_id=1, source_target_pairs={{0,2},{1,5},{2,0},{3,7},{4,6},{5,1},{6,4},{7,3},{8,10},{9,13},{10,... | collective-permute-start | bytes 1179656 | tf_op jit(solution)/shard_map/ppermute | solution.py:529
  58.0 11.7 %collective-permute-start.20 = (bf16[2,128,384]{2,1,0:T(8,128)(2,1)S(1)}, bf16[2,128,384]{2,1,0:T(8,128)(2,1)S(1)}, u32[]{:S(2)}, u32[]{:S(2)}) collective-permute-start(bf16[2,128,384]{2,1,0:T(8,128)(2,1)S(1)} %pad_maximum_fusion.1.others), channel_id=1, source_target_pairs={{0,4},{1,3},{2,6},{3,1},{4,0},{5,7},{6,2},{7,5},{8,12},{9,11},{10,... | collective-permute-start | bytes 589832 | tf_op jit(solution)/shard_map/ppermute | solution.py:529
  59.4 8.2 %collective-permute-start.18 = (bf16[128,512]{1,0:T(8,128)(2,1)S(1)}, bf16[128,512]{1,0:T(8,128)(2,1)S(1)}, u32[]{:S(2)}, u32[]{:S(2)}) collective-permute-start(bf16[128,512]{1,0:T(8,128)(2,1)S(1)} %maximum_maximum_fusion.first), channel_id=1, source_target_pairs={{0,4},{1,3},{2,6},{3,1},{4,0},{5,7},{6,2},{7,5},{8,12},{9,11},{10,... | collective-permute-start | bytes 393224 | tf_op jit(solution)/shard_map/ppermute | solution.py:529
  60.0 9.7 %collective-permute-start.19 = (bf16[128,384]{1,0:T(8,128)(2,1)S(1)}, bf16[128,384]{1,0:T(8,128)(2,1)S(1)}, u32[]{:S(2)}, u32[]{:S(2)}) collective-permute-start(bf16[128,384]{1,0:T(8,128)(2,1)S(1)} %pad_maximum_fusion.2.second), channel_id=1, source_target_pairs={{0,4},{1,3},{2,6},{3,1},{4,0},{5,7},{6,2},{7,5},{8,12},{9,11},{10,... | collective-permute-start | bytes 294920 | tf_op jit(solution)/shard_map/ppermute | solution.py:529
  62.7 11.8 %collective-permute-start.17 = (bf16[128,1536]{1,0:T(8,128)(2,1)S(1)}, bf16[128,1536]{1,0:T(8,128)(2,1)S(1)}, u32[]{:S(2)}, u32[]{:S(2)}) collective-permute-start(bf16[128,1536]{1,0:T(8,128)(2,1)S(1)} %expert.5), channel_id=1, source_target_pairs={{0,2},{1,5},{2,0},{3,7},{4,6},{5,1},{6,4},{7,3},{8,10},{9,13},{10,... | collective-permute-start | bytes 1179656 | tf_op jit(solution)/shard_map/ppermute | solution.py:529
  71.2 7.8 %collective-permute-start.25 = (bf16[128,1536]{1,0:T(8,128)(2,1)S(1)}, bf16[128,1536]{1,0:T(8,128)(2,1)S(1)}, u32[]{:S(2)}, u32[]{:S(2)}) collective-permute-start(bf16[128,1536]{1,0:T(8,128)(2,1)S(1)} %add_convert_fusion), channel_id=1, source_target_pairs={{0,4},{1,3},{2,6},{3,1},{4,0},{5,7},{6,2},{7,5},{8,12},{9,11},{10,... | collective-permute-start | bytes 1179656 | tf_op jit(solution)/shard_map/ppermute | solution.py:529
  79.2 6.5 %collective-permute-start.28 = (bf16[32,1536]{1,0:T(8,128)(2,1)S(1)}, bf16[32,1536]{1,0:T(8,128)(2,1)S(1)}, u32[]{:S(2)}, u32[]{:S(2)}) collective-permute-start(bf16[32,1536]{1,0:T(8,128)(2,1)S(1)} %get-tuple-element.30), channel_id=1, source_target_pairs={{0,8},{2,10},{4,12},{6,14},{8,16},{10,18},{12,20},{14,22},{16,24},... | collective-permute-start | bytes 294920 | tf_op jit(solution)/shard_map/ppermute | solution.py:532
  80.6 7.3 %collective-permute-start.27 = (bf16[32,1536]{1,0:T(8,128)(2,1)S(1)}, bf16[32,1536]{1,0:T(8,128)(2,1)S(1)}, u32[]{:S(2)}, u32[]{:S(2)}) collective-permute-start(bf16[32,1536]{1,0:T(8,128)(2,1)S(1)} %get-tuple-element.29), channel_id=1, source_target_pairs={{0,16},{2,18},{4,20},{6,22},{8,24},{10,26},{12,28},{14,30},{16,0},... | collective-permute-start | bytes 294920 | tf_op jit(solution)/shard_map/ppermute | solution.py:532
  83.0 5.6 %collective-permute-start.26 = (bf16[32,1536]{1,0:T(8,128)(2,1)S(1)}, bf16[32,1536]{1,0:T(8,128)(2,1)S(1)}, u32[]{:S(2)}, u32[]{:S(2)}) collective-permute-start(bf16[32,1536]{1,0:T(8,128)(2,1)S(1)} %get-tuple-element.28), channel_id=1, source_target_pairs={{0,24},{2,26},{4,28},{6,30},{8,0},{10,2},{12,4},{14,6},{16,8},{18,... | collective-permute-start | bytes 294920 | tf_op jit(solution)/shard_map/ppermute | solution.py:532
  (1 other events, 12.2 us)

commit v3 on v2

--- a/solution.py
+++ b/solution.py
@@ -465,37 +465,53 @@
     )(mine_at, line_at, gain, *groups, *weights)
 
 
-def finish_kernel(line_ref, own_ref, near_ref, over_ref, *refs, deep):
-    blocks, rest_ref, sent = refs[:deep], refs[deep], refs[deep + 1 :]
-    half, share, line = rest_ref.shape[0], blocks[0].shape[2], line_ref[0]
-    for c in range(deep):
-        rows = pl.ds(c * half, half)
-        total = own_ref[rows, :] + near_ref[rows, :].astype(jnp.float32)
-        total = total + over_ref[rows, :].astype(jnp.float32)
-        if c == 0:
-            rest_ref[...] = total
-        else:
-            sent[deep - c - 1][...] = total.astype(jnp.bfloat16)
+def resid_kernel(line_ref, *refs):
+    blocks, out_ref = refs[:-1], refs[-1]
+    deep, share, line = len(blocks), blocks[0].shape[2], line_ref[0]
     for b, block in enumerate(blocks):
         columns = pl.ds(pl.multiple_of(lax.rem(line + deep - b, deep) * share, 128), share)
-        rest_ref[:, columns] += block[(deep - b) % deep].astype(jnp.float32)
-
-
-def finish(line_at, own, near_back, over, blocks):
+        out_ref[:, columns] = block[(deep - b) % deep].astype(jnp.float32)
+
+
+def resid_rows(line_at, blocks):
     deep, half, share = blocks[0].shape
-    width = deep * share
     return pl.pallas_call(
-        functools.partial(finish_kernel, deep=deep),
-        out_shape=[pltpu.VMEM((half, width), jnp.float32)]
-        + [pltpu.VMEM((half, width), jnp.bfloat16)] * (deep - 1),
-        in_specs=[SCALARS] + [VECTORS] * (3 + deep),
-        out_specs=[VECTORS] * deep,
+        resid_kernel,
+        out_shape=pltpu.VMEM((half, deep * share), jnp.float32),
+        in_specs=[SCALARS] + [VECTORS] * deep,
+        out_specs=VECTORS,
+        cost_estimate=pl.CostEstimate(flops=1_000_000, bytes_accessed=10_000, transcendentals=0),
+        compiler_params=pltpu.CompilerParams(vmem_limit_bytes=4 * 2**20),
+        name="resid",
+    )(line_at, *blocks)
+
+
+def finish_kernel(own_ref, near_ref, over_ref, *refs, first, count):
+    resid, outs = refs[:-count], refs[-count:]
+    half = outs[0].shape[0]
+    for n, out_ref in enumerate(outs):
+        rows = pl.ds((first + n) * half, half)
+        total = own_ref[rows, :] + near_ref[rows, :].astype(jnp.float32)
+        total = total + over_ref[pl.ds(n * half, half), :].astype(jnp.float32)
+        if first + n == 0:
+            total = total + resid[0][...]
+        out_ref[...] = total.astype(out_ref.dtype)
+
+
+def finish(own, near_back, over, first, count, resid=()):
+    half, width = over.shape[0] // count, over.shape[1]
+    kinds = [jnp.float32 if first + n == 0 else jnp.bfloat16 for n in range(count)]
+    return pl.pallas_call(
+        functools.partial(finish_kernel, first=first, count=count),
+        out_shape=[pltpu.VMEM((half, width), kind) for kind in kinds],
+        in_specs=[VECTORS] * (3 + len(resid)),
+        out_specs=[VECTORS] * count,
         cost_estimate=pl.CostEstimate(
             flops=500_000_000, bytes_accessed=1_000_000, transcendentals=0
         ),
         compiler_params=pltpu.CompilerParams(vmem_limit_bytes=8 * 2**20),
         name="finish",
-    )(line_at, own, near_back, over, *blocks)
+    )(own, near_back, over, *resid)
 
 
 PLANE = 4
@@ -514,12 +530,13 @@
 def dense_plan(
     inputs, x_pre, x_dec, o_weight, norm_gain, expert_ids, route_logits, w_gate_up, w_down
 ):
-    width = x_pre.shape[1]
+    tokens_here, width = x_pre.shape[0] + x_dec.shape[0], x_pre.shape[1]
     holders = lax.axis_size("ep")
     experts = holders // 2
     deep = holders // PLANE
     place, core = lax.axis_index("ep"), lax.axis_index("hp")
     line, spot = place // PLANE, place % PLANE
+    half = tokens_here // 2
     swap = [(0, 1), (1, 0)]
     far_first = range(deep - 1, 0, -1)
     where = [jnp.reshape(v, (1,)).astype(jnp.int32) for v in (line, core, spot, place // 2)]
@@ -581,9 +598,17 @@
     far_out = expert(far_groups, jnp.float32)
     far_back = plane(both_out, 0)
     near_back = plane(near_out, 0)
-    over = plane((far_out + far_back.astype(jnp.float32)).astype(jnp.bfloat16), 1)
-    rest, *sent = finish(line_at, own, near_back, over, blocks)
-    got = [along(sent[k - 1], k) for k in far_first]
+    low = deep // 2
+    edge = low * half
+    over_high = plane(
+        (far_out[edge:] + far_back[edge:].astype(jnp.float32)).astype(jnp.bfloat16), 1
+    )
+    over_low = plane((far_out[:edge] + far_back[:edge].astype(jnp.float32)).astype(jnp.bfloat16), 1)
+    sent = finish(own, near_back, over_high, low, deep - low)
+    got = [along(block, deep - low - n) for n, block in enumerate(sent)]
+    own_stream = resid_rows(line_at, blocks)
+    rest, *sent = finish(own, near_back, over_low, 0, low, (own_stream,))
+    got += [along(block, deep - 1 - n) for n, block in enumerate(sent)]
     for block in got:
         rest = rest + block.astype(jnp.float32)
     return rest.astype(jnp.bfloat16)

time: 89.4 us -> 88.9 us (level)
  waiting for transfers between devices: 40.9 us -> 38.3 us
  starting transfers between devices: 36.6 us -> 38.6 us
    ppermute x14 -> x15, waiting for transfers between devices: 20.6 us -> 18.4 us  [plane(): return lax.ppermute(value, ('ep', 'hp'), plane_perm(holders, stage))]
    ppermute x12, starting transfers between devices: 18 us -> 20 us  [along(): return lax.ppermute(value, 'ep', line_perm(holders, step))]
    ppermute x14 -> x15, starting transfers between devices: 18.1 us -> 18.1 us  [plane(): return lax.ppermute(value, ('ep', 'hp'), plane_perm(holders, stage))]
  transfers between devices with their start and end apart: 29 -> 30, of which waited for: 15 -> 14; matrix products, arithmetic and copies ran while one was open for 0% -> 0% of each run, Pallas kernels for 6% -> 6%
where the time goes in v3:
time: 88.9 us; the launch traced here: 88.8 us
  starting transfers between devices  38.6 us (43%)
  waiting for transfers between devices  38.3 us (43%)
  Pallas kernels  10.6 us (12%)
  other arithmetic  0.92 us (1%)
    ppermute x12, starting transfers between devices, along(): return lax.ppermute(value, 'ep', line_perm(holders, step))  20 us
    ppermute x15, waiting for transfers between devices, plane(): return lax.ppermute(value, ('ep', 'hp'), plane_perm(holders, stage))  18.4 us
    ppermute x12, waiting for transfers between devices, along(): return lax.ppermute(value, 'ep', line_perm(holders, step))  18.4 us
    ppermute x15, starting transfers between devices, plane(): return lax.ppermute(value, ('ep', 'hp'), plane_perm(holders, stage))  18.1 us
    pallas_call x4, Pallas kernels, expert_rows(): pl.pallas_call(functools.partial(expert_kernel, experts=experts), out_sha...  5.44 us
    pallas_call x1, Pallas kernels, start(): pl.pallas_call(functools.partial(start_kernel, experts=experts), out_shap...  3.52 us
  transfers between devices with their start and end apart: 30, of which 14 were waited for; matrix products, arithmetic and copies ran while one was open for 0% of the time, Pallas kernels for 6%

profile of v3, /device:TPU:0, one launch (start us, length us, event | category | flops | bytes accessed | tf_op | source)
XLA Modules:
  0.0 88.8 jit_solution(4011119836402253306)
XLA Ops:
  0.0 3.5 %start.1 = (bf16[64,1024]{1,0:T(8,128)(2,1)S(1)}, bf16[32,512]{1,0:T(8,128)(2,1)S(1)}, bf16[32,512]{1,0:T(8,128)(2,1)S(1)}, bf16[32,512]{1,0:T(8,128)(2,1)S(1)}, bf16[32,512]{1,0:T(8,128)(2,1)S(1)}) custom-call(s32[1]{0:T(128)} %bitcast.1.line_ref, s32[1]{0:T(128)} %bitcast.2.core_ref, s32[1]{0:T(128)} %bitcast.3.spot_ref, s32[1]{0:T(128)} %bitcast.mine_ref, ...), custom_call_target="tpu_custom_call" | custom-call | flops 4000000000 | bytes 1000000 | tf_op jit(solution)/shard_map/start/pallas_call | solution.py:245
  3.5 5.1 %collective-permute-start.8 = (bf16[32,512]{1,0:T(8,128)(2,1)S(1)}, bf16[32,512]{1,0:T(8,128)(2,1)S(1)}, u32[]{:S(2)}, u32[]{:S(2)}) collective-permute-start(bf16[32,512]{1,0:T(8,128)(2,1)S(1)} %get-tuple-element.24), channel_id=1, source_target_pairs={{0,24},{2,26},{4,28},{6,30},{8,0},{10,2},{12,4},{14,6},{16,8},{18,... | collective-permute-start | bytes 98312 | tf_op jit(solution)/shard_map/ppermute | solution.py:549
  9.7 2.5 %collective-permute-start = (bf16[64,1024]{1,0:T(8,128)(2,1)S(1)}, bf16[64,1024]{1,0:T(8,128)(2,1)S(1)}, u32[]{:S(2)}, u32[]{:S(2)}) collective-permute-start(bf16[64,1024]{1,0:T(8,128)(2,1)S(1)} %get-tuple-element.18.refs_0_), channel_id=1, source_target_pairs={{0,8},{2,10},{4,12},{6,14},{8,16},{10,18},{12,20},{14,22},{16,24},... | collective-permute-start | bytes 393224 | tf_op jit(solution)/shard_map/ppermute | solution.py:549
  12.2 1.5 %collective-permute-start.3 = (bf16[96,1024]{1,0:T(8,128)(2,1)S(1)}, bf16[96,1024]{1,0:T(8,128)(2,1)S(1)}, u32[]{:S(2)}, u32[]{:S(2)}) collective-permute-start(bf16[96,1024]{1,0:T(8,128)(2,1)S(1)} %bitcast.56), channel_id=1, source_target_pairs={{0,2},{1,5},{2,0},{3,7},{4,6},{5,1},{6,4},{7,3},{8,10},{9,13},{10,... | collective-permute-start | bytes 589832 | tf_op jit(solution)/shard_map/ppermute | solution.py:546
  14.6 3.9 %collective-permute-done.7 = bf16[32,512]{1,0:T(8,128)(2,1)S(1)} collective-permute-done((bf16[32,512]{1,0:T(8,128)(2,1)S(1)}, bf16[32,512]{1,0:T(8,128)(2,1)S(1)}, u32[]{:S(2)}, u32[]{:S(2)}) %collective-permute-start.7) | collective-permute-done | bytes 32800 | tf_op jit(solution)/shard_map/ppermute | solution.py:549
  18.7 1.6 %collective-permute-start.4 = (bf16[2,96,1024]{2,1,0:T(8,128)(2,1)S(1)}, bf16[2,96,1024]{2,1,0:T(8,128)(2,1)S(1)}, u32[]{:S(2)}, u32[]{:S(2)}) collective-permute-start(bf16[2,96,1024]{2,1,0:T(8,128)(2,1)S(1)} %pad_maximum_fusion), channel_id=1, source_target_pairs={{0,4},{1,3},{2,6},{3,1},{4,0},{5,7},{6,2},{7,5},{8,12},{9,11},{10,... | collective-permute-start | bytes 1179656 | tf_op jit(solution)/shard_map/ppermute | solution.py:546
  20.8 1.5 %collective-permute-done.1.refs_2_ = bf16[64,1024]{1,0:T(8,128)(2,1)S(1)} collective-permute-done((bf16[64,1024]{1,0:T(8,128)(2,1)S(1)}, bf16[64,1024]{1,0:T(8,128)(2,1)S(1)}, u32[]{:S(2)}, u32[]{:S(2)}) %collective-permute-start.1) | collective-permute-done | bytes 131104 | tf_op jit(solution)/shard_map/ppermute | solution.py:549
  22.3 1.3 %collective-permute-done.2.refs_3_ = bf16[64,1024]{1,0:T(8,128)(2,1)S(1)} collective-permute-done((bf16[64,1024]{1,0:T(8,128)(2,1)S(1)}, bf16[64,1024]{1,0:T(8,128)(2,1)S(1)}, u32[]{:S(2)}, u32[]{:S(2)}) %collective-permute-start.2) | collective-permute-done | bytes 131104 | tf_op jit(solution)/shard_map/ppermute | solution.py:549
  23.6 3.0 %collective-permute-done.4.refs_6_ = bf16[2,96,1024]{2,1,0:T(8,128)(2,1)S(1)} collective-permute-done((bf16[2,96,1024]{2,1,0:T(8,128)(2,1)S(1)}, bf16[2,96,1024]{2,1,0:T(8,128)(2,1)S(1)}, u32[]{:S(2)}, u32[]{:S(2)}) %collective-permute-start.4) | collective-permute-done | bytes 393248 | tf_op jit(solution)/shard_map/ppermute | solution.py:546
  27.2 1.4 %collective-permute-done.5 = f32[4,32,384]{2,1,0:T(8,128)S(1)} collective-permute-done((f32[4,32,384]{2,1,0:T(8,128)S(1)}, f32[4,32,384]{2,1,0:T(8,128)S(1)}, u32[]{:S(2)}, u32[]{:S(2)}) %collective-permute-start.5) | collective-permute-done | bytes 196640 | tf_op jit(solution)/shard_map/ppermute | solution.py:572
  28.7 2.1 %collective-permute-start.9 = (bf16[4,32,384]{2,1,0:T(8,128)(2,1)S(1)}, bf16[4,32,384]{2,1,0:T(8,128)(2,1)S(1)}, u32[]{:S(2)}, u32[]{:S(2)}) collective-permute-start(bf16[4,32,384]{2,1,0:T(8,128)(2,1)S(1)} %add_convert_fusion.1.refs_0_), channel_id=1, source_target_pairs={{0,8},{2,10},{4,12},{6,14},{8,16},{10,18},{12,20},{14,22},{16,24},... | collective-permute-start | bytes 294920 | tf_op jit(solution)/shard_map/ppermute | solution.py:549
  30.7 2.4 %collective-permute-start.11 = (bf16[4,32,384]{2,1,0:T(8,128)(2,1)S(1)}, bf16[4,32,384]{2,1,0:T(8,128)(2,1)S(1)}, u32[]{:S(2)}, u32[]{:S(2)}) collective-permute-start(bf16[4,32,384]{2,1,0:T(8,128)(2,1)S(1)} %add_convert_fusion.1.refs_0_), channel_id=1, source_target_pairs={{0,24},{2,26},{4,28},{6,30},{8,0},{10,2},{12,4},{14,6},{16,8},{18,... | collective-permute-start | bytes 294920 | tf_op jit(solution)/shard_map/ppermute | solution.py:549
  33.2 6.4 %collective-permute-done.10.refs_2_ = bf16[4,32,384]{2,1,0:T(8,128)(2,1)S(1)} collective-permute-done((bf16[4,32,384]{2,1,0:T(8,128)(2,1)S(1)}, bf16[4,32,384]{2,1,0:T(8,128)(2,1)S(1)}, u32[]{:S(2)}, u32[]{:S(2)}) %collective-permute-start.10) | collective-permute-done | bytes 98336 | tf_op jit(solution)/shard_map/ppermute | solution.py:549
  39.6 1.7 %collective-permute-start.14 = (bf16[128,512]{1,0:T(8,128)(2,1)S(1)}, bf16[128,512]{1,0:T(8,128)(2,1)S(1)}, u32[]{:S(2)}, u32[]{:S(2)}) collective-permute-start(bf16[128,512]{1,0:T(8,128)(2,1)S(1)} %maximum_maximum_fusion.first), channel_id=1, source_target_pairs={{0,2},{1,5},{2,0},{3,7},{4,6},{5,1},{6,4},{7,3},{8,10},{9,13},{10,... | collective-permute-start | bytes 393224 | tf_op jit(solution)/shard_map/ppermute | solution.py:546
  41.9 1.8 %collective-permute-start.15 = (bf16[128,384]{1,0:T(8,128)(2,1)S(1)}, bf16[128,384]{1,0:T(8,128)(2,1)S(1)}, u32[]{:S(2)}, u32[]{:S(2)}) collective-permute-start(bf16[128,384]{1,0:T(8,128)(2,1)S(1)} %pad_maximum_fusion.2.second), channel_id=1, source_target_pairs={{0,2},{1,5},{2,0},{3,7},{4,6},{5,1},{6,4},{7,3},{8,10},{9,13},{10,... | collective-permute-start | bytes 294920 | tf_op jit(solution)/shard_map/ppermute | solution.py:546
  43.6 3.5 %collective-permute-done.16.others = bf16[2,128,384]{2,1,0:T(8,128)(2,1)S(1)} collective-permute-done((bf16[2,128,384]{2,1,0:T(8,128)(2,1)S(1)}, bf16[2,128,384]{2,1,0:T(8,128)(2,1)S(1)}, u32[]{:S(2)}, u32[]{:S(2)}) %collective-permute-start.16) | collective-permute-done | bytes 196640 | tf_op jit(solution)/shard_map/ppermute | solution.py:546
  47.2 1.4 %collective-permute-start.23 = (bf16[2,128,384]{2,1,0:T(8,128)(2,1)S(1)}, bf16[2,128,384]{2,1,0:T(8,128)(2,1)S(1)}, u32[]{:S(2)}, u32[]{:S(2)}) collective-permute-start(bf16[2,128,384]{2,1,0:T(8,128)(2,1)S(1)} %collective-permute-done.16.others), channel_id=1, source_target_pairs={{0,4},{1,3},{2,6},{3,1},{4,0},{5,7},{6,2},{7,5},{8,12},{9,11},{10,... | collective-permute-start | bytes 589832 | tf_op jit(solution)/shard_map/ppermute | solution.py:546
  49.3 1.4 %collective-permute-start.22 = (bf16[128,384]{1,0:T(8,128)(2,1)S(1)}, bf16[128,384]{1,0:T(8,128)(2,1)S(1)}, u32[]{:S(2)}, u32[]{:S(2)}) collective-permute-start(bf16[128,384]{1,0:T(8,128)(2,1)S(1)} %collective-permute-done.15.second), channel_id=1, source_target_pairs={{0,4},{1,3},{2,6},{3,1},{4,0},{5,7},{6,2},{7,5},{8,12},{9,11},{10,... | collective-permute-start | bytes 294920 | tf_op jit(solution)/shard_map/ppermute | solution.py:546
  51.7 2.6 %collective-permute-done.21.first = bf16[128,512]{1,0:T(8,128)(2,1)S(1)} collective-permute-done((bf16[128,512]{1,0:T(8,128)(2,1)S(1)}, bf16[128,512]{1,0:T(8,128)(2,1)S(1)}, u32[]{:S(2)}, u32[]{:S(2)}) %collective-permute-start.21) | collective-permute-done | bytes 131104 | tf_op jit(solution)/shard_map/ppermute | solution.py:546
  55.3 1.4 %expert.7 = bf16[128,1536]{1,0:T(8,128)(2,1)S(1)} custom-call(s32[1]{0:T(128)} %bitcast.mine_ref, s32[1]{0:T(128)} %bitcast.1.line_ref, f32[1,1536]{1,0:T(1,128)S(1)} %held.1.gain_ref, bf16[128,512]{1,0:T(8,128)(2,1)S(1)} %collective-permute-done.21.first, bf16[128,384]{1,0:T(8,128)(2,1)S(1)} %collective-permute-done.22.second, ...), custom_call_target="tpu_custom_call" | custom-call | flops 905969664 | bytes 7077888 | tf_op jit(solution)/shard_map/expert/pallas_call | solution.py:452
  58.0 1.4 %collective-permute-start.20 = (bf16[2,128,384]{2,1,0:T(8,128)(2,1)S(1)}, bf16[2,128,384]{2,1,0:T(8,128)(2,1)S(1)}, u32[]{:S(2)}, u32[]{:S(2)}) collective-permute-start(bf16[2,128,384]{2,1,0:T(8,128)(2,1)S(1)} %pad_maximum_fusion.1.others), channel_id=1, source_target_pairs={{0,4},{1,3},{2,6},{3,1},{4,0},{5,7},{6,2},{7,5},{8,12},{9,11},{10,... | collective-permute-start | bytes 589832 | tf_op jit(solution)/shard_map/ppermute | solution.py:546
  60.0 1.4 %collective-permute-start.19 = (bf16[128,384]{1,0:T(8,128)(2,1)S(1)}, bf16[128,384]{1,0:T(8,128)(2,1)S(1)}, u32[]{:S(2)}, u32[]{:S(2)}) collective-permute-start(bf16[128,384]{1,0:T(8,128)(2,1)S(1)} %pad_maximum_fusion.2.second), channel_id=1, source_target_pairs={{0,4},{1,3},{2,6},{3,1},{4,0},{5,7},{6,2},{7,5},{8,12},{9,11},{10,... | collective-permute-start | bytes 294920 | tf_op jit(solution)/shard_map/ppermute | solution.py:546
  61.4 1.4 %expert.5 = bf16[128,1536]{1,0:T(8,128)(2,1)S(1)} custom-call(s32[1]{0:T(128)} %bitcast.mine_ref, s32[1]{0:T(128)} %bitcast.1.line_ref, f32[1,1536]{1,0:T(1,128)S(1)} %held.1.gain_ref, bf16[128,512]{1,0:T(8,128)(2,1)S(1)} %collective-permute-done.14.first, bf16[128,384]{1,0:T(8,128)(2,1)S(1)} %collective-permute-done.15.second, ...), custom_call_target="tpu_custom_call" | custom-call | flops 905969664 | bytes 7077888 | tf_op jit(solution)/shard_map/expert/pallas_call | solution.py:452
  63.6 4.0 %collective-permute-done.18.first = bf16[128,512]{1,0:T(8,128)(2,1)S(1)} collective-permute-done((bf16[128,512]{1,0:T(8,128)(2,1)S(1)}, bf16[128,512]{1,0:T(8,128)(2,1)S(1)}, u32[]{:S(2)}, u32[]{:S(2)}) %collective-permute-start.18) | collective-permute-done | bytes 131104 | tf_op jit(solution)/shard_map/ppermute | solution.py:546
  67.6 2.1 %collective-permute-done.19.second = bf16[128,384]{1,0:T(8,128)(2,1)S(1)} collective-permute-done((bf16[128,384]{1,0:T(8,128)(2,1)S(1)}, bf16[128,384]{1,0:T(8,128)(2,1)S(1)}, u32[]{:S(2)}, u32[]{:S(2)}) %collective-permute-start.19) | collective-permute-done | bytes 98336 | tf_op jit(solution)/shard_map/ppermute | solution.py:546
  69.7 1.4 %expert.6 = f32[128,1536]{1,0:T(8,128)S(1)} custom-call(s32[1]{0:T(128)} %bitcast.mine_ref, s32[1]{0:T(128)} %bitcast.1.line_ref, f32[1,1536]{1,0:T(1,128)S(1)} %held.1.gain_ref, bf16[128,512]{1,0:T(8,128)(2,1)S(1)} %collective-permute-done.18.first, bf16[128,384]{1,0:T(8,128)(2,1)S(1)} %collective-permute-done.19.second, ...), custom_call_target="tpu_custom_call" | custom-call | flops 905969664 | bytes 7077888 | tf_op jit(solution)/shard_map/expert/pallas_call | solution.py:452
  71.2 2.1 %collective-permute-start.25 = (bf16[64,1536]{1,0:T(8,128)(2,1)S(1)}, bf16[64,1536]{1,0:T(8,128)(2,1)S(1)}, u32[]{:S(2)}, u32[]{:S(2)}) collective-permute-start(bf16[64,1536]{1,0:T(8,128)(2,1)S(1)} %get-tuple-element.32), channel_id=1, source_target_pairs={{0,4},{1,3},{2,6},{3,1},{4,0},{5,7},{6,2},{7,5},{8,12},{9,11},{10,... | collective-permute-start | bytes 589832 | tf_op jit(solution)/shard_map/ppermute | solution.py:546
  73.3 1.4 %expert.4.own_ref = f32[128,1536]{1,0:T(8,128)S(1)} custom-call(s32[1]{0:T(128)} %bitcast.mine_ref, s32[1]{0:T(128)} %bitcast.1.line_ref, f32[1,1536]{1,0:T(1,128)S(1)} %held.1.gain_ref, bf16[128,512]{1,0:T(8,128)(2,1)S(1)} %maximum_maximum_fusion.first, bf16[128,384]{1,0:T(8,128)(2,1)S(1)} %pad_maximum_fusion.2.second, ...), custom_call_target="tpu_custom_call" | custom-call | flops 905969664 | bytes 7077888 | tf_op jit(solution)/shard_map/expert/pallas_call | solution.py:452
  74.7 2.2 %collective-permute-done.25.over_ref = bf16[64,1536]{1,0:T(8,128)(2,1)S(1)} collective-permute-done((bf16[64,1536]{1,0:T(8,128)(2,1)S(1)}, bf16[64,1536]{1,0:T(8,128)(2,1)S(1)}, u32[]{:S(2)}, u32[]{:S(2)}) %collective-permute-start.25) | collective-permute-done | bytes 196640 | tf_op jit(solution)/shard_map/ppermute | solution.py:546
  77.0 3.3 %collective-permute-start.29 = (bf16[32,1536]{1,0:T(8,128)(2,1)S(1)}, bf16[32,1536]{1,0:T(8,128)(2,1)S(1)}, u32[]{:S(2)}, u32[]{:S(2)}) collective-permute-start(bf16[32,1536]{1,0:T(8,128)(2,1)S(1)} %get-tuple-element.30), channel_id=1, source_target_pairs={{0,24},{2,26},{4,28},{6,30},{8,0},{10,2},{12,4},{14,6},{16,8},{18,... | collective-permute-start | bytes 294920 | tf_op jit(solution)/shard_map/ppermute | solution.py:549
  80.5 2.5 %collective-permute-start.27 = (bf16[32,1536]{1,0:T(8,128)(2,1)S(1)}, bf16[32,1536]{1,0:T(8,128)(2,1)S(1)}, u32[]{:S(2)}, u32[]{:S(2)}) collective-permute-start(bf16[32,1536]{1,0:T(8,128)(2,1)S(1)} %get-tuple-element.28), channel_id=1, source_target_pairs={{0,16},{2,18},{4,20},{6,22},{8,24},{10,26},{12,28},{14,30},{16,0},... | collective-permute-start | bytes 294920 | tf_op jit(solution)/shard_map/ppermute | solution.py:549
  82.9 4.0 %collective-permute-done.28 = bf16[32,1536]{1,0:T(8,128)(2,1)S(1)} collective-permute-done((bf16[32,1536]{1,0:T(8,128)(2,1)S(1)}, bf16[32,1536]{1,0:T(8,128)(2,1)S(1)}, u32[]{:S(2)}, u32[]{:S(2)}) %collective-permute-start.28) | collective-permute-done | bytes 98336 | tf_op jit(solution)/shard_map/ppermute | solution.py:549
  (68 shorter events, 11.5 us)
Async XLA Ops:
  0.0 20.4 %copy-start.2 = (bf16[1,384,1536]{2,1,0:T(8,128)(2,1)S(1)}, bf16[1,384,1536]{2,1,0:T(8,128)(2,1)}, u32[]{:S(2)}) copy-start(bf16[1,384,1536]{2,1,0:T(8,128)(2,1)} %param.29) | copy-start | bytes 3538948
  3.5 10.1 %collective-permute-start.8 = (bf16[32,512]{1,0:T(8,128)(2,1)S(1)}, bf16[32,512]{1,0:T(8,128)(2,1)S(1)}, u32[]{:S(2)}, u32[]{:S(2)}) collective-permute-start(bf16[32,512]{1,0:T(8,128)(2,1)S(1)} %get-tuple-element.24), channel_id=1, source_target_pairs={{0,24},{2,26},{4,28},{6,30},{8,0},{10,2},{12,4},{14,6},{16,8},{18,... | collective-permute-start | bytes 98312 | tf_op jit(solution)/shard_map/ppermute | solution.py:549
  8.7 9.9 %collective-permute-start.7 = (bf16[32,512]{1,0:T(8,128)(2,1)S(1)}, bf16[32,512]{1,0:T(8,128)(2,1)S(1)}, u32[]{:S(2)}, u32[]{:S(2)}) collective-permute-start(bf16[32,512]{1,0:T(8,128)(2,1)S(1)} %get-tuple-element.23), channel_id=1, source_target_pairs={{0,16},{2,18},{4,20},{6,22},{8,24},{10,26},{12,28},{14,30},{16,0},... | collective-permute-start | bytes 98312 | tf_op jit(solution)/shard_map/ppermute | solution.py:549
  8.7 9.9 %collective-permute-start.6 = (bf16[32,512]{1,0:T(8,128)(2,1)S(1)}, bf16[32,512]{1,0:T(8,128)(2,1)S(1)}, u32[]{:S(2)}, u32[]{:S(2)}) collective-permute-start(bf16[32,512]{1,0:T(8,128)(2,1)S(1)} %get-tuple-element.22), channel_id=1, source_target_pairs={{0,8},{2,10},{4,12},{6,14},{8,16},{10,18},{12,20},{14,22},{16,24},... | collective-permute-start | bytes 98312 | tf_op jit(solution)/shard_map/ppermute | solution.py:549
  9.7 10.7 %collective-permute-start = (bf16[64,1024]{1,0:T(8,128)(2,1)S(1)}, bf16[64,1024]{1,0:T(8,128)(2,1)S(1)}, u32[]{:S(2)}, u32[]{:S(2)}) collective-permute-start(bf16[64,1024]{1,0:T(8,128)(2,1)S(1)} %get-tuple-element.18.refs_0_), channel_id=1, source_target_pairs={{0,8},{2,10},{4,12},{6,14},{8,16},{10,18},{12,20},{14,22},{16,24},... | collective-permute-start | bytes 393224 | tf_op jit(solution)/shard_map/ppermute | solution.py:549
  12.2 6.5 %collective-permute-start.3 = (bf16[96,1024]{1,0:T(8,128)(2,1)S(1)}, bf16[96,1024]{1,0:T(8,128)(2,1)S(1)}, u32[]{:S(2)}, u32[]{:S(2)}) collective-permute-start(bf16[96,1024]{1,0:T(8,128)(2,1)S(1)} %bitcast.56), channel_id=1, source_target_pairs={{0,2},{1,5},{2,0},{3,7},{4,6},{5,1},{6,4},{7,3},{8,10},{9,13},{10,... | collective-permute-start | bytes 589832 | tf_op jit(solution)/shard_map/ppermute | solution.py:546
  13.7 8.7 %collective-permute-start.1 = (bf16[64,1024]{1,0:T(8,128)(2,1)S(1)}, bf16[64,1024]{1,0:T(8,128)(2,1)S(1)}, u32[]{:S(2)}, u32[]{:S(2)}) collective-permute-start(bf16[64,1024]{1,0:T(8,128)(2,1)S(1)} %get-tuple-element.18.refs_0_), channel_id=1, source_target_pairs={{0,16},{2,18},{4,20},{6,22},{8,24},{10,26},{12,28},{14,30},{16,0},... | collective-permute-start | bytes 393224 | tf_op jit(solution)/shard_map/ppermute | solution.py:549
  18.6 5.1 %collective-permute-start.2 = (bf16[64,1024]{1,0:T(8,128)(2,1)S(1)}, bf16[64,1024]{1,0:T(8,128)(2,1)S(1)}, u32[]{:S(2)}, u32[]{:S(2)}) collective-permute-start(bf16[64,1024]{1,0:T(8,128)(2,1)S(1)} %get-tuple-element.18.refs_0_), channel_id=1, source_target_pairs={{0,24},{2,26},{4,28},{6,30},{8,0},{10,2},{12,4},{14,6},{16,8},{18,... | collective-permute-start | bytes 393224 | tf_op jit(solution)/shard_map/ppermute | solution.py:549
  18.6 32.1 %collective-permute-start.12 = (bf16[2,1536,384]{2,1,0:T(8,128)(2,1)S(1)}, bf16[2,1536,384]{2,1,0:T(8,128)(2,1)S(1)}, u32[]{:S(2)}, u32[]{:S(2)}) collective-permute-start(bf16[2,1536,384]{2,1,0:T(8,128)(2,1)S(1)} %bitcast.60), channel_id=1, source_target_pairs={{0,1},{1,0},{2,3},{3,2},{4,5},{5,4},{6,7},{7,6},{8,9},{9,8},{10,11... | collective-permute-start | bytes 7077896 | tf_op jit(solution)/shard_map/ppermute | solution.py:556
  18.7 29.9 %copy-start.3 = (f32[1536]{0:T(1024)S(1)}, f32[1536]{0:T(1024)}, u32[]{:S(2)}) copy-start(f32[1536]{0:T(1024)} %param.25) | copy-start | bytes 18436
  18.7 7.8 %collective-permute-start.4 = (bf16[2,96,1024]{2,1,0:T(8,128)(2,1)S(1)}, bf16[2,96,1024]{2,1,0:T(8,128)(2,1)S(1)}, u32[]{:S(2)}, u32[]{:S(2)}) collective-permute-start(bf16[2,96,1024]{2,1,0:T(8,128)(2,1)S(1)} %pad_maximum_fusion), channel_id=1, source_target_pairs={{0,4},{1,3},{2,6},{3,1},{4,0},{5,7},{6,2},{7,5},{8,12},{9,11},{10,... | collective-permute-start | bytes 1179656 | tf_op jit(solution)/shard_map/ppermute | solution.py:546
  20.4 30.3 %collective-permute-start.13 = (bf16[384,1536]{1,0:T(8,128)(2,1)S(1)}, bf16[384,1536]{1,0:T(8,128)(2,1)S(1)}, u32[]{:S(2)}, u32[]{:S(2)}) collective-permute-start(bf16[384,1536]{1,0:T(8,128)(2,1)S(1)} %bitcast.62), channel_id=1, source_target_pairs={{0,1},{1,0},{2,3},{3,2},{4,5},{5,4},{6,7},{7,6},{8,9},{9,8},{10,11... | collective-permute-start | bytes 3538952 | tf_op jit(solution)/shard_map/ppermute | solution.py:557
  27.1 1.5 %collective-permute-start.5 = (f32[4,32,384]{2,1,0:T(8,128)S(1)}, f32[4,32,384]{2,1,0:T(8,128)S(1)}, u32[]{:S(2)}, u32[]{:S(2)}) collective-permute-start(f32[4,32,384]{2,1,0:T(8,128)S(1)} %get-tuple-element.20), channel_id=1, source_target_pairs={{0,1},{1,0},{2,3},{3,2},{4,5},{5,4},{6,7},{7,6},{8,9},{9,8},{10,11... | collective-permute-start | bytes 589832 | tf_op jit(solution)/shard_map/ppermute | solution.py:572
  28.7 13.2 %collective-permute-start.9 = (bf16[4,32,384]{2,1,0:T(8,128)(2,1)S(1)}, bf16[4,32,384]{2,1,0:T(8,128)(2,1)S(1)}, u32[]{:S(2)}, u32[]{:S(2)}) collective-permute-start(bf16[4,32,384]{2,1,0:T(8,128)(2,1)S(1)} %add_convert_fusion.1.refs_0_), channel_id=1, source_target_pairs={{0,8},{2,10},{4,12},{6,14},{8,16},{10,18},{12,20},{14,22},{16,24},... | collective-permute-start | bytes 294920 | tf_op jit(solution)/shard_map/ppermute | solution.py:549
  30.7 8.9 %collective-permute-start.10 = (bf16[4,32,384]{2,1,0:T(8,128)(2,1)S(1)}, bf16[4,32,384]{2,1,0:T(8,128)(2,1)S(1)}, u32[]{:S(2)}, u32[]{:S(2)}) collective-permute-start(bf16[4,32,384]{2,1,0:T(8,128)(2,1)S(1)} %add_convert_fusion.1.refs_0_), channel_id=1, source_target_pairs={{0,16},{2,18},{4,20},{6,22},{8,24},{10,26},{12,28},{14,30},{16,0},... | collective-permute-start | bytes 294920 | tf_op jit(solution)/shard_map/ppermute | solution.py:549
  30.7 10.6 %collective-permute-start.11 = (bf16[4,32,384]{2,1,0:T(8,128)(2,1)S(1)}, bf16[4,32,384]{2,1,0:T(8,128)(2,1)S(1)}, u32[]{:S(2)}, u32[]{:S(2)}) collective-permute-start(bf16[4,32,384]{2,1,0:T(8,128)(2,1)S(1)} %add_convert_fusion.1.refs_0_), channel_id=1, source_target_pairs={{0,24},{2,26},{4,28},{6,30},{8,0},{10,2},{12,4},{14,6},{16,8},{18,... | collective-permute-start | bytes 294920 | tf_op jit(solution)/shard_map/ppermute | solution.py:549
  39.6 8.9 %collective-permute-start.14 = (bf16[128,512]{1,0:T(8,128)(2,1)S(1)}, bf16[128,512]{1,0:T(8,128)(2,1)S(1)}, u32[]{:S(2)}, u32[]{:S(2)}) collective-permute-start(bf16[128,512]{1,0:T(8,128)(2,1)S(1)} %maximum_maximum_fusion.first), channel_id=1, source_target_pairs={{0,2},{1,5},{2,0},{3,7},{4,6},{5,1},{6,4},{7,3},{8,10},{9,13},{10,... | collective-permute-start | bytes 393224 | tf_op jit(solution)/shard_map/ppermute | solution.py:546
  41.5 5.7 %collective-permute-start.16 = (bf16[2,128,384]{2,1,0:T(8,128)(2,1)S(1)}, bf16[2,128,384]{2,1,0:T(8,128)(2,1)S(1)}, u32[]{:S(2)}, u32[]{:S(2)}) collective-permute-start(bf16[2,128,384]{2,1,0:T(8,128)(2,1)S(1)} %pad_maximum_fusion.1.others), channel_id=1, source_target_pairs={{0,2},{1,5},{2,0},{3,7},{4,6},{5,1},{6,4},{7,3},{8,10},{9,13},{10,... | collective-permute-start | bytes 589832 | tf_op jit(solution)/shard_map/ppermute | solution.py:546
  41.9 7.4 %collective-permute-start.15 = (bf16[128,384]{1,0:T(8,128)(2,1)S(1)}, bf16[128,384]{1,0:T(8,128)(2,1)S(1)}, u32[]{:S(2)}, u32[]{:S(2)}) collective-permute-start(bf16[128,384]{1,0:T(8,128)(2,1)S(1)} %pad_maximum_fusion.2.second), channel_id=1, source_target_pairs={{0,2},{1,5},{2,0},{3,7},{4,6},{5,1},{6,4},{7,3},{8,10},{9,13},{10,... | collective-permute-start | bytes 294920 | tf_op jit(solution)/shard_map/ppermute | solution.py:546
  47.2 8.1 %collective-permute-start.23 = (bf16[2,128,384]{2,1,0:T(8,128)(2,1)S(1)}, bf16[2,128,384]{2,1,0:T(8,128)(2,1)S(1)}, u32[]{:S(2)}, u32[]{:S(2)}) collective-permute-start(bf16[2,128,384]{2,1,0:T(8,128)(2,1)S(1)} %collective-permute-done.16.others), channel_id=1, source_target_pairs={{0,4},{1,3},{2,6},{3,1},{4,0},{5,7},{6,2},{7,5},{8,12},{9,11},{10,... | collective-permute-start | bytes 589832 | tf_op jit(solution)/shard_map/ppermute | solution.py:546
  48.6 5.7 %collective-permute-start.21 = (bf16[128,512]{1,0:T(8,128)(2,1)S(1)}, bf16[128,512]{1,0:T(8,128)(2,1)S(1)}, u32[]{:S(2)}, u32[]{:S(2)}) collective-permute-start(bf16[128,512]{1,0:T(8,128)(2,1)S(1)} %collective-permute-done.14.first), channel_id=1, source_target_pairs={{0,4},{1,3},{2,6},{3,1},{4,0},{5,7},{6,2},{7,5},{8,12},{9,11},{10,... | collective-permute-start | bytes 393224 | tf_op jit(solution)/shard_map/ppermute | solution.py:546
  49.3 6.0 %collective-permute-start.22 = (bf16[128,384]{1,0:T(8,128)(2,1)S(1)}, bf16[128,384]{1,0:T(8,128)(2,1)S(1)}, u32[]{:S(2)}, u32[]{:S(2)}) collective-permute-start(bf16[128,384]{1,0:T(8,128)(2,1)S(1)} %collective-permute-done.15.second), channel_id=1, source_target_pairs={{0,4},{1,3},{2,6},{3,1},{4,0},{5,7},{6,2},{7,5},{8,12},{9,11},{10,... | collective-permute-start | bytes 294920 | tf_op jit(solution)/shard_map/ppermute | solution.py:546
  56.7 14.4 %collective-permute-start.24 = (bf16[128,1536]{1,0:T(8,128)(2,1)S(1)}, bf16[128,1536]{1,0:T(8,128)(2,1)S(1)}, u32[]{:S(2)}, u32[]{:S(2)}) collective-permute-start(bf16[128,1536]{1,0:T(8,128)(2,1)S(1)} %expert.7), channel_id=1, source_target_pairs={{0,2},{1,5},{2,0},{3,7},{4,6},{5,1},{6,4},{7,3},{8,10},{9,13},{10,... | collective-permute-start | bytes 1179656 | tf_op jit(solution)/shard_map/ppermute | solution.py:546
  58.0 11.7 %collective-permute-start.20 = (bf16[2,128,384]{2,1,0:T(8,128)(2,1)S(1)}, bf16[2,128,384]{2,1,0:T(8,128)(2,1)S(1)}, u32[]{:S(2)}, u32[]{:S(2)}) collective-permute-start(bf16[2,128,384]{2,1,0:T(8,128)(2,1)S(1)} %pad_maximum_fusion.1.others), channel_id=1, source_target_pairs={{0,4},{1,3},{2,6},{3,1},{4,0},{5,7},{6,2},{7,5},{8,12},{9,11},{10,... | collective-permute-start | bytes 589832 | tf_op jit(solution)/shard_map/ppermute | solution.py:546
  59.4 8.3 %collective-permute-start.18 = (bf16[128,512]{1,0:T(8,128)(2,1)S(1)}, bf16[128,512]{1,0:T(8,128)(2,1)S(1)}, u32[]{:S(2)}, u32[]{:S(2)}) collective-permute-start(bf16[128,512]{1,0:T(8,128)(2,1)S(1)} %maximum_maximum_fusion.first), channel_id=1, source_target_pairs={{0,4},{1,3},{2,6},{3,1},{4,0},{5,7},{6,2},{7,5},{8,12},{9,11},{10,... | collective-permute-start | bytes 393224 | tf_op jit(solution)/shard_map/ppermute | solution.py:546
  60.0 9.7 %collective-permute-start.19 = (bf16[128,384]{1,0:T(8,128)(2,1)S(1)}, bf16[128,384]{1,0:T(8,128)(2,1)S(1)}, u32[]{:S(2)}, u32[]{:S(2)}) collective-permute-start(bf16[128,384]{1,0:T(8,128)(2,1)S(1)} %pad_maximum_fusion.2.second), channel_id=1, source_target_pairs={{0,4},{1,3},{2,6},{3,1},{4,0},{5,7},{6,2},{7,5},{8,12},{9,11},{10,... | collective-permute-start | bytes 294920 | tf_op jit(solution)/shard_map/ppermute | solution.py:546
  62.7 12.0 %collective-permute-start.17 = (bf16[128,1536]{1,0:T(8,128)(2,1)S(1)}, bf16[128,1536]{1,0:T(8,128)(2,1)S(1)}, u32[]{:S(2)}, u32[]{:S(2)}) collective-permute-start(bf16[128,1536]{1,0:T(8,128)(2,1)S(1)} %expert.5), channel_id=1, source_target_pairs={{0,2},{1,5},{2,0},{3,7},{4,6},{5,1},{6,4},{7,3},{8,10},{9,13},{10,... | collective-permute-start | bytes 1179656 | tf_op jit(solution)/shard_map/ppermute | solution.py:546
  71.2 5.7 %collective-permute-start.25 = (bf16[64,1536]{1,0:T(8,128)(2,1)S(1)}, bf16[64,1536]{1,0:T(8,128)(2,1)S(1)}, u32[]{:S(2)}, u32[]{:S(2)}) collective-permute-start(bf16[64,1536]{1,0:T(8,128)(2,1)S(1)} %get-tuple-element.32), channel_id=1, source_target_pairs={{0,4},{1,3},{2,6},{3,1},{4,0},{5,7},{6,2},{7,5},{8,12},{9,11},{10,... | collective-permute-start | bytes 589832 | tf_op jit(solution)/shard_map/ppermute | solution.py:546
  73.2 7.0 %collective-permute-start.26 = (bf16[64,1536]{1,0:T(8,128)(2,1)S(1)}, bf16[64,1536]{1,0:T(8,128)(2,1)S(1)}, u32[]{:S(2)}, u32[]{:S(2)}) collective-permute-start(bf16[64,1536]{1,0:T(8,128)(2,1)S(1)} %get-tuple-element.31), channel_id=1, source_target_pairs={{0,4},{1,3},{2,6},{3,1},{4,0},{5,7},{6,2},{7,5},{8,12},{9,11},{10,... | collective-permute-start | bytes 589832 | tf_op jit(solution)/shard_map/ppermute | solution.py:546
  77.0 6.0 %collective-permute-start.29 = (bf16[32,1536]{1,0:T(8,128)(2,1)S(1)}, bf16[32,1536]{1,0:T(8,128)(2,1)S(1)}, u32[]{:S(2)}, u32[]{:S(2)}) collective-permute-start(bf16[32,1536]{1,0:T(8,128)(2,1)S(1)} %get-tuple-element.30), channel_id=1, source_target_pairs={{0,24},{2,26},{4,28},{6,30},{8,0},{10,2},{12,4},{14,6},{16,8},{18,... | collective-permute-start | bytes 294920 | tf_op jit(solution)/shard_map/ppermute | solution.py:549
  80.3 6.6 %collective-permute-start.28 = (bf16[32,1536]{1,0:T(8,128)(2,1)S(1)}, bf16[32,1536]{1,0:T(8,128)(2,1)S(1)}, u32[]{:S(2)}, u32[]{:S(2)}) collective-permute-start(bf16[32,1536]{1,0:T(8,128)(2,1)S(1)} %get-tuple-element.29), channel_id=1, source_target_pairs={{0,8},{2,10},{4,12},{6,14},{8,16},{10,18},{12,20},{14,22},{16,24},... | collective-permute-start | bytes 294920 | tf_op jit(solution)/shard_map/ppermute | solution.py:549
  80.5 7.6 %collective-permute-start.27 = (bf16[32,1536]{1,0:T(8,128)(2,1)S(1)}, bf16[32,1536]{1,0:T(8,128)(2,1)S(1)}, u32[]{:S(2)}, u32[]{:S(2)}) collective-permute-start(bf16[32,1536]{1,0:T(8,128)(2,1)S(1)} %get-tuple-element.28), channel_id=1, source_target_pairs={{0,16},{2,18},{4,20},{6,22},{8,24},{10,26},{12,28},{14,30},{16,0},... | collective-permute-start | bytes 294920 | tf_op jit(solution)/shard_map/ppermute | solution.py:549
  (2 other events, 30.7 us)
